TPU v7x, 32 devices: a whole 2x2x4 slice. The times are simulated.
32 devices in a mesh: expert: 16 (over z, y, x), shard: 2 (over core).
Axes of the slice: x: 2, y: 2, z: 4, core: 2. Of those that a mesh axis runs over, the one named last changes fastest.
Arguments:
- tokens: bfloat16 [4096, 2048], P(('expert', 'shard')), may hold values from -6 to 6
- lengths: int32 [32, 4], P(('expert', 'shard')), may hold values from 1 to 64, 128 in all within a row
- routes: int32 [4096, 8], P(('expert', 'shard')), may hold values from 0 to 31, all different within a row; in each aligned block of 128 rows (0 to 127, 128 to 255, ...) at most 48 rows name the same one
- cotangent: bfloat16 [4096, 2048], P(('expert', 'shard')), may hold values from -6 to 6
- query_weight: bfloat16 [2048, 4096], P(('expert', 'shard')), may hold values from -0.125 to 0.125
- key_weight: bfloat16 [2048, 512], P(('expert', 'shard')), may hold values from -0.125 to 0.125
- value_weight: bfloat16 [2048, 512], P(('expert', 'shard')), may hold values from -0.125 to 0.125
- output_weight: bfloat16 [4096, 2048], P(('expert', 'shard')), may hold values from -0.375 to 0.375
- router_weight: bfloat16 [2048, 32], P(('expert', 'shard')), may hold values from -0.125 to 0.125
- norm_gains: bfloat16 [4352], P(('expert', 'shard')), may hold values from 0.25 to 1.75
- gate_weight: bfloat16 [32, 2048, 768], P(('expert', 'shard')), may hold values from -0.125 to 0.125
- up_weight: bfloat16 [32, 2048, 768], P(('expert', 'shard')), may hold values from -0.125 to 0.125
- down_weight: bfloat16 [32, 768, 2048], P(('expert', 'shard')), may hold values from -0.875 to 0.875
Outputs:
- block_out: bfloat16 [4096, 2048], P(('expert', 'shard'))
- input_grad: float32 [4096, 2048], P(('expert', 'shard'))
- query_grad: float32 [2048, 4096], P(('expert', 'shard'))
- key_grad: float32 [2048, 512], P(('expert', 'shard'))
- value_grad: float32 [2048, 512], P(('expert', 'shard'))
- output_grad: float32 [4096, 2048], P(('expert', 'shard'))
- router_grad: float32 [2048, 32], P(('expert', 'shard'))
- gains_grad: float32 [4352], P(('expert', 'shard'))
- gate_grad: float32 [32, 2048, 768], P(('expert', 'shard'))
- up_grad: float32 [32, 2048, 768], P(('expert', 'shard'))
- down_grad: float32 [32, 768, 2048], P(('expert', 'shard'))
Inputs may be any that keep to these rules, and one draw needn't show every extreme that they name: `lengths`: each row of a device sums with the others to 128; the longest is exactly 64. `routes`: each token names 8 different experts. Among the 128 rows of one device no expert is named more than 48 times; in every draw some expert is named exactly 48 times by some device's rows.
All inputs are finite; a program needn't handle non-finite values.
Results may differ from a plain program's by a relative error of at most 0.018.
Values may be sent and summed in bfloat16 or wider, within the bound.
A program may use at most 256 MiB of HBM per device.

v0:
```python
import jax
import jax.numpy as jnp
from jax import lax
from jax.sharding import PartitionSpec as P

D = 2048
HEADS = 32
KV_HEADS = 4
HEAD_DIM = 128
TOP = 8


epsilon = 1e-06
rope_base = 1000000.0
masked_score = -1e30


def rms_scale(values):
    return lax.rsqrt(jnp.mean(values * values, axis=-1, keepdims=True) + epsilon)


def norm_back(upstream, normed, scale_rows):
    return scale_rows * (upstream - normed * jnp.mean(upstream * normed, axis=-1, keepdims=True))


def sequence_layout(lengths_row, row_count):
    seq_ends = jnp.cumsum(lengths_row)
    places = jnp.arange(row_count, dtype=jnp.int32)
    segment = jnp.sum((places[:, None] >= seq_ends[None, :]).astype(jnp.int32), axis=1)
    starts = seq_ends - lengths_row
    member = segment[:, None] == jnp.arange(lengths_row.shape[0], dtype=jnp.int32)[None, :]
    seg_start = jnp.sum(jnp.where(member, starts[None, :], 0), axis=1)
    return (segment, places - seg_start)


def rope_tables(positions, head_dim):
    half_dim = head_dim // 2
    inverse = rope_base ** (-2.0 * jnp.arange(half_dim, dtype=jnp.float32) / head_dim)
    angles = positions.astype(jnp.float32)[:, None] * inverse[None, :]
    return (jnp.cos(angles)[:, None, :], jnp.sin(angles)[:, None, :])


def rotate(values, cosine, sine_table):
    half_dim = values.shape[-1] // 2
    first_half = values[..., :half_dim]
    second_half = values[..., half_dim:]
    return jnp.concatenate(
        [
            first_half * cosine - second_half * sine_table,
            second_half * cosine + first_half * sine_table,
        ],
        axis=-1,
    )


def slot_layout(routes, experts, capacity):
    flat_routes = routes.reshape(-1)
    onehot = (flat_routes[:, None] == jnp.arange(experts, dtype=jnp.int32)[None, :]).astype(
        jnp.int32
    )
    earlier = jnp.cumsum(onehot, axis=0) - onehot
    slot_index = jnp.sum(earlier * onehot, axis=1)
    return flat_routes * capacity + slot_index


def masked_scores(query, keys, allowed, score_scale):
    scores = (
        jnp.einsum("qkgd,skd->kgqs", query, keys, preferred_element_type=jnp.float32) * score_scale
    )
    return jnp.where(allowed[None, None], scores, masked_score)


def attend(query, keys, values_in, allowed, score_scale):
    scores = masked_scores(query, keys, allowed, score_scale)
    top_score = jnp.max(scores, axis=-1, keepdims=True)
    exponent = jnp.exp(scores - top_score)
    row_total = jnp.sum(exponent, axis=-1, keepdims=True)
    attn_probs = (exponent / row_total).astype(jnp.bfloat16)
    mixed_heads = jnp.einsum(
        "kgqs,skd->qkgd", attn_probs, values_in, preferred_element_type=jnp.float32
    )
    return (mixed_heads, top_score + jnp.log(row_total))


def attend_back(query, keys, values_in, allowed, score_scale, log_total, grad_mixed):
    scores = masked_scores(query, keys, allowed, score_scale)
    attn_probs = jnp.exp(scores - log_total)
    grad_probs = jnp.einsum(
        "qkgd,skd->kgqs", grad_mixed, values_in, preferred_element_type=jnp.float32
    )
    grad_scores = (
        attn_probs * (grad_probs - jnp.sum(attn_probs * grad_probs, axis=-1, keepdims=True))
    ).astype(jnp.bfloat16)
    grad_query = (
        jnp.einsum("kgqs,skd->qkgd", grad_scores, keys, preferred_element_type=jnp.float32)
        * score_scale
    )
    grad_keys = (
        jnp.einsum("kgqs,qkgd->skd", grad_scores, query, preferred_element_type=jnp.float32)
        * score_scale
    )
    grad_values = jnp.einsum(
        "kgqs,qkgd->skd",
        attn_probs.astype(jnp.bfloat16),
        grad_mixed,
        preferred_element_type=jnp.float32,
    )
    return (grad_query, grad_keys, grad_values)


def on_device(
    tokens,
    lengths,
    routes,
    cotangent,
    query_weight,
    key_weight,
    value_weight,
    output_weight,
    router_weight,
    norm_gains,
    gate_weight,
    up_weight,
    down_weight,
):
    row_count = tokens.shape[0]
    expert_count = lax.axis_size("expert")
    shard_count = lax.axis_size("shard")
    experts = expert_count * shard_count
    capacity = (3 * row_count * TOP + 2 * experts - 1) // (2 * experts)
    groups = HEADS // KV_HEADS
    score_scale = HEAD_DIM ** (-0.5)
    query_width = HEADS * HEAD_DIM
    key_width = KV_HEADS * HEAD_DIM
    gathered = (
        lax.all_gather(query_weight, ("expert", "shard"), axis=0, tiled=True),
        lax.all_gather(key_weight, ("expert", "shard"), axis=0, tiled=True),
        lax.all_gather(value_weight, ("expert", "shard"), axis=0, tiled=True),
        lax.all_gather(output_weight, ("expert", "shard"), axis=0, tiled=True),
        lax.all_gather(router_weight, ("expert", "shard"), axis=0, tiled=True),
        lax.all_gather(norm_gains, ("expert", "shard"), axis=0, tiled=True),
    )
    full_query, full_key, full_value, full_output, full_router, full_gains = gathered
    gains_float = full_gains.astype(jnp.float32)
    gain_attn = gains_float[:D]
    gain_ffn = gains_float[D : 2 * D]
    gain_query = gains_float[2 * D : 2 * D + HEAD_DIM]
    gain_key = gains_float[2 * D + HEAD_DIM :]
    inputs = tokens.astype(jnp.float32)
    attn_scale = rms_scale(inputs)
    attn_normed = inputs * attn_scale
    hidden_one = (attn_normed * gain_attn).astype(jnp.bfloat16)
    query_proj = jnp.dot(hidden_one, full_query, preferred_element_type=jnp.float32).reshape(
        row_count, HEADS, HEAD_DIM
    )
    key_proj = jnp.dot(hidden_one, full_key, preferred_element_type=jnp.float32).reshape(
        row_count, KV_HEADS, HEAD_DIM
    )
    value_proj = (
        jnp.dot(hidden_one, full_value, preferred_element_type=jnp.float32)
        .astype(jnp.bfloat16)
        .reshape(row_count, KV_HEADS, HEAD_DIM)
    )
    query_scale = rms_scale(query_proj)
    query_normed = query_proj * query_scale
    key_scale = rms_scale(key_proj)
    key_normed = key_proj * key_scale
    segment, positions = sequence_layout(lengths[0], row_count)
    cosine, sine_table = rope_tables(positions, HEAD_DIM)
    query_rot = (
        rotate(query_normed * gain_query, cosine, sine_table)
        .astype(jnp.bfloat16)
        .reshape(row_count, KV_HEADS, groups, HEAD_DIM)
    )
    key_rot = rotate(key_normed * gain_key, cosine, sine_table).astype(jnp.bfloat16)
    allowed = (segment[:, None] == segment[None, :]) & (positions[None, :] <= positions[:, None])
    mixed_heads, log_total = attend(query_rot, key_rot, value_proj, allowed, score_scale)
    mixed_low = mixed_heads.reshape(row_count, query_width).astype(jnp.bfloat16)
    residual = inputs + jnp.dot(mixed_low, full_output, preferred_element_type=jnp.float32)
    ffn_scale = rms_scale(residual)
    ffn_normed = residual * ffn_scale
    hidden_two = (ffn_normed * gain_ffn).astype(jnp.bfloat16)
    logits = jnp.dot(hidden_two, full_router, preferred_element_type=jnp.float32)
    picked = (routes[:, :, None] == jnp.arange(experts, dtype=jnp.int32)[None, None, :]).astype(
        jnp.float32
    )
    chosen = jnp.sum(picked * logits[:, None, :], axis=-1)
    route_weight = jax.nn.softmax(chosen, axis=-1)
    destination = slot_layout(routes, experts, capacity)
    source_row = jnp.arange(row_count * TOP, dtype=jnp.int32) // TOP
    outgoing = (
        jnp.zeros((experts * capacity, D), jnp.bfloat16).at[destination].set(hidden_two[source_row])
    )
    arrived = lax.all_to_all(
        outgoing.reshape(experts, capacity, D),
        ("expert", "shard"),
        split_axis=0,
        concat_axis=0,
        tiled=True,
    )
    expert_rows = arrived.reshape(experts * capacity, D)
    gate_act = jnp.dot(expert_rows, gate_weight[0], preferred_element_type=jnp.float32)
    up_act = jnp.dot(expert_rows, up_weight[0], preferred_element_type=jnp.float32)
    gate_sig = jax.nn.sigmoid(gate_act)
    gate_silu = gate_act * gate_sig
    expert_hidden = (gate_silu * up_act).astype(jnp.bfloat16)
    expert_out = jnp.dot(expert_hidden, down_weight[0], preferred_element_type=jnp.float32).astype(
        jnp.bfloat16
    )
    returned = lax.all_to_all(
        expert_out.reshape(experts, capacity, D),
        ("expert", "shard"),
        split_axis=0,
        concat_axis=0,
        tiled=True,
    )
    route_out = returned.reshape(experts * capacity, D)[destination].reshape(row_count, TOP, D)
    block_out = (residual + jnp.sum(route_weight[:, :, None] * route_out, axis=1)).astype(
        jnp.bfloat16
    )
    back_set = (
        lax.all_gather(query_weight, ("expert", "shard"), axis=0, tiled=True),
        lax.all_gather(key_weight, ("expert", "shard"), axis=0, tiled=True),
        lax.all_gather(value_weight, ("expert", "shard"), axis=0, tiled=True),
        lax.all_gather(output_weight, ("expert", "shard"), axis=0, tiled=True),
        lax.all_gather(router_weight, ("expert", "shard"), axis=0, tiled=True),
    )
    back_query, back_key, back_value, back_output, back_router = back_set
    grad_out = cotangent.astype(jnp.float32)
    grad_weight = jnp.sum(grad_out[:, None, :] * route_out, axis=-1)
    grad_chosen = route_weight * (
        grad_weight - jnp.sum(route_weight * grad_weight, axis=-1, keepdims=True)
    )
    grad_logits = jnp.sum(picked * grad_chosen[:, :, None], axis=1).astype(jnp.bfloat16)
    grad_hidden_two = jnp.dot(grad_logits, back_router.T, preferred_element_type=jnp.float32)
    slot_grads = (
        (route_weight[:, :, None] * grad_out[:, None, :])
        .astype(jnp.bfloat16)
        .reshape(row_count * TOP, D)
    )
    outgoing_grad = jnp.zeros((experts * capacity, D), jnp.bfloat16).at[destination].set(slot_grads)
    arrived_grad = lax.all_to_all(
        outgoing_grad.reshape(experts, capacity, D),
        ("expert", "shard"),
        split_axis=0,
        concat_axis=0,
        tiled=True,
    )
    arrived_grad = arrived_grad.reshape(experts * capacity, D)
    grad_expert_hidden = jnp.dot(arrived_grad, down_weight[0].T, preferred_element_type=jnp.float32)
    grad_down = jnp.dot(expert_hidden.T, arrived_grad, preferred_element_type=jnp.float32)
    grad_gate_act = (
        grad_expert_hidden * up_act * gate_sig * (1.0 + gate_act * (1.0 - gate_sig))
    ).astype(jnp.bfloat16)
    grad_up_act = (grad_expert_hidden * gate_silu).astype(jnp.bfloat16)
    grad_rows = (
        jnp.dot(grad_gate_act, gate_weight[0].T, preferred_element_type=jnp.float32)
        + jnp.dot(grad_up_act, up_weight[0].T, preferred_element_type=jnp.float32)
    ).astype(jnp.bfloat16)
    grad_gate = jnp.dot(expert_rows.T, grad_gate_act, preferred_element_type=jnp.float32)
    grad_up = jnp.dot(expert_rows.T, grad_up_act, preferred_element_type=jnp.float32)
    returned_grad = lax.all_to_all(
        grad_rows.reshape(experts, capacity, D),
        ("expert", "shard"),
        split_axis=0,
        concat_axis=0,
        tiled=True,
    )
    routed_back = returned_grad.reshape(experts * capacity, D)[destination].reshape(
        row_count, TOP, D
    )
    grad_hidden_two = grad_hidden_two + jnp.sum(routed_back.astype(jnp.float32), axis=1)
    grad_gain_ffn = jnp.sum(grad_hidden_two * ffn_normed, axis=0)
    grad_residual = grad_out + norm_back(grad_hidden_two * gain_ffn, ffn_normed, ffn_scale)
    grad_attn = grad_residual.astype(jnp.bfloat16)
    grad_output_w = jnp.dot(mixed_low.T, grad_attn, preferred_element_type=jnp.float32)
    grad_mixed = (
        jnp.dot(grad_attn, back_output.T, preferred_element_type=jnp.float32)
        .astype(jnp.bfloat16)
        .reshape(row_count, KV_HEADS, groups, HEAD_DIM)
    )
    grad_query_rot, grad_key_rot, grad_value_rot = attend_back(
        query_rot, key_rot, value_proj, allowed, score_scale, log_total, grad_mixed
    )
    grad_value_proj = grad_value_rot.astype(jnp.bfloat16).reshape(row_count, key_width)
    grad_query_gained = rotate(
        grad_query_rot.reshape(row_count, HEADS, HEAD_DIM), cosine, -sine_table
    )
    grad_gain_query = jnp.sum(grad_query_gained * query_normed, axis=(0, 1))
    grad_query_proj = (
        norm_back(grad_query_gained * gain_query, query_normed, query_scale)
        .astype(jnp.bfloat16)
        .reshape(row_count, query_width)
    )
    grad_key_gained = rotate(grad_key_rot, cosine, -sine_table)
    grad_gain_key = jnp.sum(grad_key_gained * key_normed, axis=(0, 1))
    grad_key_proj = (
        norm_back(grad_key_gained * gain_key, key_normed, key_scale)
        .astype(jnp.bfloat16)
        .reshape(row_count, key_width)
    )
    grad_hidden_one = jnp.dot(grad_query_proj, back_query.T, preferred_element_type=jnp.float32)
    grad_hidden_one = grad_hidden_one + jnp.dot(
        grad_key_proj, back_key.T, preferred_element_type=jnp.float32
    )
    grad_hidden_one = grad_hidden_one + jnp.dot(
        grad_value_proj, back_value.T, preferred_element_type=jnp.float32
    )
    grad_gain_attn = jnp.sum(grad_hidden_one * attn_normed, axis=0)
    input_grad = grad_residual + norm_back(grad_hidden_one * gain_attn, attn_normed, attn_scale)
    gains_local = jnp.concatenate([grad_gain_attn, grad_gain_ffn, grad_gain_query, grad_gain_key])
    grad_query_w = jnp.dot(hidden_one.T, grad_query_proj, preferred_element_type=jnp.float32)
    grad_key_w = jnp.dot(hidden_one.T, grad_key_proj, preferred_element_type=jnp.float32)
    grad_value_w = jnp.dot(hidden_one.T, grad_value_proj, preferred_element_type=jnp.float32)
    grad_router = jnp.dot(hidden_two.T, grad_logits, preferred_element_type=jnp.float32)
    summed = (
        lax.psum_scatter(grad_query_w, ("expert", "shard"), scatter_dimension=0, tiled=True),
        lax.psum_scatter(grad_key_w, ("expert", "shard"), scatter_dimension=0, tiled=True),
        lax.psum_scatter(grad_value_w, ("expert", "shard"), scatter_dimension=0, tiled=True),
        lax.psum_scatter(grad_output_w, ("expert", "shard"), scatter_dimension=0, tiled=True),
        lax.psum_scatter(grad_router, ("expert", "shard"), scatter_dimension=0, tiled=True),
        lax.psum_scatter(gains_local, ("expert", "shard"), scatter_dimension=0, tiled=True),
    )
    query_part, key_part, value_part, output_part, router_part, gains_part = summed
    return (
        block_out,
        input_grad,
        query_part,
        key_part,
        value_part,
        output_part,
        router_part,
        gains_part,
        grad_gate[None],
        grad_up[None],
        grad_down[None],
    )


def solution(mesh):
    return jax.shard_map(
        on_device,
        mesh=mesh,
        in_specs=(
            P(("expert", "shard"), None),
            P(("expert", "shard"), None),
            P(("expert", "shard"), None),
            P(("expert", "shard"), None),
            P(("expert", "shard"), None),
            P(("expert", "shard"), None),
            P(("expert", "shard"), None),
            P(("expert", "shard"), None),
            P(("expert", "shard"), None),
            P(("expert", "shard")),
            P(("expert", "shard"), None, None),
            P(("expert", "shard"), None, None),
            P(("expert", "shard"), None, None),
        ),
        out_specs=(
            P(("expert", "shard"), None),
            P(("expert", "shard"), None),
            P(("expert", "shard"), None),
            P(("expert", "shard"), None),
            P(("expert", "shard"), None),
            P(("expert", "shard"), None),
            P(("expert", "shard"), None),
            P(("expert", "shard")),
            P(("expert", "shard"), None, None),
            P(("expert", "shard"), None, None),
            P(("expert", "shard"), None, None),
        ),
        check_vma=False,
    )
```

profile of v0, /device:TPU:0, one launch (start us, length us, event | category | flops | bytes accessed | tf_op | source)
XLA Modules:
  0.0 2218.1 jit_solution(9981403889136243515)
XLA Ops:
  22.9 42.5 %all-reduce = bf16[4352]{0:T(1024)(128)(2,1)S(1)} all-reduce(bf16[4352]{0:T(1024)(128)(2,1)S(1)} %dynamic-update-slice), channel_id=1, replica_groups=mesh['expert'=16,'shard'=2] {'expert','shard'}, use_global_device_ids=true, to_apply=%add | all-reduce | flops 4352 | bytes 17408
  78.1 49.8 %all-gather.6.cloned.1.call-done = bf16[2048,512]{1,0:T(8,128)(2,1)} async-done(((bf16[64,512]{1,0:T(8,128)(2,1)}), bf16[2048,512]{1,0:T(8,128)(2,1)}) %all-gather.6.cloned.1.call-update) | async-done | bytes 2097168 | tf_op jit(solution)/shard_map/all_gather | solution.py:138
  135.3 108.7 %all-gather.10.cloned.1.call-done = bf16[2048,4096]{1,0:T(8,128)(2,1)} async-done(((bf16[64,4096]{1,0:T(8,128)(2,1)}), bf16[2048,4096]{1,0:T(8,128)(2,1)}) %all-gather.10.cloned.1.call-update) | async-done | bytes 16777232 | tf_op jit(solution)/shard_map/all_gather | solution.py:136
  261.2 98.1 %all-gather.12.cloned.1.call-done = bf16[4096,2048]{1,0:T(8,128)(2,1)} async-done(((bf16[128,2048]{1,0:T(8,128)(2,1)}), bf16[4096,2048]{1,0:T(8,128)(2,1)}) %all-gather.12.cloned.1.call-update) | async-done | bytes 16777232 | tf_op jit(solution)/shard_map/all_gather | solution.py:139
  369.7 24.6 %scatter_custom_fusion = bf16[1536,2048]{1,0:T(8,128)(2,1)} fusion(s32[1024]{0:T(1024)} %bitcast.266, bf16[128,2048]{1,0:T(8,128)(2,1)} %multiply_convert_fusion.3, s32[1024]{0:T(1024)} %broadcast_clamp_fusion.1, bf16[]{:T(256)} %constant.65.clone.1), kind=kCustom, calls=%fused_computation.21 | custom fusion | bytes 6291968 | tf_op jit(solution)/shard_map/scatter | solution.py:192
  398.1 140.7 %all-gather = bf16[32,64,32]{1,2,0:T(8,128)(2,1)S(1)} all-gather(bf16[1,64,32]{1,2,0:T(8,128)(2,1)S(1)} %bitcast.270), channel_id=1, replica_groups=mesh['expert'=16,'shard'=2] {'expert','shard'}, dimensions={0}, use_global_device_ids=true | all-gather | bytes 135168 | tf_op jit(solution)/shard_map/all_gather | solution.py:140
  547.6 11.0 scatter_custom_fusion.1
  558.6 27.3 %all-to-all-start.2 = ((bf16[32,48,2048]{2,1,0:T(8,128)(2,1)}), bf16[32,48,2048]{2,1,0:T(8,128)(2,1)}, u32[]{:S(2)}, u32[]{:S(2)}) async-start(bf16[32,48,2048]{2,1,0:T(8,128)(2,1)} %bitcast.241), calls=%async_computation.2 | async-start | bytes 12582912 | tf_op jit(solution)/shard_map/all_to_all | solution.py:242
  604.1 121.9 %all-to-all-done.2 = bf16[32,48,2048]{2,1,0:T(8,128)(2,1)} async-done(((bf16[32,48,2048]{2,1,0:T(8,128)(2,1)}), bf16[32,48,2048]{2,1,0:T(8,128)(2,1)}, u32[]{:S(2)}, u32[]{:S(2)}) %all-to-all-start.2) | async-done | bytes 6291488 | tf_op jit(solution)/shard_map/all_to_all | solution.py:242
  726.0 12.3 multiply_convert_fusion
  763.9 125.4 %all-to-all-done.1 = bf16[32,48,2048]{2,1,0:T(8,128)(2,1)} async-done(((bf16[32,48,2048]{2,1,0:T(8,128)(2,1)}), bf16[32,48,2048]{2,1,0:T(8,128)(2,1)}, u32[]{:S(2)}, u32[]{:S(2)}) %all-to-all-start.1) | async-done | bytes 6291488 | tf_op jit(solution)/shard_map/all_to_all | solution.py:210
  893.8 12.5 gather_fusion
  912.3 120.6 %all-to-all-done.3 = bf16[32,48,2048]{2,1,0:T(8,128)(2,1)} async-done(((bf16[32,48,2048]{2,1,0:T(8,128)(2,1)}), bf16[32,48,2048]{2,1,0:T(8,128)(2,1)}, u32[]{:S(2)}, u32[]{:S(2)}) %all-to-all-start.3) | async-done | bytes 6291488 | tf_op jit(solution)/shard_map/all_to_all | solution.py:262
  1032.8 12.8 gather_fusion.1
  1056.8 11.5 fusion.35
  1109.4 13.3 fusion.78
  1124.2 13.5 fusion.52
  1159.3 10.2 convolution_bitcast_fusion.2
  1169.5 12.4 fusion.90
  1186.7 37.5 %all-reduce.1 = f32[4352]{0:T(1024)S(1)} all-reduce(f32[4352]{0:T(1024)S(1)} %pad_maximum_fusion.5), channel_id=7, replica_groups=mesh['expert'=16,'shard'=2] {'expert','shard'}, use_global_device_ids=true, to_apply=%region_38.39.clone | all-reduce | flops 4352 | bytes 34816
  1229.4 121.9 %reduce-scatter.12.cloned.1.call-done = f32[64,512]{1,0:T(8,128)} async-done(((f32[2048,512]{1,0:T(8,128)}), f32[64,512]{1,0:T(8,128)}) %reduce-scatter.12.cloned.1.call-update) | async-done | bytes 131088 | tf_op jit(solution)/shard_map/reduce_scatter | solution.py:319
  1351.2 141.7 %reduce-scatter.10.cloned.1.call-done = f32[64,512]{1,0:T(8,128)} async-done(((f32[2048,512]{1,0:T(8,128)}), f32[64,512]{1,0:T(8,128)}) %reduce-scatter.10.cloned.1.call-update) | async-done | bytes 131088 | tf_op jit(solution)/shard_map/reduce_scatter | solution.py:318
  1492.9 353.2 %reduce-scatter.8.cloned.1.call-done = f32[64,4096]{1,0:T(8,128)} async-done(((f32[2048,4096]{1,0:T(8,128)}), f32[64,4096]{1,0:T(8,128)}) %reduce-scatter.8.cloned.1.call-update) | async-done | bytes 1048592 | tf_op jit(solution)/shard_map/reduce_scatter | solution.py:317
  1846.1 365.0 %reduce-scatter.14.cloned.1.call-done = f32[128,2048]{1,0:T(8,128)} async-done(((f32[4096,2048]{1,0:T(8,128)}), f32[128,2048]{1,0:T(8,128)}) %reduce-scatter.14.cloned.1.call-update) | async-done | bytes 1048592 | tf_op jit(solution)/shard_map/reduce_scatter | solution.py:320
  (287 shorter events, 214.5 us)
Async XLA Ops:
  7.2 718.8 %copy-start = (bf16[1,768,2048]{2,1,0:T(8,128)(2,1)S(1)}, bf16[1,768,2048]{2,1,0:T(8,128)(2,1)}, u32[]{:S(2)}) copy-start(bf16[1,768,2048]{2,1,0:T(8,128)(2,1)} %param.25) | copy-start | bytes 9437188
  7.2 64.5 %all-gather.8.cloned.1.call-start = ((), (), s32[]{:S(2)}) async-start(), calls=%async_computation.10 | async-start | bytes 2162688 | tf_op jit(solution)/shard_map/all_gather | solution.py:137
  7.9 120.0 %all-gather.6.cloned.1.call-start = ((), (), s32[]{:S(2)}) async-start(), calls=%async_computation.9 | async-start | bytes 2162688 | tf_op jit(solution)/shard_map/all_gather | solution.py:138
  8.7 235.3 %all-gather.10.cloned.1.call-start = ((), (), s32[]{:S(2)}) async-start(), calls=%async_computation.11 | async-start | bytes 17301504 | tf_op jit(solution)/shard_map/all_gather | solution.py:136
  9.4 349.9 %all-gather.12.cloned.1.call-start = ((), (), s32[]{:S(2)}) async-start(), calls=%async_computation.12 | async-start | bytes 17301504 | tf_op jit(solution)/shard_map/all_gather | solution.py:139
  70.8 297.1 %copy-start.42 = (f32[2048]{0:T(1024)}, f32[2048]{0:T(1024)S(1)}, u32[]{:S(2)}) copy-start(f32[2048]{0:T(1024)S(1)} %get-tuple-element.42) | copy-start | bytes 24580
  74.0 178.4 %copy-start.23 = (f32[128,512]{1,0:T(8,128)}, f32[128,512]{1,0:T(8,128)S(1)}, u32[]{:S(2)}) copy-start(f32[128,512]{1,0:T(8,128)S(1)} %fusion.82) | copy-start | bytes 786436
  367.8 26.5 %copy-start.61 = (f32[128]{0:T(128)}, f32[128]{0:T(128)S(1)}, u32[]{:S(2)}) copy-start(f32[128]{0:T(128)S(1)} %add_rsqrt_fusion.2) | copy-start | bytes 1540
  394.4 164.2 %all-to-all-start = ((bf16[32,48,2048]{2,1,0:T(8,128)(2,1)}), bf16[32,48,2048]{2,1,0:T(8,128)(2,1)}, u32[]{:S(2)}, u32[]{:S(2)}) async-start(bf16[32,48,2048]{2,1,0:T(8,128)(2,1)} %bitcast.240), calls=%async_computation | async-start | bytes 12582912 | tf_op jit(solution)/shard_map/all_to_all | solution.py:194
  398.1 146.2 %copy-start.47 = (s32[128,8]{0,1:T(8,128)S(1)}, s32[128,8]{0,1:T(8,128)}, u32[]{:S(2)}) copy-start(s32[128,8]{0,1:T(8,128)} %param.15) | copy-start | bytes 12292
  558.6 167.4 %all-to-all-start.2 = ((bf16[32,48,2048]{2,1,0:T(8,128)(2,1)}), bf16[32,48,2048]{2,1,0:T(8,128)(2,1)}, u32[]{:S(2)}, u32[]{:S(2)}) async-start(bf16[32,48,2048]{2,1,0:T(8,128)(2,1)} %bitcast.241), calls=%async_computation.2 | async-start | bytes 12582912 | tf_op jit(solution)/shard_map/all_to_all | solution.py:242
  745.4 143.9 %all-to-all-start.1 = ((bf16[32,48,2048]{2,1,0:T(8,128)(2,1)}), bf16[32,48,2048]{2,1,0:T(8,128)(2,1)}, u32[]{:S(2)}, u32[]{:S(2)}) async-start(bf16[32,48,2048]{2,1,0:T(8,128)(2,1)} %bitcast.254), calls=%async_computation.1 | async-start | bytes 12582912 | tf_op jit(solution)/shard_map/all_to_all | solution.py:210
  889.3 143.5 %all-to-all-start.3 = ((bf16[32,48,2048]{2,1,0:T(8,128)(2,1)}), bf16[32,48,2048]{2,1,0:T(8,128)(2,1)}, u32[]{:S(2)}, u32[]{:S(2)}) async-start(bf16[32,48,2048]{2,1,0:T(8,128)(2,1)} %bitcast.253), calls=%async_computation.3 | async-start | bytes 12582912 | tf_op jit(solution)/shard_map/all_to_all | solution.py:262
  893.1 334.9 %reduce-scatter.16.cloned.1.call-start = ((), (), s32[]{:S(2)}) async-start(), calls=%async_computation.17 | async-start | bytes 1081344
  893.8 12.5 copy-start.16
  1056.8 12.7 copy-start.38
  1056.8 12.7 copy-start.41
  1074.5 276.7 %reduce-scatter.12.cloned.1.call-start = ((), (), s32[]{:S(2)}) async-start(), calls=%async_computation.15 | async-start | bytes 4325376 | tf_op jit(solution)/shard_map/reduce_scatter | solution.py:319
  1079.8 413.1 %reduce-scatter.10.cloned.1.call-start = ((), (), s32[]{:S(2)}) async-start(), calls=%async_computation.14 | async-start | bytes 4325376 | tf_op jit(solution)/shard_map/reduce_scatter | solution.py:318
  1087.9 758.2 %reduce-scatter.8.cloned.1.call-start = ((), (), s32[]{:S(2)}) async-start(), calls=%async_computation.13 | async-start | bytes 34603008 | tf_op jit(solution)/shard_map/reduce_scatter | solution.py:317
  1122.7 1088.4 %reduce-scatter.14.cloned.1.call-start = ((), (), s32[]{:S(2)}) async-start(), calls=%async_computation.16 | async-start | bytes 34603008 | tf_op jit(solution)/shard_map/reduce_scatter | solution.py:320
  1149.3 10.0 copy-start.68
  1159.3 10.2 copy-start.15
  1181.9 1029.2 %copy-start.1 = (bf16[1,768,2048]{2,1,0:T(8,128)(2,1)S(1)}, bf16[1,768,2048]{2,1,0:T(8,128)(2,1)}, u32[]{:S(2)}) copy-start(bf16[1,768,2048]{2,1,0:T(8,128)(2,1)} %param.25) | copy-start | bytes 9437188
  (60 other events, 168.3 us)
Sparse Core Ops, SparseCore 0:
  10.9 59.0 all-gather.7
  72.8 55.0 all-gather.5
  130.8 113.1 all-gather.9
  246.7 112.5 all-gather.11
  1074.6 134.9 reduce-scatter.15
  1212.2 138.9 reduce-scatter.11
  1354.1 138.8 reduce-scatter.9
  1495.8 350.2 reduce-scatter.7
  1849.0 362.0 reduce-scatter.13
where the time goes:
time: 2230 us; the launch traced here: 2220 us
  waiting for transfers between devices  1610 us (72%)
  blocking collectives  221 us (10%)
  matrix products  176 us (8%)
  local copies, waits for them, and re-layouts  87.9 us (4%)
  other arithmetic  69.7 us (3%)
  starting transfers between devices  39.5 us (2%)
    reduce_scatter x1, waiting for transfers between devices, on_device(): lax.psum_scatter(grad_output_w, ('expert', 'shard'), scatter_dimension=0,...  365 us
    reduce_scatter x1, waiting for transfers between devices, on_device(): lax.psum_scatter(grad_query_w, ('expert', 'shard'), scatter_dimension=0,...  353 us
    reduce_scatter x1, waiting for transfers between devices, on_device(): lax.psum_scatter(grad_key_w, ('expert', 'shard'), scatter_dimension=0, ti...  142 us
    all_gather x1, blocking collectives, on_device(): lax.all_gather(router_weight, ('expert', 'shard'), axis=0, tiled=True)  141 us
    all_to_all x1, waiting for transfers between devices, on_device(): lax.all_to_all(expert_out.reshape(experts, capacity, D), ('expert', 'shar...  125 us
    all_to_all x1, waiting for transfers between devices, on_device(): lax.all_to_all(outgoing_grad.reshape(experts, capacity, D), ('expert', 's...  122 us
    reduce_scatter x1, waiting for transfers between devices, on_device(): lax.psum_scatter(grad_value_w, ('expert', 'shard'), scatter_dimension=0,...  122 us
    all_to_all x1, waiting for transfers between devices, on_device(): lax.all_to_all(grad_rows.reshape(experts, capacity, D), ('expert', 'shard...  121 us
  transfers between devices with their start and end apart: 13, of which 10 were waited for; matrix products, arithmetic and copies ran while one was open for 10% of the time, Pallas kernels for 0%

commit v1 on v0

v1 whole, which is shorter than its diff:
```python
import jax
import jax.numpy as jnp
from jax import lax
from jax.sharding import Mesh
from jax.sharding import PartitionSpec as P

D = 2048
HEADS = 32
KV_HEADS = 4
HEAD_DIM = 128
TOP = 8

epsilon = 1e-06
rope_base = 1000000.0
masked_score = -1e30

GROUPS = HEADS // KV_HEADS
Q_COLS = GROUPS * HEAD_DIM
LINE = "line"
PLANE = ("plane", "core")
ALL = ("line", "plane", "core")
F32 = jnp.float32
BF16 = jnp.bfloat16


def dot(left, right):
    return jnp.dot(left, right, preferred_element_type=F32)


def rms_scale(values):
    return lax.rsqrt(jnp.mean(values * values, axis=-1, keepdims=True) + epsilon)


def norm_back(upstream, normed, scale_rows):
    return scale_rows * (upstream - normed * jnp.mean(upstream * normed, axis=-1, keepdims=True))


def sequence_layout(lengths_row, row_count):
    seq_ends = jnp.cumsum(lengths_row)
    places = jnp.arange(row_count, dtype=jnp.int32)
    segment = jnp.sum((places[:, None] >= seq_ends[None, :]).astype(jnp.int32), axis=1)
    starts = seq_ends - lengths_row
    member = segment[:, None] == jnp.arange(lengths_row.shape[0], dtype=jnp.int32)[None, :]
    seg_start = jnp.sum(jnp.where(member, starts[None, :], 0), axis=1)
    return (segment, places - seg_start)


def rope_tables(positions, head_dim):
    half_dim = head_dim // 2
    inverse = rope_base ** (-2.0 * jnp.arange(half_dim, dtype=F32) / head_dim)
    angles = positions.astype(F32)[..., None] * inverse
    return (jnp.cos(angles), jnp.sin(angles))


def rotate(values, cosine, sine_table):
    half_dim = values.shape[-1] // 2
    first_half = values[..., :half_dim]
    second_half = values[..., half_dim:]
    return jnp.concatenate(
        [
            first_half * cosine - second_half * sine_table,
            second_half * cosine + first_half * sine_table,
        ],
        axis=-1,
    )


def masked_scores(query, keys, allowed, score_scale):
    scores = jnp.einsum("bqgd,bsd->bgqs", query, keys, preferred_element_type=F32) * score_scale
    return jnp.where(allowed[:, None], scores, masked_score)


def attend(query, keys, values_in, allowed, score_scale):
    scores = masked_scores(query, keys, allowed, score_scale)
    top_score = jnp.max(scores, axis=-1, keepdims=True)
    exponent = jnp.exp(scores - top_score)
    row_total = jnp.sum(exponent, axis=-1, keepdims=True)
    attn_probs = (exponent / row_total).astype(BF16)
    mixed_heads = jnp.einsum("bgqs,bsd->bqgd", attn_probs, values_in, preferred_element_type=F32)
    return (mixed_heads, top_score + jnp.log(row_total))


def attend_back(query, keys, values_in, allowed, score_scale, log_total, grad_mixed):
    scores = masked_scores(query, keys, allowed, score_scale)
    attn_probs = jnp.exp(scores - log_total)
    grad_probs = jnp.einsum("bqgd,bsd->bgqs", grad_mixed, values_in, preferred_element_type=F32)
    grad_scores = (
        attn_probs * (grad_probs - jnp.sum(attn_probs * grad_probs, axis=-1, keepdims=True))
    ).astype(BF16)
    grad_query = (
        jnp.einsum("bgqs,bsd->bqgd", grad_scores, keys, preferred_element_type=F32) * score_scale
    )
    grad_keys = (
        jnp.einsum("bgqs,bqgd->bsd", grad_scores, query, preferred_element_type=F32) * score_scale
    )
    grad_values = jnp.einsum(
        "bgqs,bqgd->bsd", attn_probs.astype(BF16), grad_mixed, preferred_element_type=F32
    )
    return (grad_query, grad_keys, grad_values)


def on_device(
    tokens,
    lengths,
    routes,
    cotangent,
    query_weight,
    key_weight,
    value_weight,
    output_weight,
    router_weight,
    norm_gains,
    gate_weight,
    up_weight,
    down_weight,
):
    rows = tokens.shape[0]
    lines = lax.axis_size("line")
    cells = lax.axis_size("plane") * lax.axis_size("core")
    experts = lines * cells
    capacity = (3 * rows * TOP + 2 * experts - 1) // (2 * experts)
    score_scale = HEAD_DIM ** (-0.5)
    large = experts > 32
    own_rows = query_weight.shape[0]
    line = lax.axis_index("line")
    me = (line * lax.axis_size("plane") + lax.axis_index("plane")) * lax.axis_size(
        "core"
    ) + lax.axis_index("core")

    packed = jnp.concatenate(
        [
            query_weight.reshape(own_rows, lines, Q_COLS),
            key_weight.reshape(own_rows, lines, HEAD_DIM),
            value_weight.reshape(own_rows, lines, HEAD_DIM),
        ],
        axis=2,
    ).transpose(1, 0, 2)
    width = packed.shape[2]
    packed = lax.all_to_all(packed, LINE, split_axis=0, concat_axis=0, tiled=True)
    packed = lax.all_gather(packed, PLANE, axis=1, tiled=False)
    weight_qkv = packed.reshape(lines * cells * own_rows, width)
    weight_o = lax.all_gather(output_weight, PLANE, axis=0, tiled=True)
    gains = lax.all_gather(norm_gains, ALL, axis=0, tiled=True).astype(F32)
    router = lax.all_gather(router_weight, ALL, axis=0, tiled=True)
    gain_attn = gains[:D]
    gain_ffn = gains[D : 2 * D]
    gain_query = gains[2 * D : 2 * D + HEAD_DIM]
    gain_key = gains[2 * D + HEAD_DIM :]

    routes_all = lax.all_gather(routes, ALL, axis=0, tiled=True)

    line_tokens = lax.all_gather(tokens, LINE, axis=0, tiled=True)
    line_lengths = lax.all_gather(lengths, LINE, axis=0, tiled=True)
    inputs = line_tokens.astype(F32)
    attn_scale = rms_scale(inputs)
    attn_normed = inputs * attn_scale
    hidden_one = (attn_normed * gain_attn).astype(BF16)
    proj = dot(hidden_one, weight_qkv)
    query_proj = proj[:, :Q_COLS].reshape(lines, rows, GROUPS, HEAD_DIM)
    key_proj = proj[:, Q_COLS : Q_COLS + HEAD_DIM].reshape(lines, rows, HEAD_DIM)
    value_proj = proj[:, Q_COLS + HEAD_DIM :].astype(BF16).reshape(lines, rows, HEAD_DIM)
    query_scale = rms_scale(query_proj)
    query_normed = query_proj * query_scale
    key_scale = rms_scale(key_proj)
    key_normed = key_proj * key_scale
    segment, positions = jax.vmap(lambda row: sequence_layout(row, rows))(line_lengths)
    cosine, sine_table = rope_tables(positions, HEAD_DIM)
    query_rot = rotate(
        query_normed * gain_query, cosine[:, :, None], sine_table[:, :, None]
    ).astype(BF16)
    key_rot = rotate(key_normed * gain_key, cosine, sine_table).astype(BF16)
    allowed = (segment[:, :, None] == segment[:, None, :]) & (
        positions[:, None, :] <= positions[:, :, None]
    )
    mixed_heads, log_total = attend(query_rot, key_rot, value_proj, allowed, score_scale)
    mixed_low = mixed_heads.reshape(lines * rows, Q_COLS).astype(BF16)
    projected = lax.psum_scatter(dot(mixed_low, weight_o), LINE, scatter_dimension=0, tiled=True)
    own_inputs = tokens.astype(F32)
    residual = own_inputs + projected
    ffn_scale = rms_scale(residual)
    ffn_normed = residual * ffn_scale
    hidden_two = (ffn_normed * gain_ffn).astype(BF16)

    hidden_all = lax.all_gather(hidden_two, ALL, axis=0, tiled=True)
    logits = dot(hidden_all, router)
    expert_ids = jnp.arange(experts, dtype=jnp.int32)
    picked = jnp.any(routes_all[:, :, None] == expert_ids, axis=1)
    masked = jnp.where(picked, logits, masked_score)
    exponent = jnp.where(picked, jnp.exp(masked - jnp.max(masked, axis=1, keepdims=True)), 0.0)
    weights_all = exponent / jnp.sum(exponent, axis=1, keepdims=True)
    mine = jnp.any(routes_all == me, axis=1).reshape(experts, rows)
    weight_mine = jnp.sum(jnp.where(expert_ids == me, weights_all, 0.0), axis=1).reshape(
        experts, rows
    )
    rank = jnp.cumsum(mine.astype(jnp.int32), axis=1) - 1
    slots = jnp.arange(capacity, dtype=jnp.int32)
    select = (rank[:, None, :] == slots[None, :, None]) & mine[:, None, :]
    select_low = select.astype(BF16)
    slot_weight = jnp.sum(jnp.where(select, weight_mine[:, None, :], 0.0), axis=2).reshape(-1, 1)

    def pick(values):
        return jnp.einsum(
            "sjt,std->sjd",
            select_low,
            values.reshape(experts, rows, D),
            preferred_element_type=F32,
        ).reshape(experts * capacity, D)

    def place(values):
        return (
            jnp.einsum(
                "sjt,sjd->std",
                select_low,
                values.reshape(experts, capacity, D),
                preferred_element_type=F32,
            )
            .astype(BF16)
            .reshape(experts * rows, D)
        )

    expert_rows = pick(hidden_all).astype(BF16)
    own_columns = lax.dynamic_slice_in_dim(hidden_all, me * own_rows, own_rows, axis=1)
    if large:
        expert_rows, own_columns, cotangent = lax.optimization_barrier(
            (expert_rows, own_columns, cotangent)
        )
    cotangent_all = lax.all_gather(cotangent, ALL, axis=0, tiled=True)
    grad_rows_out = pick(cotangent_all)
    grad_slots = (slot_weight * grad_rows_out).astype(BF16)
    gate_act = dot(expert_rows, gate_weight[0])
    up_act = dot(expert_rows, up_weight[0])
    gate_sig = jax.nn.sigmoid(gate_act)
    gate_silu = gate_act * gate_sig
    expert_hidden = (gate_silu * up_act).astype(BF16)
    grad_expert_hidden = dot(grad_slots, down_weight[0].T)
    grad_gate_act = (
        grad_expert_hidden * up_act * gate_sig * (1.0 + gate_act * (1.0 - gate_sig))
    ).astype(BF16)
    grad_up_act = (grad_expert_hidden * gate_silu).astype(BF16)
    grad_rows_in = (
        dot(grad_gate_act, gate_weight[0].T) + dot(grad_up_act, up_weight[0].T)
    ).astype(BF16)
    expert_out = dot(expert_hidden, down_weight[0]).astype(BF16).astype(F32)
    grad_weight_slot = jnp.sum(grad_rows_out * expert_out, axis=1).reshape(experts, capacity)
    grad_weight_mine = jnp.sum(jnp.where(select, grad_weight_slot[:, :, None], 0.0), axis=1)
    grad_weight = lax.all_gather(grad_weight_mine.reshape(-1), ALL, axis=0, tiled=False).T
    grad_rows_sum = lax.psum_scatter(place(grad_rows_in), ALL, scatter_dimension=0, tiled=True)
    if large:
        expert_out, grad_rows_sum = lax.optimization_barrier((expert_out, grad_rows_sum))
    out_sum = lax.psum_scatter(
        place((slot_weight * expert_out).astype(BF16)), ALL, scatter_dimension=0, tiled=True
    )
    block_out = (residual + out_sum.astype(F32)).astype(BF16)
    grad_down = dot(expert_hidden.T, grad_slots)
    grad_gate = dot(expert_rows.T, grad_gate_act)
    grad_up = dot(expert_rows.T, grad_up_act)

    grad_logits = weights_all * (
        grad_weight - jnp.sum(weights_all * grad_weight, axis=1, keepdims=True)
    )
    grad_logits = grad_logits.astype(BF16)
    router_grad = dot(own_columns.T, grad_logits)
    own_grad_logits = lax.dynamic_slice_in_dim(grad_logits, me * rows, rows, axis=0)

    grad_out = cotangent.astype(F32)
    grad_hidden_two = dot(own_grad_logits, router.T) + grad_rows_sum.astype(F32)
    grad_gain_ffn = jnp.sum(grad_hidden_two * ffn_normed, axis=0)
    grad_residual = grad_out + norm_back(grad_hidden_two * gain_ffn, ffn_normed, ffn_scale)
    grad_attn = lax.all_gather(grad_residual.astype(BF16), LINE, axis=0, tiled=True)
    output_part = dot(mixed_low.T, grad_attn).astype(BF16)
    output_grad = lax.psum_scatter(output_part, PLANE, scatter_dimension=0, tiled=True)
    grad_mixed = dot(grad_attn, weight_o.T).astype(BF16).reshape(lines, rows, GROUPS, HEAD_DIM)
    grad_query_rot, grad_key_rot, grad_value_rot = attend_back(
        query_rot, key_rot, value_proj, allowed, score_scale, log_total, grad_mixed
    )
    grad_value_proj = grad_value_rot.astype(BF16)
    grad_query_gained = rotate(grad_query_rot, cosine[:, :, None], -sine_table[:, :, None])
    grad_gain_query = jnp.sum(grad_query_gained * query_normed, axis=(0, 1, 2))
    grad_query_proj = norm_back(grad_query_gained * gain_query, query_normed, query_scale).astype(
        BF16
    )
    grad_key_gained = rotate(grad_key_rot, cosine, -sine_table)
    grad_gain_key = jnp.sum(grad_key_gained * key_normed, axis=(0, 1))
    grad_key_proj = norm_back(grad_key_gained * gain_key, key_normed, key_scale).astype(BF16)
    grad_proj = jnp.concatenate(
        [
            grad_query_proj.reshape(lines * rows, Q_COLS),
            grad_key_proj.reshape(lines * rows, HEAD_DIM),
            grad_value_proj.reshape(lines * rows, HEAD_DIM),
        ],
        axis=1,
    )
    grad_hidden_one = lax.psum_scatter(
        dot(grad_proj, weight_qkv.T), LINE, scatter_dimension=0, tiled=True
    )
    own_scale = rms_scale(own_inputs)
    own_normed = own_inputs * own_scale
    grad_gain_attn = jnp.sum(grad_hidden_one * own_normed, axis=0)
    input_grad = grad_residual + norm_back(grad_hidden_one * gain_attn, own_normed, own_scale)
    qkv_part = dot(hidden_one.T, grad_proj).astype(BF16).reshape(lines, cells, own_rows, width)
    qkv_part = qkv_part.transpose(1, 0, 2, 3).reshape(cells * lines * own_rows, width)
    qkv_part = lax.psum_scatter(qkv_part, PLANE, scatter_dimension=0, tiled=True)
    qkv_part = qkv_part.reshape(lines, own_rows, width)
    qkv_part = lax.all_to_all(qkv_part, LINE, split_axis=0, concat_axis=0, tiled=True)
    qkv_part = qkv_part.transpose(1, 0, 2).astype(F32)
    query_grad = qkv_part[:, :, :Q_COLS].reshape(own_rows, lines * Q_COLS)
    key_grad = qkv_part[:, :, Q_COLS : Q_COLS + HEAD_DIM].reshape(own_rows, lines * HEAD_DIM)
    value_grad = qkv_part[:, :, Q_COLS + HEAD_DIM :].reshape(own_rows, lines * HEAD_DIM)
    gains_local = jnp.concatenate([grad_gain_attn, grad_gain_ffn, grad_gain_query, grad_gain_key])
    gains_grad = lax.psum_scatter(gains_local, ALL, scatter_dimension=0, tiled=True)
    return (
        block_out,
        input_grad,
        query_grad,
        key_grad,
        value_grad,
        output_grad.astype(F32),
        router_grad,
        gains_grad,
        grad_gate[None],
        grad_up[None],
        grad_down[None],
    )


def solution(mesh):
    chips = mesh.shape["expert"]
    cores = mesh.shape["shard"]
    inner = Mesh(
        mesh.devices.reshape(KV_HEADS, chips // KV_HEADS, cores), ("line", "plane", "core")
    )
    return jax.shard_map(
        on_device,
        mesh=inner,
        in_specs=(
            P(ALL, None),
            P(ALL, None),
            P(ALL, None),
            P(ALL, None),
            P(ALL, None),
            P(ALL, None),
            P(ALL, None),
            P(ALL, None),
            P(ALL, None),
            P(ALL),
            P(ALL, None, None),
            P(ALL, None, None),
            P(ALL, None, None),
        ),
        out_specs=(
            P(ALL, None),
            P(ALL, None),
            P(ALL, None),
            P(ALL, None),
            P(ALL, None),
            P(ALL, None),
            P(ALL, None),
            P(ALL),
            P(ALL, None, None),
            P(ALL, None, None),
            P(ALL, None, None),
        ),
        check_vma=False,
    )
```

time: 2230 us -> 1230 us (0.55)
  waiting for transfers between devices: 1610 us -> 666 us
  local copies, waits for them, and re-layouts: 87.9 us -> 41.7 us
  blocking collectives: 221 us -> 260 us
  starting transfers between devices: 39.5 us -> 5.08 us
    reduce_scatter x4 -> x6, waiting for transfers between devices: 982 us -> 491 us  [the longest x1 178 us: on_device(): lax.psum_scatter(place(grad_rows_in), ALL, scatter_dimension=0, tiled=True)]
    all_to_all x4 -> x1, waiting for transfers between devices: 368 us -> 0.01 us  [on_device(): lax.all_to_all(qkv_part, LINE, split_axis=0, concat_axis=0, tiled=True)]
    all_gather x4 -> x6, waiting for transfers between devices: 257 us -> 172 us  [the longest x1 104 us: on_device(): hidden_all = lax.all_gather(hidden_two, ALL, axis=0, tiled=True)]
    all_to_all x0 -> x1, blocking collectives: none -> 40.4 us  [on_device(): lax.all_to_all(packed, LINE, split_axis=0, concat_axis=0, tiled=True)]
    all_to_all x4 -> x1, starting transfers between devices: 39 us -> 4.59 us  [on_device(): lax.all_to_all(qkv_part, LINE, split_axis=0, concat_axis=0, tiled=True)]
    gather x2 -> x0, local copies, waits for them, and re-layouts: 25.3 us -> none  [the longest x1 12.8 us: on_device(): returned_grad.reshape(experts * capacity, D)[destination]]
    scatter x1 -> x0, local copies, waits for them, and re-layouts: 24.6 us -> none  [on_device(): jnp.zeros((experts * capacity, D), jnp.bfloat16).at[destination]]
    convert_element_type x5 -> x11, other arithmetic: 4.79 us -> 28.9 us  [the longest x2 21.9 us: on_device(): grad_slots = (slot_weight * grad_rows_out).astype(BF16)]
  transfers between devices with their start and end apart: 13 -> 13, of which waited for: 10 -> 10; matrix products, arithmetic and copies ran while one was open for 10% -> 12% of each run, Pallas kernels for 0% -> 0%
where the time goes in v1:
time: 1230 us
  waiting for transfers between devices  666 us (54%)
  blocking collectives  260 us (21%)
  matrix products  177 us (14%)
  other arithmetic  61.1 us (5%)
  local copies, waits for them, and re-layouts  41.7 us (3%)
  between operations  17.1 us (1%)
    reduce_scatter x1, waiting for transfers between devices, on_device(): lax.psum_scatter(place(grad_rows_in), ALL, scatter_dimension=0, tiled=True)  178 us
    reduce_scatter x1, waiting for transfers between devices, on_device(): lax.psum_scatter(place((slot_weight * expert_out).astype(BF16)), ALL, sca...  140 us
    dot_general x18, matrix products, dot(): return jnp.dot(left, right, preferred_element_type=F32)  124 us
    all_gather x1, waiting for transfers between devices, on_device(): hidden_all = lax.all_gather(hidden_two, ALL, axis=0, tiled=True)  104 us
    unnamed x2, blocking collectives  85.1 us
    reduce_scatter x1, waiting for transfers between devices, on_device(): lax.psum_scatter(dot(mixed_low, weight_o), LINE, scatter_dimension=0, til...  84.1 us
    reduce_scatter x1, waiting for transfers between devices, on_device(): lax.psum_scatter(dot(grad_proj, weight_qkv.T), LINE, scatter_dimension=0,...  81.6 us
    all_gather x1, waiting for transfers between devices, on_device(): lax.all_gather(grad_residual.astype(BF16), LINE, axis=0, tiled=True)  47.4 us
  transfers between devices with their start and end apart: 13, of which 10 were waited for; matrix products, arithmetic and copies ran while one was open for 12% of the time, Pallas kernels for 0%

profile of v1, /device:TPU:0, one launch (start us, length us, event | category | flops | bytes accessed | tf_op | source)
XLA Modules:
  0.0 1227.6 jit_solution(14616548618546211668)
XLA Ops:
  14.4 40.4 %all_to_all.10 = bf16[4,64,1280]{2,1,0:T(8,128)(2,1)S(1)} all-to-all(bf16[4,64,1280]{2,1,0:T(8,128)(2,1)S(1)} %copy.154), channel_id=1, replica_groups=mesh['line'=4,'plane'=4,'core'=2] {'line'}, dimensions={0} | all-to-all | bytes 1310720 | tf_op jit(solution)/shard_map/all_to_all | solution.py:139
  56.9 10.6 all-gather.1
  68.0 39.2 %all-reduce = bf16[4352]{0:T(1024)(128)(2,1)S(1)} all-reduce(bf16[4352]{0:T(1024)(128)(2,1)S(1)} %dynamic-update-slice), channel_id=1, replica_groups=mesh['line'=4,'plane'=4,'core'=2] {'line','plane','core'}, use_global_device_ids=true, to_apply=%add | all-reduce | flops 4352 | bytes 17408
  137.4 16.2 %all-gather.13.cloned.1.call-done = bf16[1024,2048]{1,0:T(8,128)(2,1)} async-done(((bf16[128,2048]{1,0:T(8,128)(2,1)}), bf16[1024,2048]{1,0:T(8,128)(2,1)}) %all-gather.13.cloned.1.call-update) | async-done | bytes 4194320 | tf_op jit(solution)/shard_map/all_gather | solution.py:142
  161.2 84.1 %reduce-scatter.7.cloned.1.call-done = f32[128,2048]{1,0:T(8,128)} async-done(((f32[512,2048]{1,0:T(8,128)}), f32[128,2048]{1,0:T(8,128)}) %reduce-scatter.7.cloned.1.call-update) | async-done | bytes 1048592 | tf_op jit(solution)/shard_map/reduce_scatter | solution.py:177
  249.5 44.0 %all_gather.42 = s32[4096,8]{0,1:T(8,128)S(1)} all-gather(s32[128,8]{0,1:T(8,128)S(1)} %copy-done.88), channel_id=1, replica_groups=mesh['line'=4,'plane'=4,'core'=2] {'line','plane','core'}, dimensions={0}, use_global_device_ids=true | all-gather | bytes 135168 | tf_op jit(solution)/shard_map/all_gather | solution.py:150
  295.7 39.6 %all-gather.2 = bf16[32,64,32]{1,2,0:T(8,128)(2,1)S(1)} all-gather(bf16[1,64,32]{1,2,0:T(8,128)(2,1)S(1)} %bitcast.259), channel_id=1, replica_groups=mesh['line'=4,'plane'=4,'core'=2] {'line','plane','core'}, dimensions={0}, use_global_device_ids=true | all-gather | bytes 135168 | tf_op jit(solution)/shard_map/all_gather | solution.py:144
  341.6 12.8 %fusion.55 = f32[32,48,2048]{2,1,0:T(8,128)} fusion(bf16[32,128,2048]{2,1,0:T(8,128)(2,1)} %bitcast.217, s32[32,128]{1,0:T(8,128)S(1)} %broadcast_add_fusion, pred[32,128]{1,0:T(8,128)(4,1)} %bitcast.247), kind=kOutput, calls=%fused_computation.116 | convolution fusion | flops 805699584 | bytes 29380608 | tf_op jit(solution)/shard_map/sjt,std->sjd/dot_general | solution.py:202
  354.3 103.6 %all-gather.15.cloned.1.call-done = bf16[4096,2048]{1,0:T(8,128)(2,1)} async-done(((bf16[128,2048]{1,0:T(8,128)(2,1)}), bf16[4096,2048]{1,0:T(8,128)(2,1)}) %all-gather.15.cloned.1.call-update) | async-done | bytes 16777232 | tf_op jit(solution)/shard_map/all_gather | solution.py:184
  479.2 9.7 fusion.1
  491.4 40.2 %all-gather.3 = f32[32,1,4096]{2,1,0:T(1,128)S(1)} all-gather(f32[1,1,4096]{2,1,0:T(1,128)S(1)} %bitcast.256), channel_id=1, replica_groups=mesh['line'=4,'plane'=4,'core'=2] {'line','plane','core'}, dimensions={0}, use_global_device_ids=true | all-gather | bytes 540672 | tf_op jit(solution)/shard_map/all_gather | solution.py:246
  531.5 11.1 fusion.103
  552.9 12.8 %multiply_convert_fusion.1 = (bf16[1536,768]{1,0:T(8,128)(2,1)}, bf16[1536,768]{1,0:T(8,128)(2,1)}) fusion(f32[1536,768]{1,0:T(8,128)} %copy-done.105, f32[1536,768]{1,0:T(8,128)} %get-tuple-element.60, bf16[1536,2048]{1,0:T(8,128)(2,1)} %bitcast.231, bf16[1,768,2048]{2,1,0:T(8,128)(2,1)S(1)} %copy-done), kind=kOutput, calls=%fused_computation.14 | convolution fusion | flops 4847173632 | bytes 23592960 | tf_op jit(solution)/shard_map/dot_general | solution.py:27
  580.3 13.1 %convolution_convert_fusion = bf16[32,128,2048]{2,1,0:T(8,128)(2,1)} fusion(bf16[32,48,2048]{2,1,0:T(8,128)(2,1)} %bitcast.232, s32[32,128]{1,0:T(8,128)S(1)} %broadcast_add_fusion, pred[32,128]{1,0:T(8,128)(4,1)S(1)} %bitcast.251), kind=kOutput, calls=%fused_computation.2 | convolution fusion | flops 814088192 | bytes 23089152 | tf_op jit(solution)/shard_map/sjt,sjd->std/dot_general | solution.py:211
  595.1 177.5 %reduce-scatter.11.cloned.1.call-done = bf16[128,2048]{1,0:T(8,128)(2,1)} async-done(((bf16[4096,2048]{1,0:T(8,128)(2,1)}), bf16[128,2048]{1,0:T(8,128)(2,1)}) %reduce-scatter.11.cloned.1.call-update) | async-done | bytes 524304 | tf_op jit(solution)/shard_map/reduce_scatter | solution.py:247
  776.0 47.4 %all-gather.19.cloned.1.call-done = bf16[512,2048]{1,0:T(8,128)(2,1)} async-done(((bf16[128,2048]{1,0:T(8,128)(2,1)}), bf16[512,2048]{1,0:T(8,128)(2,1)}) %all-gather.19.cloned.1.call-update) | async-done | bytes 2097168 | tf_op jit(solution)/shard_map/all_gather | solution.py:269
  870.3 13.9 %fusion.2 = (bf16[1536,2048]{1,0:T(8,128)(2,1)}, bf16[1536,2048]{1,0:T(8,128)(2,1)}) fusion(f32[32,48,2048]{2,1,0:T(8,128)} %fusion.55, f32[1536]{0:T(1024)S(1)} %mul.461, bf16[1536,2048]{1,0:T(8,128)(2,1)} %get-tuple-element.62), kind=kLoop, calls=%fused_computation.7 | loop fusion | flops 15728640 | bytes 31463424 | tf_op jit(solution)/shard_map/convert_element_type | solution.py:229
  884.2 14.5 %convolution_convert_fusion.1 = bf16[32,128,2048]{2,1,0:T(8,128)(2,1)} fusion(bf16[32,48,2048]{2,1,0:T(8,128)(2,1)} %bitcast.218, s32[32,128]{1,0:T(8,128)S(1)} %broadcast_add_fusion, pred[32,128]{1,0:T(8,128)(4,1)S(1)} %bitcast.252), kind=kOutput, calls=%fused_computation.3 | convolution fusion | flops 814088192 | bytes 23089152 | tf_op jit(solution)/shard_map/sjt,sjd->std/dot_general | solution.py:211
  901.9 9.8 convolution_bitcast_fusion.1
  911.7 10.1 convolution_bitcast_fusion.2
  931.4 8.4 reduce-scatter.15.cloned.1.call-done
  944.4 81.6 %reduce-scatter.13.cloned.1.call-done = f32[128,2048]{1,0:T(8,128)} async-done(((f32[512,2048]{1,0:T(8,128)}), f32[128,2048]{1,0:T(8,128)}) %reduce-scatter.13.cloned.1.call-update) | async-done | bytes 1048592 | tf_op jit(solution)/shard_map/reduce_scatter | solution.py:293
  1027.6 45.9 %all-reduce.1 = f32[4352]{0:T(1024)S(1)} all-reduce(f32[4352]{0:T(1024)S(1)} %pad_maximum_fusion.8), channel_id=9, replica_groups=mesh['line'=4,'plane'=4,'core'=2] {'line','plane','core'}, use_global_device_ids=true, to_apply=%region_36.37.clone | all-reduce | flops 4352 | bytes 34816
  1074.2 139.6 %reduce-scatter.9.cloned.1.call-done = bf16[128,2048]{1,0:T(8,128)(2,1)} async-done(((bf16[4096,2048]{1,0:T(8,128)(2,1)}), bf16[128,2048]{1,0:T(8,128)(2,1)}) %reduce-scatter.9.cloned.1.call-update) | async-done | bytes 524304 | tf_op jit(solution)/shard_map/reduce_scatter | solution.py:250
  (362 shorter events, 184.5 us)
Async XLA Ops:
  8.0 471.2 %copy-start = (bf16[1,768,2048]{2,1,0:T(8,128)(2,1)S(1)}, bf16[1,768,2048]{2,1,0:T(8,128)(2,1)}, u32[]{:S(2)}) copy-start(bf16[1,768,2048]{2,1,0:T(8,128)(2,1)} %param.25) | copy-start | bytes 9437188
  8.0 100.8 %all-gather.11.cloned.1.call-start = ((), (), s32[]{:S(2)}) async-start(), calls=%async_computation.8 | async-start | bytes 2621440 | tf_op jit(solution)/shard_map/all_gather | solution.py:152
  8.8 106.4 %all-gather.21.cloned.1.call-start = ((), (), s32[]{:S(2)}) async-start(), calls=%async_computation.19 | async-start | bytes 5898240 | tf_op jit(solution)/shard_map/all_gather | solution.py:140
  56.1 97.5 %all-gather.13.cloned.1.call-start = ((), (), s32[]{:S(2)}) async-start(), calls=%async_computation.9 | async-start | bytes 4718592 | tf_op jit(solution)/shard_map/all_gather | solution.py:142
  56.9 188.4 %reduce-scatter.7.cloned.1.call-start = ((), (), s32[]{:S(2)}) async-start(), calls=%async_computation.10 | async-start | bytes 5242880 | tf_op jit(solution)/shard_map/reduce_scatter | solution.py:177
  160.6 181.0 %all-gather.17.cloned.1.call-start = ((), (), s32[]{:S(2)}) async-start(), calls=%async_computation.13 | async-start | bytes 17301504 | tf_op jit(solution)/shard_map/all_gather | solution.py:227
  161.2 296.8 %all-gather.15.cloned.1.call-start = ((), (), s32[]{:S(2)}) async-start(), calls=%async_computation.11 | async-start | bytes 17301504 | tf_op jit(solution)/shard_map/all_gather | solution.py:184
  249.4 523.2 %reduce-scatter.11.cloned.1.call-start = ((), (), s32[]{:S(2)}) async-start(), calls=%async_computation.14 | async-start | bytes 17301504 | tf_op jit(solution)/shard_map/reduce_scatter | solution.py:247
  593.5 179.1 %copy-start.8 = (f32[128,2048]{1,0:T(8,128)S(1)}, f32[128,2048]{1,0:T(8,128)}, u32[]{:S(2)}) copy-start(f32[128,2048]{1,0:T(8,128)} %copy-done.7) | copy-start | bytes 3145732
  593.5 179.1 %copy-start.32 = (bf16[2048,32]{0,1:T(8,128)(2,1)S(1)}, bf16[2048,32]{0,1:T(8,128)(2,1)}, u32[]{:S(2)}) copy-start(bf16[2048,32]{0,1:T(8,128)(2,1)} %reshape.302) | copy-start | bytes 393220
  593.5 179.1 %copy-start.58 = (f32[2048]{0:T(1024)S(1)}, f32[2048]{0:T(1024)}, u32[]{:S(2)}) copy-start(f32[2048]{0:T(1024)} %copy-done.57) | copy-start | bytes 24580
  593.5 181.2 %copy-start.28 = (bf16[128,2048]{1,0:T(8,128)(2,1)S(1)}, bf16[128,2048]{1,0:T(8,128)(2,1)}, u32[]{:S(2)}) copy-start(bf16[128,2048]{1,0:T(8,128)(2,1)} %param.16) | copy-start | bytes 1572868
  593.5 229.9 %all-gather.19.cloned.1.call-start = ((), (), s32[]{:S(2)}) async-start(), calls=%async_computation.15 | async-start | bytes 2621440 | tf_op jit(solution)/shard_map/all_gather | solution.py:269
  595.0 180.9 %copy-start.38 = (bf16[4096,32]{0,1:T(8,128)(2,1)}, bf16[4096,32]{0,1:T(8,128)(2,1)S(1)}, u32[]{:S(2)}) copy-start(bf16[4096,32]{0,1:T(8,128)(2,1)S(1)} %fusion.65) | copy-start | bytes 786436
  775.9 153.2 %reduce-scatter.17.cloned.1.call-start = ((), (), s32[]{:S(2)}) async-start(), calls=%async_computation.18 | async-start | bytes 4718592 | tf_op jit(solution)/shard_map/reduce_scatter | solution.py:271
  829.7 110.1 %reduce-scatter.15.cloned.1.call-start = ((), (), s32[]{:S(2)}) async-start(), calls=%async_computation.17 | async-start | bytes 5898240 | tf_op jit(solution)/shard_map/reduce_scatter | solution.py:302
  861.3 164.6 %reduce-scatter.13.cloned.1.call-start = ((), (), s32[]{:S(2)}) async-start(), calls=%async_computation.16 | async-start | bytes 5242880 | tf_op jit(solution)/shard_map/reduce_scatter | solution.py:293
  869.5 344.2 %reduce-scatter.9.cloned.1.call-start = ((), (), s32[]{:S(2)}) async-start(), calls=%async_computation.12 | async-start | bytes 17301504 | tf_op jit(solution)/shard_map/reduce_scatter | solution.py:250
  929.0 284.7 %copy-start.21 = (f32[128,2048]{1,0:T(8,128)S(1)}, f32[128,2048]{1,0:T(8,128)}, u32[]{:S(2)}) copy-start(f32[128,2048]{1,0:T(8,128)} %copy-done.20) | copy-start | bytes 3145732
  929.0 284.7 %copy-start.29 = (bf16[128,2048]{1,0:T(8,128)(2,1)S(1)}, bf16[128,2048]{1,0:T(8,128)(2,1)}, u32[]{:S(2)}) copy-start(bf16[128,2048]{1,0:T(8,128)(2,1)} %param.16) | copy-start | bytes 1572868
  929.0 284.7 %copy-start.59 = (f32[2048]{0:T(1024)S(1)}, f32[2048]{0:T(1024)}, u32[]{:S(2)}) copy-start(f32[2048]{0:T(1024)} %copy-done.57) | copy-start | bytes 24580
  929.0 284.7 %copy-start.87 = (f32[128]{0:T(128)S(1)}, f32[128]{0:T(128)}, u32[]{:S(2)}) copy-start(f32[128]{0:T(128)} %copy-done.85) | copy-start | bytes 1540
  929.0 284.7 %copy-start.91 = (f32[128]{0:T(128)S(1)}, f32[128]{0:T(128)}, u32[]{:S(2)}) copy-start(f32[128]{0:T(128)} %copy-done.90) | copy-start | bytes 1540
  939.8 276.9 %all-to-all-start.1 = ((bf16[4,64,1280]{2,1,0:T(8,128)(2,1)}), bf16[4,64,1280]{2,1,0:T(8,128)(2,1)}, u32[]{:S(2)}, u32[]{:S(2)}) async-start(bf16[4,64,1280]{2,1,0:T(8,128)(2,1)} %bitcast.244), calls=%async_computation.6 | async-start | bytes 1310720 | tf_op jit(solution)/shard_map/all_to_all | solution.py:304
  (101 other events, 1443.1 us)
Sparse Core Ops, SparseCore 0:
  10.4 61.5 all-gather.10
  74.5 40.6 all-gather.20
  117.1 36.5 all-gather.12
  160.7 84.5 reduce-scatter.6
  776.1 47.3 all-gather.18
  829.9 49.9 reduce-scatter.16
  883.2 56.5 reduce-scatter.14
  942.1 83.8 reduce-scatter.12
  1028.3 185.4 reduce-scatter.8
Sparse Core Ops, SparseCore 1:
  163.9 177.6 all-gather.16
  344.9 113.0 all-gather.14
  593.6 178.9 reduce-scatter.10

commit v2 on v1

--- a/solution.py
+++ b/solution.py
@@ -1,6 +1,8 @@
 import jax
 import jax.numpy as jnp
 from jax import lax
+from jax.experimental import pallas as pl
+from jax.experimental.pallas import tpu as pltpu
 from jax.sharding import Mesh
 from jax.sharding import PartitionSpec as P
 
@@ -21,6 +23,8 @@
 ALL = ("line", "plane", "core")
 F32 = jnp.float32
 BF16 = jnp.bfloat16
+MESH = pl.DeviceIdType.MESH
+DMA = pltpu.SemaphoreType.DMA
 
 
 def dot(left, right):
@@ -97,6 +101,492 @@
         "bgqs,bqgd->bsd", attn_probs.astype(BF16), grad_mixed, preferred_element_type=F32
     )
     return (grad_query, grad_keys, grad_values)
+
+
+class Spot:
+    def __init__(self, lines):
+        self.lines = lines
+        self.z = lax.axis_index("line")
+        self.b = lax.axis_index("plane")
+        self.c = lax.axis_index("core")
+        self.xn = self.b + 1 - 2 * (self.b % 2)
+        self.yn = (self.b + 2) % 4
+        self.dg = 3 - self.b
+
+    def each(self, d, fn):
+        if d == 0:
+            fn(self.z, 0)
+            return
+
+        @pl.when(self.z - d >= 0)
+        def _():
+            fn(self.z - d, 1)
+
+        @pl.when(self.z + d < self.lines)
+        def _():
+            fn(self.z + d, -1)
+
+    def greet(self):
+        sem = pltpu.get_barrier_semaphore()
+
+        def tell(dev):
+            pl.semaphore_signal(sem, inc=1, device_id=dev, device_id_type=MESH)
+
+        tell((self.z, self.xn, self.c))
+        tell((self.z, self.yn, self.c))
+        tell((self.z, self.b, 1 - self.c))
+        for d in range(1, self.lines):
+            self.each(d, lambda zz, way: tell((zz, self.b, self.c)))
+        pl.semaphore_wait(sem, self.lines + 2)
+
+
+def send(src, dst, ssem, rsem, dev):
+    return pltpu.make_async_remote_copy(
+        src_ref=src, dst_ref=dst, send_sem=ssem, recv_sem=rsem, device_id=dev, device_id_type=MESH
+    )
+
+
+def gather_sems(mode, lines):
+    n = 1 if mode == "plane" else lines
+    return [DMA, DMA((2, n)), DMA((n,)), DMA((n, 8)), DMA((n, 8))]
+
+
+def gather(spot, mode, x_ref, out_ref, sems):
+    own_sem, zs, zr, ps, pr = sems
+    z, b, c, xn, yn, dg, lines = spot.z, spot.b, spot.c, spot.xn, spot.yn, spot.dg, spot.lines
+    here = (z, b, c)
+    rows = out_ref.shape[-2]
+    lo, hi = pl.ds(0, rows // 2), pl.ds(rows // 2, rows // 2)
+    flat = mode == "plane"
+    planar = mode != "line"
+    steps = 1 if flat else lines
+
+    def blk(zz, bb, cc=c):
+        if flat:
+            return out_ref.at[bb, cc]
+        return out_ref.at[zz, bb, cc] if planar else out_ref.at[zz]
+
+    mine = 0 if flat else z
+
+    def each(d, fn):
+        if flat:
+            fn(0, 0)
+        else:
+            spot.each(d, fn)
+
+    def own():
+        return x_ref.at[z] if mode == "swap" else x_ref
+
+    def source(zz, d):
+        return own() if d == 0 else blk(zz, b)
+
+    def hop(zz, way, d):
+        return send(source(zz, d), blk(zz, b), zs.at[way, zz], zr.at[zz], (z + 1 - 2 * way, b, c))
+
+    def plane_copies(zz, d):
+        s = source(zz, d)
+        return [
+            send(s, blk(zz, b), ps.at[zz, 0], pr.at[zz, 0], (z, xn, c)),
+            send(s, blk(zz, b), ps.at[zz, 1], pr.at[zz, 1], (z, yn, c)),
+            send(s, blk(zz, b), ps.at[zz, 4], pr.at[zz, 4], (z, b, 1 - c)),
+        ]
+
+    def cross(zz, k):
+        if k == 0:
+            piece = blk(zz, yn).at[lo]
+            return send(piece, piece, ps.at[zz, 2], pr.at[zz, 2], (z, xn, c))
+        piece = blk(zz, xn).at[hi]
+        return send(piece, piece, ps.at[zz, 3], pr.at[zz, 3], (z, yn, c))
+
+    def share(zz, k):
+        bb = (b, xn, yn, dg)[k]
+        piece = blk(zz, bb)
+        return send(piece, piece, ps.at[zz, 4 + k], pr.at[zz, 4 + k], (z, b, 1 - c))
+
+    def received(piece, sem):
+        send(piece, piece, own_sem, sem, here).wait_recv()
+
+    def start():
+        pltpu.make_async_copy(own(), blk(mine, b), own_sem).start()
+        if mode in ("all", "line"):
+
+            @pl.when(z < lines - 1)
+            def _():
+                hop(z, 0, 0).start()
+
+            @pl.when(z > 0)
+            def _():
+                hop(z, 1, 0).start()
+
+        if mode == "swap":
+            for d in range(lines - 1, 0, -1):
+                spot.each(
+                    d,
+                    lambda zz, way: send(
+                        x_ref.at[zz], blk(z, b), zs.at[0, zz], zr.at[z], (zz, b, c)
+                    ).start(),
+                )
+        if planar:
+            for copy in plane_copies(mine, 0):
+                copy.start()
+
+    def line_arrive(zz, way):
+        received(blk(zz, b), zr.at[zz])
+        if mode in ("all", "line"):
+            if way > 0:
+
+                @pl.when(z < lines - 1)
+                def _():
+                    hop(zz, 0, 1).start()
+            else:
+
+                @pl.when(z > 0)
+                def _():
+                    hop(zz, 1, 1).start()
+
+        if planar:
+            for copy in plane_copies(zz, 1):
+                copy.start()
+
+    def plane_arrive(zz, way):
+        received(blk(zz, xn), pr.at[zz, 0])
+        cross(zz, 1).start()
+        received(blk(zz, yn), pr.at[zz, 1])
+        cross(zz, 0).start()
+        share(zz, 1).start()
+        share(zz, 2).start()
+
+    def cross_arrive(zz, way):
+        received(blk(zz, dg).at[lo], pr.at[zz, 2])
+        received(blk(zz, dg).at[hi], pr.at[zz, 3])
+        share(zz, 3).start()
+
+    def drain(zz, way):
+        if planar:
+            for k, bb in enumerate((b, xn, yn, dg)):
+                received(blk(zz, bb, 1 - c), pr.at[zz, 4 + k])
+                share(zz, k).wait_send()
+            for copy in plane_copies(zz, 1)[:2]:
+                copy.wait_send()
+            cross(zz, 0).wait_send()
+            cross(zz, 1).wait_send()
+        if mode in ("all", "line"):
+            if way >= 0:
+
+                @pl.when(z < lines - 1)
+                def _():
+                    hop(zz, 0, 1).wait_send()
+
+            if way <= 0:
+
+                @pl.when(z > 0)
+                def _():
+                    hop(zz, 1, 1).wait_send()
+
+        if mode == "swap" and way != 0:
+            send(x_ref.at[zz], blk(z, b), zs.at[0, zz], zr.at[z], (zz, b, c)).wait_send()
+
+    start()
+    yield
+    for s in range(1, steps + 2):
+        if s < steps:
+            each(s, line_arrive)
+        if planar and 0 <= s - 1 < steps:
+            each(s - 1, plane_arrive)
+        if planar and 0 <= s - 2 < steps:
+            each(s - 2, cross_arrive)
+        yield
+    for d in range(steps):
+        each(d, drain)
+    pltpu.make_async_copy(own(), blk(mine, b), own_sem).wait()
+    yield
+
+
+def reduce_scratch(mode, lines, rows, cols, dtype=BF16):
+    n = 1 if mode == "plane" else lines
+    out = []
+    if mode != "line":
+        out += [
+            pltpu.VMEM((n, 4, rows, cols), dtype),
+            pltpu.VMEM((n, 2, rows // 2, cols), dtype),
+            pltpu.VMEM((n, 2, rows, cols), dtype),
+            DMA((n, 8)),
+            DMA((n, 8)),
+        ]
+    if mode in ("all", "line"):
+        out += [pltpu.VMEM((2, lines, rows, cols), dtype)]
+    if mode != "plane":
+        out += [DMA((2, lines)), DMA((2, lines))]
+    if mode == "line":
+        out += [pltpu.VMEM((lines, rows, cols), dtype)]
+    return out
+
+
+def add_into(dst, *parts, chunk=16):
+    rows = dst.shape[0]
+
+    @pl.loop(0, rows // chunk)
+    def _(i):
+        at = pl.ds(pl.multiple_of(i * chunk, chunk), chunk)
+        total = parts[0][at].astype(F32)
+        for part in parts[1:]:
+            total = total + part[at].astype(F32)
+        dst[at] = total.astype(dst.dtype)
+
+
+def reduce(spot, mode, p_ref, out_ref, scratch):
+    z, b, c, xn, yn, dg, lines = spot.z, spot.b, spot.c, spot.xn, spot.yn, spot.dg, spot.lines
+    here = (z, b, c)
+    flat = mode == "plane"
+    planar = mode != "line"
+    steps = 1 if flat else lines
+    scratch = list(scratch)
+    if planar:
+        pair, crossed, met, ps, pr = scratch[:5]
+        scratch = scratch[5:]
+        rows = pair.shape[-2]
+        lo, hi = pl.ds(0, rows // 2), pl.ds(rows // 2, rows // 2)
+    if mode in ("all", "line"):
+        passed = scratch.pop(0)
+    if mode != "plane":
+        zs, zr = scratch[:2]
+        scratch = scratch[2:]
+    if mode == "line":
+        total_ref = scratch[0]
+
+    def total(zz):
+        return met.at[zz, 0] if planar else total_ref.at[zz]
+
+    def term(zz, bb, cc):
+        return p_ref.at[bb, cc] if flat else p_ref.at[zz, bb, cc]
+
+    def each(d, fn):
+        if flat:
+            fn(0, 0)
+        else:
+            spot.each(d, fn)
+
+    bbs = (dg, xn, yn, b)
+
+    def share(zz, k):
+        return send(
+            term(zz, bbs[k], 1 - c), pair.at[zz, k], ps.at[zz, k], pr.at[zz, k], (z, b, 1 - c)
+        )
+
+    def cross(zz, k):
+        piece = pair.at[zz, 0, (lo, hi)[k]]
+        dev = (z, (yn, xn)[k], c)
+        return send(piece, crossed.at[zz, k], ps.at[zz, 4 + k], pr.at[zz, 4 + k], dev)
+
+    def meet(zz, k):
+        dev = (z, (xn, yn)[k], c)
+        return send(pair.at[zz, 1 + k], met.at[zz, k], ps.at[zz, 6 + k], pr.at[zz, 6 + k], dev)
+
+    def hop(zz, way):
+        return send(
+            total(zz),
+            passed.at[way, zz],
+            zs.at[way, zz],
+            zr.at[way, zz],
+            (z + 1 - 2 * way, b, c),
+        )
+
+    def received(piece, sem):
+        send(piece, piece, ps.at[0, 0] if planar else zs.at[0, 0], sem, here).wait_recv()
+
+    def start(zz, way):
+        for k in range(4):
+            share(zz, k).start()
+
+    def first(zz, way):
+        for k in range(3):
+            received(pair.at[zz, k], pr.at[zz, k])
+            add_into(pair.at[zz, k], pair.at[zz, k], term(zz, bbs[k], c))
+            if k == 0:
+                cross(zz, 0).start()
+                cross(zz, 1).start()
+
+    def second(zz, way):
+        received(crossed.at[zz, 0], pr.at[zz, 4])
+        add_into(pair.at[zz, 1, lo], pair.at[zz, 1, lo], crossed.at[zz, 0])
+        meet(zz, 0).start()
+        received(crossed.at[zz, 1], pr.at[zz, 5])
+        add_into(pair.at[zz, 2, hi], pair.at[zz, 2, hi], crossed.at[zz, 1])
+        meet(zz, 1).start()
+
+    def third(zz, way):
+        received(pair.at[zz, 3], pr.at[zz, 3])
+        received(met.at[zz, 0], pr.at[zz, 6])
+        received(met.at[zz, 1], pr.at[zz, 7])
+        dst = out_ref if flat else total(zz)
+        add_into(dst, met.at[zz, 0], met.at[zz, 1], pair.at[zz, 3], term(zz, b, c))
+        if mode == "swap" and way != 0:
+            send(total(zz), out_ref.at[z], zs.at[0, zz], zr.at[0, z], (zz, b, c)).start()
+
+    def line(zz, way):
+        if way == 0:
+            base = total(zz) if planar else p_ref.at[zz]
+            both = (passed.at[0, zz], passed.at[1, zz])
+
+            @pl.when(z > 0)
+            def _():
+                received(passed.at[0, zz], zr.at[0, zz])
+
+            @pl.when(z < lines - 1)
+            def _():
+                received(passed.at[1, zz], zr.at[1, zz])
+
+            @pl.when(z == 0)
+            def _():
+                add_into(out_ref, base, both[1])
+
+            @pl.when(z == lines - 1)
+            def _():
+                add_into(out_ref, base, both[0])
+
+            @pl.when((z > 0) & (z < lines - 1))
+            def _():
+                add_into(out_ref, base, both[0], both[1])
+
+            return
+        down = 1 if way > 0 else 0
+        first_one = (z == lines - 1) if down else (z == 0)
+        base = total(zz) if planar else p_ref.at[zz]
+
+        @pl.when(jnp.logical_not(first_one))
+        def _():
+            received(passed.at[down, zz], zr.at[down, zz])
+            add_into(total(zz), base, passed.at[down, zz])
+            hop(zz, down).start()
+
+        @pl.when(first_one)
+        def _():
+            if planar:
+                hop(zz, down).start()
+            else:
+                send(
+                    p_ref.at[zz],
+                    passed.at[down, zz],
+                    zs.at[down, zz],
+                    zr.at[down, zz],
+                    (z + 1 - 2 * down, b, c),
+                ).start()
+
+    order = list(range(steps - 1, -1, -1))
+    if planar:
+        for d in order:
+            each(d, start)
+    lag = (1, 2, 3, 4) if planar else (9, 9, 9, 1)
+    yield
+    for s in range(1, steps + 4):
+        for fn, behind in zip((first, second, third, line), lag):
+            i = s - behind
+            if not 0 <= i < steps or behind > 8:
+                continue
+            if fn is line and mode not in ("all", "line"):
+                continue
+            each(order[i], fn)
+        yield
+
+    def drain(zz, way):
+        if planar:
+            for k in range(4):
+                share(zz, k).wait_send()
+            for k in range(2):
+                cross(zz, k).wait_send()
+                meet(zz, k).wait_send()
+        if mode in ("all", "line") and way != 0:
+            hop(zz, 1 if way > 0 else 0).wait_send()
+        if mode == "swap" and way != 0:
+            send(total(zz), out_ref.at[z], zs.at[0, zz], zr.at[0, z], (zz, b, c)).wait_send()
+            received(out_ref.at[zz], zr.at[0, zz])
+
+    for d in range(steps):
+        each(d, drain)
+    if mode == "swap":
+        add_into(out_ref.at[z], total(z))
+    yield
+
+
+def run_steps(makers):
+    live = list(makers)
+    while live:
+        for g in list(live):
+            try:
+                next(g)
+            except StopIteration:
+                live.remove(g)
+
+def exchange(name, cid, jobs):
+    lines = lax.axis_size("line")
+    cells = lax.axis_size("plane") * lax.axis_size("core")
+    if cells != 8 or lines != 4:
+        return [exchange_by_xla(kind, mode, x, lines, cells) for kind, mode, x in jobs]
+    in_specs, out_shapes, out_specs, scratch, counts = [], [], [], [], []
+    for kind, mode, x in jobs:
+        rows, cols = x.shape[-2:]
+        space = pltpu.VMEM if kind == "reduce" else pl.ANY
+        in_specs.append(pl.BlockSpec(memory_space=space))
+        if kind == "gather":
+            lead = {"line": (lines,), "plane": (4, 2)}.get(mode, (lines, 4, 2))
+            out_shapes.append(jax.ShapeDtypeStruct((*lead, rows, cols), x.dtype))
+            own = gather_sems(mode, lines)
+        else:
+            if mode == "swap":
+                out_shapes.append(jax.ShapeDtypeStruct((lines, rows, cols), x.dtype))
+            else:
+                out_shapes.append(jax.ShapeDtypeStruct((rows, cols), F32))
+            own = reduce_scratch(mode, lines, rows, cols, x.dtype)
+        out_specs.append(pl.BlockSpec(memory_space=space))
+        scratch += own
+        counts.append(len(own))
+    n = len(jobs)
+
+    def body(*refs):
+        spot = Spot(lines)
+        spot.greet()
+        at = 2 * n
+        makers = []
+        for i, (kind, mode, _) in enumerate(jobs):
+            mine = refs[at : at + counts[i]]
+            at += counts[i]
+            fn = gather if kind == "gather" else reduce
+            makers.append(fn(spot, mode, refs[i], refs[n + i], mine))
+        run_steps(makers)
+
+    return pl.pallas_call(
+        body,
+        out_shape=tuple(out_shapes),
+        in_specs=in_specs,
+        out_specs=tuple(out_specs),
+        scratch_shapes=scratch,
+        compiler_params=pltpu.CompilerParams(
+            collective_id=cid, has_side_effects=True, vmem_limit_bytes=60 << 20
+        ),
+        name=name,
+    )(*[x for _, _, x in jobs])
+
+
+def exchange_by_xla(kind, mode, x, lines, cells):
+    rows, cols = x.shape[-2:]
+    if kind == "gather":
+        if mode == "swap":
+            x = lax.all_to_all(x, LINE, split_axis=0, concat_axis=0, tiled=True)
+            return lax.all_gather(x, PLANE, axis=1)
+        return lax.all_gather(x, {"line": LINE, "plane": PLANE, "all": ALL}[mode])
+    if mode == "swap":
+        x = x.reshape(lines, cells, rows, cols).transpose(1, 0, 2, 3)
+        x = lax.psum_scatter(x, PLANE, scatter_dimension=0, tiled=True)
+        x = x.reshape(lines, rows, cols)
+        return lax.all_to_all(x, LINE, split_axis=0, concat_axis=0, tiled=True)
+    x = x.reshape(-1, cols)
+    axes = {"line": LINE, "plane": PLANE, "all": ALL}[mode]
+    return lax.psum_scatter(x, axes, scatter_dimension=0, tiled=True).astype(F32)
+
+
+def padded(flat, unit):
+    size = -(-flat.shape[0] // unit) * unit
+    return jnp.pad(flat, (0, size - flat.shape[0])).reshape(-1, 128)
 
 
 def on_device(
@@ -136,22 +626,37 @@
         axis=2,
     ).transpose(1, 0, 2)
     width = packed.shape[2]
-    packed = lax.all_to_all(packed, LINE, split_axis=0, concat_axis=0, tiled=True)
-    packed = lax.all_gather(packed, PLANE, axis=1, tiled=False)
-    weight_qkv = packed.reshape(lines * cells * own_rows, width)
-    weight_o = lax.all_gather(output_weight, PLANE, axis=0, tiled=True)
-    gains = lax.all_gather(norm_gains, ALL, axis=0, tiled=True).astype(F32)
-    router = lax.all_gather(router_weight, ALL, axis=0, tiled=True)
+    floats = padded(jnp.concatenate([router_weight.reshape(-1), norm_gains]), 32 * 128)
+    whole_numbers = padded(jnp.concatenate([routes.reshape(-1), lengths.reshape(-1)]), 16 * 128)
+    floats_all, numbers_all, weight_qkv, line_tokens, weight_o = exchange(
+        "gather_inputs",
+        0,
+        [
+            ("gather", "all", floats),
+            ("gather", "all", whole_numbers),
+            ("gather", "swap", packed),
+            ("gather", "line", tokens),
+            ("gather", "plane", output_weight),
+        ],
+    )
+    weight_qkv = weight_qkv.reshape(lines * cells * own_rows, width)
+    weight_o = weight_o.reshape(cells * output_weight.shape[0], D)
+    floats_all = floats_all.reshape(experts, -1)
+    router_size = own_rows * experts
+    router = floats_all[:, :router_size].reshape(D, experts)
+    gains = floats_all[:, router_size : router_size + norm_gains.shape[0]].reshape(-1).astype(F32)
+    numbers_all = numbers_all.reshape(experts, -1)
+    routes_all = numbers_all[:, : rows * TOP].reshape(experts * rows, TOP)
+    lengths_all = numbers_all[:, rows * TOP : rows * TOP + lengths.shape[1]]
+    line_lengths = lax.dynamic_slice_in_dim(
+        lengths_all.reshape(lines, cells, -1), me % cells, 1, axis=1
+    )[:, 0]
     gain_attn = gains[:D]
     gain_ffn = gains[D : 2 * D]
     gain_query = gains[2 * D : 2 * D + HEAD_DIM]
     gain_key = gains[2 * D + HEAD_DIM :]
 
-    routes_all = lax.all_gather(routes, ALL, axis=0, tiled=True)
-
-    line_tokens = lax.all_gather(tokens, LINE, axis=0, tiled=True)
-    line_lengths = lax.all_gather(lengths, LINE, axis=0, tiled=True)
-    inputs = line_tokens.astype(F32)
+    inputs = line_tokens.reshape(lines * rows, D).astype(F32)
     attn_scale = rms_scale(inputs)
     attn_normed = inputs * attn_scale
     hidden_one = (attn_normed * gain_attn).astype(BF16)
@@ -174,14 +679,16 @@
     )
     mixed_heads, log_total = attend(query_rot, key_rot, value_proj, allowed, score_scale)
     mixed_low = mixed_heads.reshape(lines * rows, Q_COLS).astype(BF16)
-    projected = lax.psum_scatter(dot(mixed_low, weight_o), LINE, scatter_dimension=0, tiled=True)
+    projected = dot(mixed_low, weight_o).astype(BF16).reshape(lines, rows, D)
+    (projected,) = exchange("sum_residual", 1, [("reduce", "line", projected)])
     own_inputs = tokens.astype(F32)
     residual = own_inputs + projected
     ffn_scale = rms_scale(residual)
     ffn_normed = residual * ffn_scale
     hidden_two = (ffn_normed * gain_ffn).astype(BF16)
 
-    hidden_all = lax.all_gather(hidden_two, ALL, axis=0, tiled=True)
+    (hidden_all,) = exchange("gather_hidden", 2, [("gather", "all", hidden_two)])
+    hidden_all = hidden_all.reshape(experts * rows, D)
     logits = dot(hidden_all, router)
     expert_ids = jnp.arange(experts, dtype=jnp.int32)
     picked = jnp.any(routes_all[:, :, None] == expert_ids, axis=1)
@@ -243,8 +750,16 @@
     expert_out = dot(expert_hidden, down_weight[0]).astype(BF16).astype(F32)
     grad_weight_slot = jnp.sum(grad_rows_out * expert_out, axis=1).reshape(experts, capacity)
     grad_weight_mine = jnp.sum(jnp.where(select, grad_weight_slot[:, :, None], 0.0), axis=1)
-    grad_weight = lax.all_gather(grad_weight_mine.reshape(-1), ALL, axis=0, tiled=False).T
-    grad_rows_sum = lax.psum_scatter(place(grad_rows_in), ALL, scatter_dimension=0, tiled=True)
+    placed = place(grad_rows_in).reshape(lines, -1, 2, rows, D)
+    grad_weight, grad_rows_sum = exchange(
+        "sum_rows",
+        3,
+        [
+            ("gather", "all", grad_weight_mine.reshape(experts, rows)),
+            ("reduce", "all", placed),
+        ],
+    )
+    grad_weight = grad_weight.reshape(experts, experts * rows).T
     if large:
         expert_out, grad_rows_sum = lax.optimization_barrier((expert_out, grad_rows_sum))
     out_sum = lax.psum_scatter(
@@ -266,9 +781,11 @@
     grad_hidden_two = dot(own_grad_logits, router.T) + grad_rows_sum.astype(F32)
     grad_gain_ffn = jnp.sum(grad_hidden_two * ffn_normed, axis=0)
     grad_residual = grad_out + norm_back(grad_hidden_two * gain_ffn, ffn_normed, ffn_scale)
-    grad_attn = lax.all_gather(grad_residual.astype(BF16), LINE, axis=0, tiled=True)
+    (grad_attn,) = exchange(
+        "gather_grad", 4, [("gather", "line", grad_residual.astype(BF16))]
+    )
+    grad_attn = grad_attn.reshape(lines * rows, D)
     output_part = dot(mixed_low.T, grad_attn).astype(BF16)
-    output_grad = lax.psum_scatter(output_part, PLANE, scatter_dimension=0, tiled=True)
     grad_mixed = dot(grad_attn, weight_o.T).astype(BF16).reshape(lines, rows, GROUPS, HEAD_DIM)
     grad_query_rot, grad_key_rot, grad_value_rot = attend_back(
         query_rot, key_rot, value_proj, allowed, score_scale, log_total, grad_mixed
@@ -290,31 +807,38 @@
         ],
         axis=1,
     )
-    grad_hidden_one = lax.psum_scatter(
-        dot(grad_proj, weight_qkv.T), LINE, scatter_dimension=0, tiled=True
+    hidden_one_part = dot(grad_proj, weight_qkv.T)
+    grad_gain_attn = jnp.sum(hidden_one_part * attn_normed, axis=0)
+    qkv_part = dot(hidden_one.T, grad_proj).astype(BF16)
+    gains_local = jnp.concatenate([grad_gain_attn, grad_gain_ffn, grad_gain_query, grad_gain_key])
+    gains_all, grad_hidden_one, qkv_part, output_grad = exchange(
+        "sum_gradients",
+        5,
+        [
+            ("gather", "all", padded(gains_local, 16 * 128)),
+            ("reduce", "line", hidden_one_part.astype(BF16).reshape(lines, rows, D)),
+            ("reduce", "swap", qkv_part.reshape(lines, -1, 2, own_rows, width)),
+            ("reduce", "plane", output_part.reshape(-1, 2, output_weight.shape[0], D)),
+        ],
     )
     own_scale = rms_scale(own_inputs)
     own_normed = own_inputs * own_scale
-    grad_gain_attn = jnp.sum(grad_hidden_one * own_normed, axis=0)
     input_grad = grad_residual + norm_back(grad_hidden_one * gain_attn, own_normed, own_scale)
-    qkv_part = dot(hidden_one.T, grad_proj).astype(BF16).reshape(lines, cells, own_rows, width)
-    qkv_part = qkv_part.transpose(1, 0, 2, 3).reshape(cells * lines * own_rows, width)
-    qkv_part = lax.psum_scatter(qkv_part, PLANE, scatter_dimension=0, tiled=True)
-    qkv_part = qkv_part.reshape(lines, own_rows, width)
-    qkv_part = lax.all_to_all(qkv_part, LINE, split_axis=0, concat_axis=0, tiled=True)
     qkv_part = qkv_part.transpose(1, 0, 2).astype(F32)
     query_grad = qkv_part[:, :, :Q_COLS].reshape(own_rows, lines * Q_COLS)
     key_grad = qkv_part[:, :, Q_COLS : Q_COLS + HEAD_DIM].reshape(own_rows, lines * HEAD_DIM)
     value_grad = qkv_part[:, :, Q_COLS + HEAD_DIM :].reshape(own_rows, lines * HEAD_DIM)
-    gains_local = jnp.concatenate([grad_gain_attn, grad_gain_ffn, grad_gain_query, grad_gain_key])
-    gains_grad = lax.psum_scatter(gains_local, ALL, scatter_dimension=0, tiled=True)
+    share = norm_gains.shape[0]
+    gains_all = gains_all.reshape(experts, -1)
+    gains_all = lax.dynamic_slice_in_dim(gains_all, me * share, share, axis=1)
+    gains_grad = jnp.sum(gains_all, axis=0)
     return (
         block_out,
         input_grad,
         query_grad,
         key_grad,
         value_grad,
-        output_grad.astype(F32),
+        output_grad,
         router_grad,
         gains_grad,
         grad_gate[None],

time: 1230 us -> 812 us (0.66)
  waiting for transfers between devices: 666 us -> 0.7 us
  Pallas kernels: 0 us -> 519 us
  blocking collectives: 260 us -> 0 us
  matrix products: 177 us -> 159 us
    pallas_call x0 -> x6, Pallas kernels: none -> 519 us  [exchange(): pl.pallas_call(body, out_shape=tuple(out_shapes), in_specs=in_specs, out_...]
    reduce_scatter x5 -> x0, waiting for transfers between devices: 352 us -> none  [the longest x1 178 us: on_device(): lax.psum_scatter(place(grad_rows_in), ALL, scatter_dimension=0, tiled=True)]
    all_gather x5 -> x0, waiting for transfers between devices: 171 us -> none  [the longest x1 104 us: on_device(): hidden_all = lax.all_gather(hidden_two, ALL, axis=0, tiled=True)]
    reduce_scatter x1, waiting for transfers between devices: 140 us -> 0.01 us  [on_device(): lax.psum_scatter(place((slot_weight * expert_out).astype(BF16)), ALL, sca...]
    all_gather x4 -> x0, blocking collectives: 134 us -> none  [the longest x1 44 us: on_device(): routes_all = lax.all_gather(routes, ALL, axis=0, tiled=True)]
    unnamed x2 -> x0, blocking collectives: 85.1 us -> none
    all_to_all x1 -> x0, blocking collectives: 40.4 us -> none  [on_device(): lax.all_to_all(packed, LINE, split_axis=0, concat_axis=0, tiled=True)]
  transfers between devices with their start and end apart: 13 -> 2, of which waited for: 10 -> 0; matrix products, arithmetic and copies ran while one was open for 12% -> 26% of each run, Pallas kernels for 0% -> 65%
where the time goes in v2:
time: 812 us; the launch traced here: 801 us
  Pallas kernels  519 us (64%)
  matrix products  159 us (20%)
  other arithmetic  66.8 us (8%)
  local copies, waits for them, and re-layouts  40.1 us (5%)
  between operations  15.6 us (2%)
    pallas_call x6, Pallas kernels, exchange(): pl.pallas_call(body, out_shape=tuple(out_shapes), in_specs=in_specs, out_...  519 us
    dot_general x18, matrix products, dot(): return jnp.dot(left, right, preferred_element_type=F32)  113 us
    dot_general x2, matrix products, place(): jnp.einsum('sjt,sjd->std', select_low, values.reshape(experts, capacity,...  26.2 us
    convert_element_type x2, other arithmetic, on_device(): grad_slots = (slot_weight * grad_rows_out).astype(BF16)  21.8 us
    unnamed x200, local copies, waits for them, and re-layouts  18.2 us
  transfers between devices with their start and end apart: 2, of which 0 were waited for; matrix products, arithmetic and copies ran while one was open for 26% of the time, Pallas kernels for 65%

profile of v2, /device:TPU:0, one launch (start us, length us, event | category | flops | bytes accessed | tf_op | source)
XLA Modules:
  0.0 801.4 jit_solution(6859278802002755233)
XLA Ops:
  15.3 116.4 %gather_inputs.1 = (bf16[4,4,2,32,128]{4,3,2,1,0:T(8,128)(2,1)}, s32[4,4,2,16,128]{4,3,2,1,0:T(8,128)}, bf16[4,4,2,64,1280]{4,3,2,1,0:T(8,128)(2,1)}, bf16[4,128...) custom-call(bf16[32,128]{1,0:T(8,128)(2,1)} %fusion.86.refs_0_, s32[16,128]{1,0:T(8,128)} %pad_bitcast_fusion.refs_1_, ...), custom_call_target="tpu_custom_call" | custom-call | tf_op jit(solution)/shard_map/gather_inputs/pallas_call | solution.py:557
  136.4 5.4 fusion.105
  162.1 6.2 convolution_convert_fusion.6
  168.2 44.1 %sum_residual.1 = f32[128,2048]{1,0:T(8,128)} custom-call(bf16[4,128,2048]{2,1,0:T(8,128)(2,1)} %bitcast.316), custom_call_target="tpu_custom_call" | custom-call | tf_op jit(solution)/shard_map/sum_residual/pallas_call | solution.py:557
  224.7 73.3 %gather_hidden.1 = bf16[4,4,2,128,2048]{4,3,2,1,0:T(8,128)(2,1)} custom-call(bf16[128,2048]{1,0:T(8,128)(2,1)} %multiply_convert_fusion.6.refs_0_), custom_call_target="tpu_custom_call" | custom-call | tf_op jit(solution)/shard_map/gather_hidden/pallas_call | solution.py:557
  299.9 11.7 %fusion.104 = (f32[4096]{0:T(1024)S(1)}, f32[4096,32]{0,1:T(8,128)}) fusion(pred[4096,32]{0,1:T(8,128)(4,1)S(1)} %fusion.4, bf16[4096,2048]{1,0:T(8,128)(2,1)} %bitcast.280, bf16[2048,32]{1,0:T(8,128)(2,1)} %reshape.364), kind=kOutput, calls=%fused_computation.225 | convolution fusion | flops 537128960 | bytes 17580032 | tf_op jit(solution)/shard_map/dot_general | solution.py:31
  314.0 8.2 %convolution_convert_fusion.4 = bf16[32,48,2048]{2,1,0:T(8,128)(2,1)S(1)} fusion(bf16[32,128,2048]{2,1,0:T(8,128)(2,1)} %bitcast.281, s32[32,128]{1,0:T(8,128)S(1)} %broadcast_add_fusion, pred[32,128]{1,0:T(8,128)(4,1)S(1)} %bitcast.332), kind=kOutput, calls=%fused_computation.17 | convolution fusion | flops 808845312 | bytes 23089152 | tf_op jit(solution)/shard_map/sjt,std->sjd/dot_general | solution.py:709
  322.3 5.5 fusion.13
  329.9 7.4 multiply_convert_fusion.3
  337.3 7.2 fusion.49
  344.5 7.2 fusion.1
  352.8 13.4 %fusion.2 = (bf16[1536,2048]{1,0:T(8,128)(2,1)}, bf16[1536,2048]{1,0:T(8,128)(2,1)}) fusion(f32[32,48,2048]{2,1,0:T(8,128)} %copy-done.2, f32[1536]{0:T(1024)S(1)} %mul.475, bf16[1536,2048]{1,0:T(8,128)(2,1)} %get-tuple-element.87), kind=kLoop, calls=%fused_computation.7 | loop fusion | flops 15728640 | bytes 31463424 | tf_op jit(solution)/shard_map/convert_element_type | solution.py:736
  366.2 13.1 %convolution_convert_fusion.1 = bf16[32,128,2048]{2,1,0:T(8,128)(2,1)} fusion(bf16[32,48,2048]{2,1,0:T(8,128)(2,1)} %bitcast.289, s32[32,128]{1,0:T(8,128)S(1)} %broadcast_add_fusion, pred[32,128]{1,0:T(8,128)(4,1)S(1)} %bitcast.335), kind=kOutput, calls=%fused_computation.3 | convolution fusion | flops 814088192 | bytes 23089152 | tf_op jit(solution)/shard_map/sjt,sjd->std/dot_general | solution.py:718
  382.6 8.4 %multiply_convert_fusion = bf16[32,48,2048]{2,1,0:T(8,128)(2,1)} fusion(f32[32,48,2048]{2,1,0:T(8,128)} %copy-done.2, f32[32,48]{1,0:T(8,128)S(1)} %get-tuple-element.38), kind=kLoop, calls=%fused_computation.9 | loop fusion | flops 6291456 | bytes 18880512 | tf_op jit(solution)/shard_map/convert_element_type | solution.py:736
  391.0 11.6 %multiply_convert_fusion.1 = (bf16[1536,768]{1,0:T(8,128)(2,1)S(1)}, bf16[1536,768]{1,0:T(8,128)(2,1)S(1)}) fusion(f32[1536,768]{1,0:T(8,128)} %copy-done.87, f32[1536,768]{1,0:T(8,128)} %get-tuple-element.85, bf16[1536,2048]{1,0:T(8,128)(2,1)} %bitcast.303, bf16[1,768,2048]{2,1,0:T(8,128)(2,1)S(1)} %copy-done), kind=kOutput, calls=%fused_computation.12 | convolution fusion | flops 4847173632 | bytes 23592960 | tf_op jit(solution)/shard_map/dot_general | solution.py:31
  407.8 7.5 add_convert_fusion
  415.3 13.2 %convolution_convert_fusion = bf16[32,128,2048]{2,1,0:T(8,128)(2,1)} fusion(bf16[32,48,2048]{2,1,0:T(8,128)(2,1)} %bitcast.304, s32[32,128]{1,0:T(8,128)S(1)} %broadcast_add_fusion, pred[32,128]{1,0:T(8,128)(4,1)S(1)} %bitcast.336), kind=kOutput, calls=%fused_computation.2 | convolution fusion | flops 814088192 | bytes 23089152 | tf_op jit(solution)/shard_map/sjt,sjd->std/dot_general | solution.py:718
  428.5 175.2 %sum_rows.1 = (f32[4,4,2,32,128]{4,3,2,1,0:T(8,128)}, f32[128,2048]{1,0:T(8,128)}) custom-call(f32[32,128]{1,0:T(8,128)} %get-tuple-element.37.refs_0_, bf16[4,4,2,128,2048]{4,3,2,1,0:T(8,128)(2,1)} %bitcast.284), custom_call_target="tpu_custom_call" | custom-call | tf_op jit(solution)/shard_map/sum_rows/pallas_call | solution.py:557
  608.6 46.1 %gather_grad.1 = bf16[4,128,2048]{2,1,0:T(8,128)(2,1)} custom-call(bf16[128,2048]{1,0:T(8,128)(2,1)} %fusion.99.refs_0_), custom_call_target="tpu_custom_call" | custom-call | tf_op jit(solution)/shard_map/gather_grad/pallas_call | solution.py:557
  680.0 6.8 fusion.100
  696.7 63.9 %sum_gradients.1 = (f32[4,4,2,48,128]{4,3,2,1,0:T(8,128)}, f32[128,2048]{1,0:T(8,128)}, bf16[4,64,1280]{2,1,0:T(8,128)(2,1)}, f32[128,2048]{1,0:T(8,128)}) custom-call(f32[48,128]{1,0:T(8,128)} %fusion.82.refs_0_, bf16[4,128,2048]{2,1,0:T(8,128)(2,1)} %bitcast.311, bf16[4,4,2,64,1280]{4,3,2,1,0:T(8,128)(2,1)} %bitcast.305, bf16[4,2,128,2048]{3,2,1,0:T(8,128)(2,1)} %bitcast.306), custom_call_target="tpu_custom_call" | custom-call | tf_op jit(solution)/shard_map/sum_gradients/pallas_call | solution.py:557
  768.2 7.0 convolution_bitcast_fusion.2
  775.2 7.0 convolution_bitcast_fusion.1
  782.3 7.0 convolution_bitcast_fusion
  (305 shorter events, 113.3 us)
Async XLA Ops:
  7.2 337.3 %copy-start = (bf16[1,768,2048]{2,1,0:T(8,128)(2,1)S(1)}, bf16[1,768,2048]{2,1,0:T(8,128)(2,1)}, u32[]{:S(2)}) copy-start(bf16[1,768,2048]{2,1,0:T(8,128)(2,1)} %param.25) | copy-start | bytes 9437188
  7.2 330.1 %all-gather.2.cloned.1.call-start = ((), (), s32[]{:S(2)}) async-start(), calls=%async_computation.2 | async-start | bytes 17301504 | tf_op jit(solution)/shard_map/all_gather | solution.py:734
  7.9 781.4 %reduce-scatter.2.cloned.1.call-start = ((), (), s32[]{:S(2)}) async-start(), calls=%async_computation.1 | async-start | bytes 17301504 | tf_op jit(solution)/shard_map/reduce_scatter | solution.py:765
  135.9 87.0 %copy-start.51 = (f32[2048]{0:T(1024)}, f32[2048]{0:T(1024)S(1)}, u32[]{:S(2)}) copy-start(f32[2048]{0:T(1024)S(1)} %get-tuple-element.65) | copy-start | bytes 24580
  168.2 44.1 %copy-start.41 = (s32[32,1024]{1,0:T(8,128)S(1)}, s32[32,1024]{1,0:T(8,128)}, u32[]{:S(2)}) copy-start(s32[32,1024]{1,0:T(8,128)} %slice.101) | copy-start | bytes 393220
  299.9 14.1 %copy-start.61 = (s32[32,128]{1,0:T(8,128)S(1)}, s32[32,128]{1,0:T(8,128)}, u32[]{:S(2)}) copy-start(s32[32,128]{1,0:T(8,128)} %reduce_window_sum.26) | copy-start | bytes 49156
  299.9 14.1 %copy-start.45 = (pred[4096]{0:T(1024)(128)(4,1)S(1)}, pred[4096]{0:T(1024)(128)(4,1)}, u32[]{:S(2)}) copy-start(pred[4096]{0:T(1024)(128)(4,1)} %copy-done.44) | copy-start | bytes 12292
  312.8 291.0 %copy-start.47 = (f32[4096]{0:T(1024)}, f32[4096]{0:T(1024)S(1)}, u32[]{:S(2)}) copy-start(f32[4096]{0:T(1024)S(1)} %fusion.72) | copy-start | bytes 49156
  314.0 8.3 %copy-start.79 = (bf16[1,2048,768]{2,1,0:T(8,128)(2,1)S(1)}, bf16[1,2048,768]{2,1,0:T(8,128)(2,1)}, u32[]{:S(2)}) copy-start(bf16[1,2048,768]{2,1,0:T(8,128)(2,1)} %param.23) | copy-start | bytes 9437188
  322.3 7.6 copy-start.81
  337.3 7.2 copy-start.83
  344.5 7.2 copy-start.2
  391.0 11.6 %copy-start.80 = (bf16[1,2048,768]{2,1,0:T(8,128)(2,1)S(1)}, bf16[1,2048,768]{2,1,0:T(8,128)(2,1)}, u32[]{:S(2)}) copy-start(bf16[1,2048,768]{2,1,0:T(8,128)(2,1)} %param.23) | copy-start | bytes 9437188
  428.5 175.3 %copy-start.11 = (f32[4096,32]{0,1:T(8,128)S(1)}, f32[4096,32]{0,1:T(8,128)}, u32[]{:S(2)}) copy-start(f32[4096,32]{0,1:T(8,128)} %get-tuple-element.89) | copy-start | bytes 1572868
  607.5 47.2 %copy-start.18 = (f32[128,2048]{1,0:T(8,128)}, f32[128,2048]{1,0:T(8,128)S(1)}, u32[]{:S(2)}) copy-start(f32[128,2048]{1,0:T(8,128)S(1)} %get-tuple-element.90) | copy-start | bytes 3145732
  680.0 7.4 copy-start.29
  680.0 7.4 copy-start.37
  760.6 7.5 slice-start
  768.2 7.1 copy-start.89
  768.2 14.1 %slice-start.2 = ((s8[6291456]{0:T(1024)(128)(4,1)}), s8[4194304]{0:T(1024)(128)(4,1)S(1)}, s32[]{:S(2)}) async-start(s8[6291456]{0:T(1024)(128)(4,1)} %bitcast.301), calls=%async_computation.5 | async-start | bytes 8388608
  775.2 7.1 slice-start.3
  775.2 7.1 copy-start.84
  782.3 7.0 copy-start.53
  782.3 7.0 copy-start.68
  (72 other events, 190.1 us)
Sparse Core Ops, SparseCore 0:
  10.9 139.0 all-gather.1
  379.4 259.4 reduce-scatter.1

commit v3 on v2

--- a/solution.py
+++ b/solution.py
@@ -1,3 +1,5 @@
+import functools
+
 import jax
 import jax.numpy as jnp
 from jax import lax
@@ -151,7 +153,7 @@
     return [DMA, DMA((2, n)), DMA((n,)), DMA((n, 8)), DMA((n, 8))]
 
 
-def gather(spot, mode, x_ref, out_ref, sems):
+def gather_parts(spot, x_ref, out_ref, sems, mode="all"):
     own_sem, zs, zr, ps, pr = sems
     z, b, c, xn, yn, dg, lines = spot.z, spot.b, spot.c, spot.xn, spot.yn, spot.dg, spot.lines
     here = (z, b, c)
@@ -263,8 +265,7 @@
 
     def drain(zz, way):
         if planar:
-            for k, bb in enumerate((b, xn, yn, dg)):
-                received(blk(zz, bb, 1 - c), pr.at[zz, 4 + k])
+            for k in range(4):
                 share(zz, k).wait_send()
             for copy in plane_copies(zz, 1)[:2]:
                 copy.wait_send()
@@ -286,19 +287,54 @@
         if mode == "swap" and way != 0:
             send(x_ref.at[zz], blk(z, b), zs.at[0, zz], zr.at[z], (zz, b, c)).wait_send()
 
-    start()
+    def shared(zz, k):
+        received(blk(zz, (b, xn, yn, dg)[k], 1 - c), pr.at[zz, 4 + k])
+
+    def end():
+        pltpu.make_async_copy(own(), blk(mine, b), own_sem).wait()
+
+    return {
+        "start": start,
+        "line": line_arrive,
+        "plane": plane_arrive,
+        "cross": cross_arrive,
+        "shared": shared,
+        "drain": drain,
+        "end": end,
+    }
+
+
+def gather(spot, mode, x_ref, out_ref, sems):
+    parts = gather_parts(spot, x_ref, out_ref, sems, mode)
+    flat = mode == "plane"
+    planar = mode != "line"
+    steps = 1 if flat else spot.lines
+
+    def each(d, fn):
+        if flat:
+            fn(0, 0)
+        else:
+            spot.each(d, fn)
+
+    def drain(zz, way):
+        if planar:
+            for k in range(4):
+                parts["shared"](zz, k)
+        parts["drain"](zz, way)
+
+    parts["start"]()
     yield
     for s in range(1, steps + 2):
         if s < steps:
-            each(s, line_arrive)
+            each(s, parts["line"])
         if planar and 0 <= s - 1 < steps:
-            each(s - 1, plane_arrive)
+            each(s - 1, parts["plane"])
         if planar and 0 <= s - 2 < steps:
-            each(s - 2, cross_arrive)
+            each(s - 2, parts["cross"])
         yield
     for d in range(steps):
         each(d, drain)
-    pltpu.make_async_copy(own(), blk(mine, b), own_sem).wait()
+    parts["end"]()
     yield
 
 
@@ -319,6 +355,8 @@
         out += [DMA((2, lines)), DMA((2, lines))]
     if mode == "line":
         out += [pltpu.VMEM((lines, rows, cols), dtype)]
+    if mode == "all":
+        out += [pltpu.VMEM((n, 4, rows, cols), dtype), DMA]
     return out
 
 
@@ -353,6 +391,8 @@
         scratch = scratch[2:]
     if mode == "line":
         total_ref = scratch[0]
+    if mode == "all":
+        kept, kept_sem = scratch
 
     def total(zz):
         return met.at[zz, 0] if planar else total_ref.at[zz]
@@ -365,6 +405,9 @@
             fn(0, 0)
         else:
             spot.each(d, fn)
+
+    def kept_term(zz, bb):
+        return kept.at[zz, bb] if mode == "all" else term(zz, bb, c)
 
     bbs = (dg, xn, yn, b)
 
@@ -401,7 +444,7 @@
     def first(zz, way):
         for k in range(3):
             received(pair.at[zz, k], pr.at[zz, k])
-            add_into(pair.at[zz, k], pair.at[zz, k], term(zz, bbs[k], c))
+            add_into(pair.at[zz, k], pair.at[zz, k], kept_term(zz, bbs[k]))
             if k == 0:
                 cross(zz, 0).start()
                 cross(zz, 1).start()
@@ -419,7 +462,7 @@
         received(met.at[zz, 0], pr.at[zz, 6])
         received(met.at[zz, 1], pr.at[zz, 7])
         dst = out_ref if flat else total(zz)
-        add_into(dst, met.at[zz, 0], met.at[zz, 1], pair.at[zz, 3], term(zz, b, c))
+        add_into(dst, met.at[zz, 0], met.at[zz, 1], pair.at[zz, 3], kept_term(zz, b))
         if mode == "swap" and way != 0:
             send(total(zz), out_ref.at[z], zs.at[0, zz], zr.at[0, z], (zz, b, c)).start()
 
@@ -476,6 +519,10 @@
     if planar:
         for d in order:
             each(d, start)
+    if mode == "all":
+        bring = pltpu.make_async_copy(p_ref.at[:, :, c], kept, kept_sem)
+        bring.start()
+        bring.wait()
     lag = (1, 2, 3, 4) if planar else (9, 9, 9, 1)
     yield
     for s in range(1, steps + 4):
@@ -526,7 +573,8 @@
     for kind, mode, x in jobs:
         rows, cols = x.shape[-2:]
         space = pltpu.VMEM if kind == "reduce" else pl.ANY
-        in_specs.append(pl.BlockSpec(memory_space=space))
+        far = kind == "gather" or mode == "all"
+        in_specs.append(pl.BlockSpec(memory_space=pl.ANY if far else pltpu.VMEM))
         if kind == "gather":
             lead = {"line": (lines,), "plane": (4, 2)}.get(mode, (lines, 4, 2))
             out_shapes.append(jax.ShapeDtypeStruct((*lead, rows, cols), x.dtype))
@@ -587,6 +635,401 @@
 def padded(flat, unit):
     size = -(-flat.shape[0] // unit) * unit
     return jnp.pad(flat, (0, size - flat.shape[0])).reshape(-1, 128)
+
+
+def pick_order(z, i):
+    far = z // 2
+    near = z * (1 - far) + (3 - z) * far
+    place = (near + i) % 2 if i < 2 else i
+    return place * (1 - far) + (3 - place) * far
+
+
+def dot_nt(left, right):
+    return lax.dot_general(left, right, (((1,), (1,)), ((), ())), preferred_element_type=F32)
+
+
+def experts_body(capacity, experts, *refs):
+    lines = 4
+    (h_ref, t_ref, sel_ref, spread_ref, named_ref, router_ref, gate_ref, up_ref, down_ref) = refs[:9]
+    (hall, tall, px, py, w_ref, dw_ref, x_out, dy_out, a_out, dg_out, du_out) = refs[9:20]
+    rest = list(refs[20:])
+    h_sems, t_sems = rest[:5], rest[5:10]
+    (wg, wu, wd, hb, tb, xs, zs, dys, acts, dgs, dus, rs, ys, stage, slot_w, acc) = rest[10:26]
+    (w_sem, l_sem, o_sem, p_sem) = rest[26:]
+    spot = Spot(lines)
+    z, b, c, xn, yn, dg_spot = spot.z, spot.b, spot.c, spot.xn, spot.yn, spot.dg
+    me = (z * 4 + b) * 2 + c
+    pair = 2 * capacity
+    spot.greet()
+    steps_h = gather_parts(spot, h_ref, hall, h_sems)
+    steps_t = gather_parts(spot, t_ref, tall, t_sems)
+    both = (steps_h, steps_t)
+    columns = (b, xn, yn, dg_spot)
+    loads = [
+        pltpu.make_async_copy(gate_ref, wg, w_sem.at[0]),
+        pltpu.make_async_copy(up_ref, wu, w_sem.at[1]),
+        pltpu.make_async_copy(down_ref, wd, w_sem.at[2]),
+    ]
+
+    def comm(name, d):
+        for s in both:
+            spot.each(d, s[name])
+
+    def load(i, k, n):
+        zz, bb = pick_order(z, i), columns[k]
+        return [
+            pltpu.make_async_copy(hall.at[zz, bb], hb.at[n % 2], l_sem.at[0, n % 2]),
+            pltpu.make_async_copy(tall.at[zz, bb], tb.at[n % 2], l_sem.at[1, n % 2]),
+        ]
+
+    def fetch(i, k, n):
+        zz = pick_order(z, i)
+        for s in both:
+            s["shared"](zz, k)
+        for copy in load(i, k, n):
+            copy.start()
+
+    def pick(i, k, n):
+        zz, bb = pick_order(z, i), columns[k]
+        at = pl.ds(pl.multiple_of(bb * pair, 16), pair)
+        which = zz * 4 + bb
+        for copy in load(i, k, n):
+            copy.wait()
+        rows = hb.shape[2]
+        width = hb.shape[3]
+        hidden = hb.at[n % 2]
+        token = tb.at[n % 2]
+        cols = pl.ds(pl.multiple_of(which * 2 * rows, 2 * rows), 2 * rows)
+        logits = dot_nt(router_ref[...], hidden[...].reshape(2 * rows, width))
+        named = named_ref[:, cols] > 0.5
+        masked = jnp.where(named, logits, masked_score)
+        top = jnp.max(masked, axis=0, keepdims=True)
+        exponent = jnp.where(named, jnp.exp(masked - top), 0.0)
+        weights = exponent / jnp.sum(exponent, axis=0, keepdims=True)
+        w_ref[:, cols] = weights
+        expert_row = lax.broadcasted_iota(jnp.int32, weights.shape, 0)
+        mine = jnp.sum(jnp.where(expert_row == me, weights, 0.0), axis=0, keepdims=True)
+        select = sel_ref[which]
+        per_slot = jnp.sum(select.astype(F32) * mine, axis=1, keepdims=True)
+        slot_w[i % 2, at, :] = jnp.broadcast_to(per_slot, (pair, 128))
+
+        @pl.loop(0, width // 512)
+        def _(j):
+            part = pl.ds(pl.multiple_of(j * 512, 512), 512)
+            h = hb[n % 2, :, :, part].reshape(2 * rows, 512)
+            t = tb[n % 2, :, :, part].reshape(2 * rows, 512)
+            xs[i % 2, at, part] = jnp.dot(select, h, preferred_element_type=F32).astype(BF16)
+            t = jnp.dot(select, t, preferred_element_type=F32)
+            zs[i % 2, at, part] = t.astype(BF16)
+            dys[i % 2, at, part] = (per_slot * t).astype(BF16)
+
+    def keep(i):
+        zz = pick_order(z, i)
+        q = i % 2
+        return [
+            pltpu.make_async_copy(xs.at[q], x_out.at[zz], o_sem.at[q, 0]),
+            pltpu.make_async_copy(dys.at[q], dy_out.at[zz], o_sem.at[q, 1]),
+            pltpu.make_async_copy(acts.at[q], a_out.at[zz], o_sem.at[q, 2]),
+            pltpu.make_async_copy(dgs.at[q], dg_out.at[zz], o_sem.at[q, 3]),
+            pltpu.make_async_copy(dus.at[q], du_out.at[zz], o_sem.at[q, 4]),
+        ]
+
+    def inner(i):
+        q = i % 2
+
+        @pl.loop(0, wg.shape[1] // 256)
+        def _(j):
+            part = pl.ds(pl.multiple_of(j * 256, 256), 256)
+            g = jnp.dot(xs[q], wg[:, part], preferred_element_type=F32)
+            u = jnp.dot(xs[q], wu[:, part], preferred_element_type=F32)
+            da = dot_nt(dys[q], wd[part, :])
+            sig = jax.nn.sigmoid(g)
+            silu = g * sig
+            acts[q, :, part] = (silu * u).astype(BF16)
+            dgs[q, :, part] = (da * u * sig * (1.0 + g * (1.0 - sig))).astype(BF16)
+            dus[q, :, part] = (da * silu).astype(BF16)
+
+        for copy in keep(i):
+            copy.start()
+
+    def outer(i):
+        q = i % 2
+        acc[...] = jnp.zeros_like(acc)
+
+        @pl.loop(0, wg.shape[0] // 256)
+        def _(j):
+            part = pl.ds(pl.multiple_of(j * 256, 256), 256)
+            r = dot_nt(dgs[q], wg[part, :]) + dot_nt(dus[q], wu[part, :])
+            rs[:, part] = r.astype(BF16)
+            y = jnp.dot(acts[q], wd[:, part], preferred_element_type=F32)
+            y = y.astype(BF16).astype(F32)
+            met = y * zs[q, :, part].astype(F32)
+            acc[...] += met[:, :128] + met[:, 128:]
+            ys[:, part] = (slot_w[q, :, 0:1] * y).astype(BF16)
+
+    def put(zz, bb, m):
+        return [
+            pltpu.make_async_copy(stage.at[m % 2, 0], px.at[zz, bb], p_sem.at[m % 2, 0]),
+            pltpu.make_async_copy(stage.at[m % 2, 1], py.at[zz, bb], p_sem.at[m % 2, 1]),
+        ]
+
+    def place(i, k, m):
+        zz, bb = pick_order(z, i), columns[k]
+        at = pl.ds(pl.multiple_of(bb * pair, 16), pair)
+        which = zz * 4 + bb
+        if m >= 2:
+            for copy in put(zz, bb, m):
+                copy.wait()
+        dw_slot = jnp.sum(acc[at, :], axis=1, keepdims=True)
+        dw_ref[pl.ds(which, 1), :] = jnp.sum(
+            sel_ref[which].astype(F32) * dw_slot, axis=0, keepdims=True
+        )
+        spread = spread_ref[which]
+        rows = stage.shape[3]
+
+        @pl.loop(0, rs.shape[1] // 512)
+        def _(j):
+            part = pl.ds(pl.multiple_of(j * 512, 512), 512)
+            for n, src in enumerate((rs, ys)):
+                full = jnp.dot(spread, src[at, part], preferred_element_type=F32)
+                stage[m % 2, n, :, :, part] = full.astype(BF16).reshape(2, rows, 512)
+
+        for copy in put(zz, bb, m):
+            copy.start()
+
+    for s in both:
+        s["start"]()
+    for copy in loads:
+        copy.start()
+    for s in both:
+        s["end"]()
+    fetch(0, 0, 0)
+    comm("line", 1)
+    comm("plane", 0)
+    fetch(0, 1, 1)
+    pick(0, 0, 0)
+    fetch(0, 2, 2)
+    pick(0, 1, 1)
+    comm("line", 2)
+    fetch(1, 0, 3)
+    pick(0, 2, 2)
+    comm("plane", 1)
+    comm("cross", 0)
+    fetch(0, 3, 4)
+    pick(1, 0, 3)
+    for copy in loads:
+        copy.wait()
+    fetch(1, 1, 5)
+    pick(0, 3, 4)
+    comm("line", 3)
+    inner(0)
+    comm("plane", 2)
+    fetch(1, 2, 6)
+    pick(1, 1, 5)
+    outer(0)
+    comm("cross", 1)
+    fetch(1, 3, 7)
+    pick(1, 2, 6)
+    place(0, 0, 0)
+    place(0, 1, 1)
+    comm("plane", 3)
+    place(0, 2, 2)
+    place(0, 3, 3)
+    pick(1, 3, 7)
+    inner(1)
+    for copy in keep(0):
+        copy.wait()
+    fetch(2, 0, 8)
+    comm("cross", 2)
+    fetch(2, 1, 9)
+    pick(2, 0, 8)
+    outer(1)
+    fetch(2, 2, 10)
+    pick(2, 1, 9)
+    for k in range(4):
+        place(1, k, 4 + k)
+    comm("cross", 3)
+    fetch(2, 3, 11)
+    pick(2, 2, 10)
+    fetch(3, 0, 12)
+    pick(2, 3, 11)
+    inner(2)
+    for copy in keep(1):
+        copy.wait()
+    fetch(3, 1, 13)
+    pick(3, 0, 12)
+    outer(2)
+    fetch(3, 2, 14)
+    pick(3, 1, 13)
+    for k in range(4):
+        place(2, k, 8 + k)
+    fetch(3, 3, 15)
+    pick(3, 2, 14)
+    pick(3, 3, 15)
+    inner(3)
+    outer(3)
+    for k in range(4):
+        place(3, k, 12 + k)
+    for m in (0, 1):
+        for copy in put(z, b, m):
+            copy.wait()
+    for i in (2, 3):
+        for copy in keep(i):
+            copy.wait()
+    for d in range(lines):
+        comm("drain", d)
+
+
+def experts_call(hidden_two, cotangent, routes_all, router, gate, up, down, capacity):
+    lines, experts = 4, 32
+    rows, width = hidden_two.shape
+    ff = gate.shape[1]
+    pair = 2 * capacity
+    group = 4 * pair
+    me = (lax.axis_index("line") * 4 + lax.axis_index("plane")) * 2 + lax.axis_index("core")
+    named = jnp.any(
+        routes_all.T[:, None, :] == jnp.arange(experts, dtype=jnp.int32)[None, :, None], axis=0
+    )
+    mine = jnp.any(routes_all == me, axis=1).reshape(experts, rows)
+    rank = jnp.cumsum(mine.astype(jnp.int32), axis=1) - 1
+    slot = rank + (jnp.arange(experts, dtype=jnp.int32) % 2 * capacity)[:, None]
+    slot = jnp.where(mine, slot, -1).reshape(experts // 2, 2 * rows)
+    places = jnp.arange(pair, dtype=jnp.int32)
+    select = (slot[:, None, :] == places[None, :, None]).astype(BF16)
+    spread = (slot[:, :, None] == places[None, None, :]).astype(BF16)
+    anywhere = pl.BlockSpec(memory_space=pl.ANY)
+    near = pl.BlockSpec(memory_space=pltpu.VMEM)
+    all_rows = jax.ShapeDtypeStruct((lines, 4, 2, rows, width), BF16)
+    wide = jax.ShapeDtypeStruct((lines, group, width), BF16)
+    thin = jax.ShapeDtypeStruct((lines, group, ff), BF16)
+    return pl.pallas_call(
+        functools.partial(experts_body, capacity, experts),
+        out_shape=(
+            all_rows,
+            all_rows,
+            all_rows,
+            all_rows,
+            jax.ShapeDtypeStruct((experts, experts * rows), F32),
+            jax.ShapeDtypeStruct((experts // 2, 2 * rows), F32),
+            wide,
+            wide,
+            thin,
+            thin,
+            thin,
+        ),
+        in_specs=[anywhere, anywhere, near, near, near, near, anywhere, anywhere, anywhere],
+        out_specs=(*[anywhere] * 4, near, near, *[anywhere] * 5),
+        scratch_shapes=[
+            *gather_sems("all", lines),
+            *gather_sems("all", lines),
+            pltpu.VMEM((width, ff), BF16),
+            pltpu.VMEM((width, ff), BF16),
+            pltpu.VMEM((ff, width), BF16),
+            pltpu.VMEM((2, 2, rows, width), BF16),
+            pltpu.VMEM((2, 2, rows, width), BF16),
+            pltpu.VMEM((2, group, width), BF16),
+            pltpu.VMEM((2, group, width), BF16),
+            pltpu.VMEM((2, group, width), BF16),
+            pltpu.VMEM((2, group, ff), BF16),
+            pltpu.VMEM((2, group, ff), BF16),
+            pltpu.VMEM((2, group, ff), BF16),
+            pltpu.VMEM((group, width), BF16),
+            pltpu.VMEM((group, width), BF16),
+            pltpu.VMEM((2, 2, 2, rows, width), BF16),
+            pltpu.VMEM((2, group, 128), F32),
+            pltpu.VMEM((group, 128), F32),
+            DMA((3,)),
+            DMA((2, 2)),
+            DMA((2, 5)),
+            DMA((2, 2)),
+        ],
+        compiler_params=pltpu.CompilerParams(
+            collective_id=2, has_side_effects=True, vmem_limit_bytes=60 << 20
+        ),
+        name="experts",
+    )(hidden_two, cotangent, select, spread, named.astype(F32), router.T, gate, up, down)
+
+
+def experts_by_xla(hidden_two, cotangent, routes_all, router, gate, up, down, capacity, me, experts):
+    rows = hidden_two.shape[0]
+    hidden_all = lax.all_gather(hidden_two, ALL, axis=0, tiled=True)
+    logits = dot(hidden_all, router)
+    expert_ids = jnp.arange(experts, dtype=jnp.int32)
+    picked = jnp.any(routes_all[:, :, None] == expert_ids, axis=1)
+    masked = jnp.where(picked, logits, masked_score)
+    exponent = jnp.where(picked, jnp.exp(masked - jnp.max(masked, axis=1, keepdims=True)), 0.0)
+    weights_all = exponent / jnp.sum(exponent, axis=1, keepdims=True)
+    mine = jnp.any(routes_all == me, axis=1).reshape(experts, rows)
+    weight_mine = jnp.sum(jnp.where(expert_ids == me, weights_all, 0.0), axis=1).reshape(
+        experts, rows
+    )
+    rank = jnp.cumsum(mine.astype(jnp.int32), axis=1) - 1
+    slots = jnp.arange(capacity, dtype=jnp.int32)
+    select = (rank[:, None, :] == slots[None, :, None]) & mine[:, None, :]
+    select_low = select.astype(BF16)
+    slot_weight = jnp.sum(jnp.where(select, weight_mine[:, None, :], 0.0), axis=2).reshape(-1, 1)
+
+    def pick(values):
+        return jnp.einsum(
+            "sjt,std->sjd",
+            select_low,
+            values.reshape(experts, rows, D),
+            preferred_element_type=F32,
+        ).reshape(experts * capacity, D)
+
+    def place(values):
+        return (
+            jnp.einsum(
+                "sjt,sjd->std",
+                select_low,
+                values.reshape(experts, capacity, D),
+                preferred_element_type=F32,
+            )
+            .astype(BF16)
+            .reshape(experts * rows, D)
+        )
+
+    expert_rows = pick(hidden_all).astype(BF16)
+    own_width = D // experts
+    own_columns = lax.dynamic_slice_in_dim(hidden_all, me * own_width, own_width, axis=1)
+    expert_rows, own_columns, cotangent = lax.optimization_barrier(
+        (expert_rows, own_columns, cotangent)
+    )
+    cotangent_all = lax.all_gather(cotangent, ALL, axis=0, tiled=True)
+    grad_rows_out = pick(cotangent_all)
+    grad_slots = (slot_weight * grad_rows_out).astype(BF16)
+    gate_act = dot(expert_rows, gate)
+    up_act = dot(expert_rows, up)
+    gate_sig = jax.nn.sigmoid(gate_act)
+    gate_silu = gate_act * gate_sig
+    expert_hidden = (gate_silu * up_act).astype(BF16)
+    grad_expert_hidden = dot(grad_slots, down.T)
+    grad_gate_act = (
+        grad_expert_hidden * up_act * gate_sig * (1.0 + gate_act * (1.0 - gate_sig))
+    ).astype(BF16)
+    grad_up_act = (grad_expert_hidden * gate_silu).astype(BF16)
+    grad_rows_in = (dot(grad_gate_act, gate.T) + dot(grad_up_act, up.T)).astype(BF16)
+    expert_out = dot(expert_hidden, down).astype(BF16).astype(F32)
+    grad_weight_slot = jnp.sum(grad_rows_out * expert_out, axis=1).reshape(experts, capacity)
+    grad_weight_mine = jnp.sum(jnp.where(select, grad_weight_slot[:, :, None], 0.0), axis=1)
+    out_rows = (slot_weight * expert_out).astype(BF16)
+
+    def placed_out(after):
+        return place(lax.optimization_barrier((out_rows, after))[0])
+
+    return (
+        own_columns,
+        cotangent_all,
+        place(grad_rows_in),
+        placed_out,
+        weights_all.T,
+        grad_weight_mine,
+        expert_rows,
+        grad_slots,
+        expert_hidden,
+        grad_gate_act,
+        grad_up_act,
+    )
 
 
 def on_device(
@@ -687,83 +1130,35 @@
     ffn_normed = residual * ffn_scale
     hidden_two = (ffn_normed * gain_ffn).astype(BF16)
 
-    (hidden_all,) = exchange("gather_hidden", 2, [("gather", "all", hidden_two)])
-    hidden_all = hidden_all.reshape(experts * rows, D)
-    logits = dot(hidden_all, router)
-    expert_ids = jnp.arange(experts, dtype=jnp.int32)
-    picked = jnp.any(routes_all[:, :, None] == expert_ids, axis=1)
-    masked = jnp.where(picked, logits, masked_score)
-    exponent = jnp.where(picked, jnp.exp(masked - jnp.max(masked, axis=1, keepdims=True)), 0.0)
-    weights_all = exponent / jnp.sum(exponent, axis=1, keepdims=True)
-    mine = jnp.any(routes_all == me, axis=1).reshape(experts, rows)
-    weight_mine = jnp.sum(jnp.where(expert_ids == me, weights_all, 0.0), axis=1).reshape(
-        experts, rows
-    )
-    rank = jnp.cumsum(mine.astype(jnp.int32), axis=1) - 1
-    slots = jnp.arange(capacity, dtype=jnp.int32)
-    select = (rank[:, None, :] == slots[None, :, None]) & mine[:, None, :]
-    select_low = select.astype(BF16)
-    slot_weight = jnp.sum(jnp.where(select, weight_mine[:, None, :], 0.0), axis=2).reshape(-1, 1)
-
-    def pick(values):
-        return jnp.einsum(
-            "sjt,std->sjd",
-            select_low,
-            values.reshape(experts, rows, D),
-            preferred_element_type=F32,
-        ).reshape(experts * capacity, D)
-
-    def place(values):
-        return (
-            jnp.einsum(
-                "sjt,sjd->std",
-                select_low,
-                values.reshape(experts, capacity, D),
-                preferred_element_type=F32,
-            )
-            .astype(BF16)
-            .reshape(experts * rows, D)
-        )
-
-    expert_rows = pick(hidden_all).astype(BF16)
-    own_columns = lax.dynamic_slice_in_dim(hidden_all, me * own_rows, own_rows, axis=1)
+    given = (hidden_two, cotangent, routes_all, router, gate_weight[0], up_weight[0], down_weight[0])
     if large:
-        expert_rows, own_columns, cotangent = lax.optimization_barrier(
-            (expert_rows, own_columns, cotangent)
-        )
-    cotangent_all = lax.all_gather(cotangent, ALL, axis=0, tiled=True)
-    grad_rows_out = pick(cotangent_all)
-    grad_slots = (slot_weight * grad_rows_out).astype(BF16)
-    gate_act = dot(expert_rows, gate_weight[0])
-    up_act = dot(expert_rows, up_weight[0])
-    gate_sig = jax.nn.sigmoid(gate_act)
-    gate_silu = gate_act * gate_sig
-    expert_hidden = (gate_silu * up_act).astype(BF16)
-    grad_expert_hidden = dot(grad_slots, down_weight[0].T)
-    grad_gate_act = (
-        grad_expert_hidden * up_act * gate_sig * (1.0 + gate_act * (1.0 - gate_sig))
-    ).astype(BF16)
-    grad_up_act = (grad_expert_hidden * gate_silu).astype(BF16)
-    grad_rows_in = (
-        dot(grad_gate_act, gate_weight[0].T) + dot(grad_up_act, up_weight[0].T)
-    ).astype(BF16)
-    expert_out = dot(expert_hidden, down_weight[0]).astype(BF16).astype(F32)
-    grad_weight_slot = jnp.sum(grad_rows_out * expert_out, axis=1).reshape(experts, capacity)
-    grad_weight_mine = jnp.sum(jnp.where(select, grad_weight_slot[:, :, None], 0.0), axis=1)
-    placed = place(grad_rows_in).reshape(lines, -1, 2, rows, D)
+        done = experts_by_xla(*given, capacity, me, experts)
+    else:
+        done = experts_call(*given, capacity)
+    hidden_all, _, placed, placed_out, weights_all, grad_weight_mine = done[:6]
+    expert_rows, grad_slots, expert_hidden, grad_gate_act, grad_up_act = [
+        v.reshape(-1, v.shape[-1]) for v in done[6:]
+    ]
+    if large:
+        own_columns = hidden_all
+    else:
+        hidden_all = hidden_all.reshape(experts * rows, D)
+        own_columns = lax.dynamic_slice_in_dim(hidden_all, me * own_rows, own_rows, axis=1)
     grad_weight, grad_rows_sum = exchange(
         "sum_rows",
         3,
         [
             ("gather", "all", grad_weight_mine.reshape(experts, rows)),
-            ("reduce", "all", placed),
+            ("reduce", "all", placed.reshape(lines, -1, 2, rows, D)),
         ],
     )
-    grad_weight = grad_weight.reshape(experts, experts * rows).T
+    grad_weight = grad_weight.reshape(experts, experts * rows)
     if large:
-        expert_out, grad_rows_sum = lax.optimization_barrier((expert_out, grad_rows_sum))
+        placed_out = placed_out(grad_rows_sum)
+    else:
+        placed_out, grad_rows_sum = lax.optimization_barrier((placed_out, grad_rows_sum))
     out_sum = lax.psum_scatter(
-        place((slot_weight * expert_out).astype(BF16)), ALL, scatter_dimension=0, tiled=True
+        placed_out.reshape(experts * rows, D), ALL, scatter_dimension=0, tiled=True
     )
     block_out = (residual + out_sum.astype(F32)).astype(BF16)
     grad_down = dot(expert_hidden.T, grad_slots)
@@ -771,11 +1166,13 @@
     grad_up = dot(expert_rows.T, grad_up_act)
 
     grad_logits = weights_all * (
-        grad_weight - jnp.sum(weights_all * grad_weight, axis=1, keepdims=True)
+        grad_weight - jnp.sum(weights_all * grad_weight, axis=0, keepdims=True)
     )
     grad_logits = grad_logits.astype(BF16)
-    router_grad = dot(own_columns.T, grad_logits)
-    own_grad_logits = lax.dynamic_slice_in_dim(grad_logits, me * rows, rows, axis=0)
+    router_grad = lax.dot_general(
+        own_columns, grad_logits, (((0,), (1,)), ((), ())), preferred_element_type=F32
+    )
+    own_grad_logits = lax.dynamic_slice_in_dim(grad_logits, me * rows, rows, axis=1).T
 
     grad_out = cotangent.astype(F32)
     grad_hidden_two = dot(own_grad_logits, router.T) + grad_rows_sum.astype(F32)

time: 812 us -> 749 us (0.922)
  matrix products: 159 us -> 62.2 us
  Pallas kernels: 519 us -> 588 us
  other arithmetic: 66.8 us -> 38.1 us
    pallas_call x0 -> x1, Pallas kernels: none -> 199 us  [experts_call(): pl.pallas_call(functools.partial(experts_body, capacity, experts), out_sh...]
    pallas_call x6 -> x5, Pallas kernels: 519 us -> 389 us  [exchange(): pl.pallas_call(body, out_shape=tuple(out_shapes), in_specs=in_specs, out_...]
    dot_general x18 -> x10, matrix products: 113 us -> 54.8 us  [dot(): return jnp.dot(left, right, preferred_element_type=F32)]
    dot_general x4 -> x1, matrix products: 41.6 us -> 2.46 us  [on_device(): lax.dot_general(own_columns, grad_logits, (((0,), (1,)), ((), ())), prefe...]
    convert_element_type x3 -> x4, other arithmetic: 21.8 us -> 3.65 us  [the longest x1 1.64 us: experts_call(): spread = (slot[:, :, None] == places[None, None, :]).astype(BF16)]
    unnamed x200 -> x114, local copies, waits for them, and re-layouts: 18.2 us -> 15.7 us
  transfers between devices with their start and end apart: 2 -> 1, of which waited for: 0 -> 0; matrix products, arithmetic and copies ran while one was open for 26% -> 10% of each run, Pallas kernels for 65% -> 23%
where the time goes in v3:
time: 749 us; the launch traced here: 741 us
  Pallas kernels  588 us (79%)
  matrix products  62.2 us (8%)
  other arithmetic  38.1 us (5%)
  local copies, waits for them, and re-layouts  37.6 us (5%)
  between operations  15.1 us (2%)
    pallas_call x5, Pallas kernels, exchange(): pl.pallas_call(body, out_shape=tuple(out_shapes), in_specs=in_specs, out_...  389 us
    pallas_call x1, Pallas kernels, experts_call(): pl.pallas_call(functools.partial(experts_body, capacity, experts), out_sh...  199 us
    dot_general x10, matrix products, dot(): return jnp.dot(left, right, preferred_element_type=F32)  54.8 us
    unnamed x114, local copies, waits for them, and re-layouts  15.7 us
  transfers between devices with their start and end apart: 1, of which 0 were waited for; matrix products, arithmetic and copies ran while one was open for 10% of the time, Pallas kernels for 23%

profile of v3, /device:TPU:0, one launch (start us, length us, event | category | flops | bytes accessed | tf_op | source)
XLA Modules:
  0.0 741.0 jit_solution(2966752572478740275)
XLA Ops:
  14.4 64.3 %gather_inputs.1 = (bf16[4,4,2,32,128]{4,3,2,1,0:T(8,128)(2,1)}, s32[4,4,2,16,128]{4,3,2,1,0:T(8,128)}, bf16[4,4,2,64,1280]{4,3,2,1,0:T(8,128)(2,1)}, bf16[4,128...) custom-call(bf16[32,128]{1,0:T(8,128)(2,1)} %fusion.58.refs_0_, s32[16,128]{1,0:T(8,128)} %pad_bitcast_fusion.refs_1_, ...), custom_call_target="tpu_custom_call" | custom-call | tf_op jit(solution)/shard_map/gather_inputs/pallas_call | solution.py:605
  80.1 2.1 multiply_reduce_fusion.1
  82.7 5.4 fusion.79
  88.3 1.9 slice_bitcast_fusion
  107.5 6.2 convolution_convert_fusion.2
  113.7 42.4 %sum_residual.1 = f32[128,2048]{1,0:T(8,128)} custom-call(bf16[4,128,2048]{2,1,0:T(8,128)(2,1)} %bitcast.254), custom_call_target="tpu_custom_call" | custom-call | tf_op jit(solution)/shard_map/sum_residual/pallas_call | solution.py:605
  157.7 2.8 copy.190
  162.8 2.1 reshape.384
  167.7 198.8 %experts.1 = (bf16[4,4,2,128,2048]{4,3,2,1,0:T(8,128)(2,1)}, bf16[4,4,2,128,2048]{4,3,2,1,0:T(8,128)(2,1)}, bf16[4,4,2,128,2048]{4,3,2,1,0:T(8,128)(2,1)}, bf16[...) custom-call(bf16[128,2048]{1,0:T(8,128)(2,1)} %multiply_convert_fusi, ...), custom_call_target="tpu_custom_call" | custom-call | tf_op jit(solution)/shard_map/experts/pallas_call | solution.py:905
  367.8 110.3 %sum_rows.1 = (f32[4,4,2,32,128]{4,3,2,1,0:T(8,128)}, f32[128,2048]{1,0:T(8,128)}) custom-call(f32[32,128]{1,0:T(8,128)} %reshape.385.refs_0_, bf16[4,4,2,128,2048]{4,3,2,1,0:T(8,128)(2,1)} %get-tuple-element.41.refs_1_), custom_call_target="tpu_custom_call" | custom-call | tf_op jit(solution)/shard_map/sum_rows/pallas_call | solution.py:605
  485.1 58.5 %gather_grad.1 = bf16[4,128,2048]{2,1,0:T(8,128)(2,1)} custom-call(bf16[128,2048]{1,0:T(8,128)(2,1)} %fusion.74.refs_0_), custom_call_target="tpu_custom_call" | custom-call | tf_op jit(solution)/shard_map/gather_grad/pallas_call | solution.py:605
  543.6 5.2 fusion.13
  554.1 2.7 multiply_reduce_fusion.2
  556.9 2.9 copy.197
  567.7 4.1 fusion.75
  572.4 4.4 convolution_convert_fusion.1
  576.8 4.9 convolution_convert_fusion
  581.7 113.5 %sum_gradients.1 = (f32[4,4,2,48,128]{4,3,2,1,0:T(8,128)}, f32[128,2048]{1,0:T(8,128)}, bf16[4,64,1280]{2,1,0:T(8,128)(2,1)}, f32[128,2048]{1,0:T(8,128)}) custom-call(f32[48,128]{1,0:T(8,128)} %fusion.52.refs_0_, bf16[4,128,2048]{2,1,0:T(8,128)(2,1)} %bitcast.251, bf16[4,4,2,64,1280]{4,3,2,1,0:T(8,128)(2,1)} %bitcast.242, bf16[4,2,128,2048]{3,2,1,0:T(8,128)(2,1)} %bitcast.243), custom_call_target="tpu_custom_call" | custom-call | tf_op jit(solution)/shard_map/sum_gradients/pallas_call | solution.py:605
  699.0 2.3 copy.284
  703.2 2.5 fusion.27
  705.7 10.0 %convolution_bitcast_fusion.2 = f32[1,2048,768]{2,1,0:T(8,128)} fusion(bf16[4,384,2048]{2,1,0:T(8,128)(2,1)} %get-tuple-element.52, bf16[4,384,768]{2,1,0:T(8,128)(2,1)S(1)} %copy-done.44), kind=kOutput, calls=%fused_computation.10 | convolution fusion | flops 4831838208 | bytes 14942208 | tf_op jit(solution)/shard_map/dot_general | solution.py:33
  715.7 7.0 convolution_bitcast_fusion.1
  722.8 7.0 convolution_bitcast_fusion
  729.8 3.1 fusion.22
  (208 shorter events, 61.4 us)
Async XLA Ops:
  7.2 5.4 copy-start
  7.2 722.6 %reduce-scatter.2.cloned.1.call-start = ((), (), s32[]{:S(2)}) async-start(), calls=%async_computation.1 | async-start | bytes 17301504 | tf_op jit(solution)/shard_map/reduce_scatter | solution.py:1160
  78.7 3.4 copy-start.19
  92.2 4.6 copy-start.4
  93.2 3.6 copy-start.21
  107.5 6.2 copy-start.35
  113.7 42.4 %copy-start.17 = (bf16[128,2048]{1,0:T(8,128)(2,1)S(1)}, bf16[128,2048]{1,0:T(8,128)(2,1)}, u32[]{:S(2)}) copy-start(bf16[128,2048]{1,0:T(8,128)(2,1)} %refs_3_.1) | copy-start | bytes 1572868
  559.8 7.2 slice-start.4
  561.6 5.3 slice-start.5
  567.7 4.7 copy-start.26
  567.7 4.7 copy-start.36
  696.5 6.3 copy-start.18
  696.6 6.3 copy-start.25
  697.7 5.6 copy-start.32
  701.3 4.4 copy-start.44
  702.9 12.8 %slice-start.2 = ((s8[6291456]{0:T(1024)(128)(4,1)}), s8[4194304]{0:T(1024)(128)(4,1)S(1)}, s32[]{:S(2)}) async-start(s8[6291456]{0:T(1024)(128)(4,1)} %bitcast.286), calls=%async_computation.4 | async-start | bytes 8388608
  705.7 10.0 %slice-start.3 = ((s8[6291456]{0:T(1024)(128)(4,1)}), s8[2097152]{0:T(1024)(128)(4,1)S(1)}, s32[]{:S(2)}) async-start(s8[6291456]{0:T(1024)(128)(4,1)} %bitcast.286), calls=%async_computation.5 | async-start | bytes 4194304
  705.7 10.0 %copy-start.43 = (bf16[4,384,768]{2,1,0:T(8,128)(2,1)S(1)}, bf16[4,384,768]{2,1,0:T(8,128)(2,1)}, u32[]{:S(2)}) copy-start(bf16[4,384,768]{2,1,0:T(8,128)(2,1)} %get-tuple-element.54) | copy-start | bytes 7077892
  705.7 17.1 %slice-start = ((s8[6291456]{0:T(1024)(128)(4,1)}), s8[4194304]{0:T(1024)(128)(4,1)S(1)}, s32[]{:S(2)}) async-start(s8[6291456]{0:T(1024)(128)(4,1)} %bitcast.284), calls=%async_computation.2 | async-start | bytes 8388608
  715.7 7.1 slice-start.1
  715.7 7.1 copy-start.42
  722.8 7.0 copy-start.10
  722.8 7.0 copy-start.23
  729.8 4.1 copy-start.1
  (28 other events, 44.4 us)
Sparse Core Ops, SparseCore 0:
  478.3 226.1 reduce-scatter.1

commit v4 on v3

--- a/solution.py
+++ b/solution.py
@@ -150,18 +150,29 @@
 
 def gather_sems(mode, lines):
     n = 1 if mode == "plane" else lines
-    return [DMA, DMA((2, n)), DMA((n,)), DMA((n, 8)), DMA((n, 8))]
-
-
-def gather_parts(spot, x_ref, out_ref, sems, mode="all"):
-    own_sem, zs, zr, ps, pr = sems
+    return [DMA, DMA((2, n)), DMA((n,)), DMA((n, 8)), DMA((n, 8)), DMA((2, n, 3)), DMA((n, 3))]
+
+
+def gather_parts(spot, x_ref, out_ref, sems, mode="all", even=False):
+    own_sem, zs, zr, ps, pr, vs, vr = sems
     z, b, c, xn, yn, dg, lines = spot.z, spot.b, spot.c, spot.xn, spot.yn, spot.dg, spot.lines
     here = (z, b, c)
     rows = out_ref.shape[-2]
-    lo, hi = pl.ds(0, rows // 2), pl.ds(rows // 2, rows // 2)
     flat = mode == "plane"
     planar = mode != "line"
-    steps = 1 if flat else lines
+    relayed = mode in ("all", "line")
+    via = rows // 4 if even else 0
+    last = pl.ds(rows - via, via)
+    columns = (b, xn, yn, dg)
+
+    def span(way):
+        return rows if way == 0 else rows - via
+
+    def lo(way):
+        return pl.ds(0, span(way) // 2)
+
+    def hi(way):
+        return pl.ds(span(way) // 2, span(way) // 2)
 
     def blk(zz, bb, cc=c):
         if flat:
@@ -170,56 +181,70 @@
 
     mine = 0 if flat else z
 
-    def each(d, fn):
-        if flat:
-            fn(0, 0)
-        else:
-            spot.each(d, fn)
-
     def own():
         return x_ref.at[z] if mode == "swap" else x_ref
 
-    def source(zz, d):
-        return own() if d == 0 else blk(zz, b)
-
-    def hop(zz, way, d):
-        return send(source(zz, d), blk(zz, b), zs.at[way, zz], zr.at[zz], (z + 1 - 2 * way, b, c))
-
-    def plane_copies(zz, d):
-        s = source(zz, d)
+    def source(zz, way):
+        return own() if way == 0 else blk(zz, b)
+
+    def onward(way, fn):
+        if way >= 0:
+
+            @pl.when(z < lines - 1)
+            def _():
+                fn(0)
+
+        if way <= 0:
+
+            @pl.when(z > 0)
+            def _():
+                fn(1)
+
+    def hop(zz, down, way):
+        return send(source(zz, way), blk(zz, b), zs.at[down, zz], zr.at[zz], (z + 1 - 2 * down, b, c))
+
+    def hop_via(zz, k, down):
+        piece = blk(zz, columns[k]).at[last]
+        return send(
+            piece, piece, vs.at[down, zz, k - 1], vr.at[zz, k - 1], (z + 1 - 2 * down, b, c)
+        )
+
+    def plane_copies(zz, way):
+        s, d = source(zz, way), blk(zz, b)
+        whole = (s, d)
+        if via and way != 0:
+            s, d = s.at[pl.ds(0, span(way))], d.at[pl.ds(0, span(way))]
         return [
-            send(s, blk(zz, b), ps.at[zz, 0], pr.at[zz, 0], (z, xn, c)),
-            send(s, blk(zz, b), ps.at[zz, 1], pr.at[zz, 1], (z, yn, c)),
-            send(s, blk(zz, b), ps.at[zz, 4], pr.at[zz, 4], (z, b, 1 - c)),
+            send(s, d, ps.at[zz, 0], pr.at[zz, 0], (z, xn, c)),
+            send(s, d, ps.at[zz, 1], pr.at[zz, 1], (z, yn, c)),
+            send(*whole, ps.at[zz, 4], pr.at[zz, 4], (z, b, 1 - c)),
         ]
 
-    def cross(zz, k):
+    def cross(zz, k, way):
         if k == 0:
-            piece = blk(zz, yn).at[lo]
+            piece = blk(zz, yn).at[lo(way)]
             return send(piece, piece, ps.at[zz, 2], pr.at[zz, 2], (z, xn, c))
-        piece = blk(zz, xn).at[hi]
+        piece = blk(zz, xn).at[hi(way)]
         return send(piece, piece, ps.at[zz, 3], pr.at[zz, 3], (z, yn, c))
 
     def share(zz, k):
-        bb = (b, xn, yn, dg)[k]
-        piece = blk(zz, bb)
+        piece = blk(zz, columns[k])
         return send(piece, piece, ps.at[zz, 4 + k], pr.at[zz, 4 + k], (z, b, 1 - c))
 
     def received(piece, sem):
         send(piece, piece, own_sem, sem, here).wait_recv()
 
+    def over_line(zz, k, way):
+        if not via:
+            return
+        if way != 0:
+            received(blk(zz, columns[k]).at[last], vr.at[zz, k - 1])
+        onward(way, lambda down: hop_via(zz, k, down).start())
+
     def start():
         pltpu.make_async_copy(own(), blk(mine, b), own_sem).start()
-        if mode in ("all", "line"):
-
-            @pl.when(z < lines - 1)
-            def _():
-                hop(z, 0, 0).start()
-
-            @pl.when(z > 0)
-            def _():
-                hop(z, 1, 0).start()
-
+        if relayed:
+            onward(0, lambda down: hop(z, down, 0).start())
         if mode == "swap":
             for d in range(lines - 1, 0, -1):
                 spot.each(
@@ -234,61 +259,47 @@
 
     def line_arrive(zz, way):
         received(blk(zz, b), zr.at[zz])
-        if mode in ("all", "line"):
-            if way > 0:
-
-                @pl.when(z < lines - 1)
-                def _():
-                    hop(zz, 0, 1).start()
-            else:
-
-                @pl.when(z > 0)
-                def _():
-                    hop(zz, 1, 1).start()
-
+        if relayed:
+            onward(way, lambda down: hop(zz, down, way).start())
         if planar:
-            for copy in plane_copies(zz, 1):
+            for copy in plane_copies(zz, way):
                 copy.start()
 
     def plane_arrive(zz, way):
-        received(blk(zz, xn), pr.at[zz, 0])
-        cross(zz, 1).start()
-        received(blk(zz, yn), pr.at[zz, 1])
-        cross(zz, 0).start()
+        part = pl.ds(0, span(way))
+        received(blk(zz, xn).at[part], pr.at[zz, 0])
+        cross(zz, 1, way).start()
+        received(blk(zz, yn).at[part], pr.at[zz, 1])
+        cross(zz, 0, way).start()
+        over_line(zz, 1, way)
+        over_line(zz, 2, way)
         share(zz, 1).start()
         share(zz, 2).start()
 
     def cross_arrive(zz, way):
-        received(blk(zz, dg).at[lo], pr.at[zz, 2])
-        received(blk(zz, dg).at[hi], pr.at[zz, 3])
+        received(blk(zz, dg).at[lo(way)], pr.at[zz, 2])
+        received(blk(zz, dg).at[hi(way)], pr.at[zz, 3])
+        over_line(zz, 3, way)
         share(zz, 3).start()
 
     def drain(zz, way):
         if planar:
             for k in range(4):
                 share(zz, k).wait_send()
-            for copy in plane_copies(zz, 1)[:2]:
+            for copy in plane_copies(zz, way)[:2]:
                 copy.wait_send()
-            cross(zz, 0).wait_send()
-            cross(zz, 1).wait_send()
-        if mode in ("all", "line"):
-            if way >= 0:
-
-                @pl.when(z < lines - 1)
-                def _():
-                    hop(zz, 0, 1).wait_send()
-
-            if way <= 0:
-
-                @pl.when(z > 0)
-                def _():
-                    hop(zz, 1, 1).wait_send()
-
+            cross(zz, 0, way).wait_send()
+            cross(zz, 1, way).wait_send()
+        if relayed:
+            onward(way, lambda down: hop(zz, down, way).wait_send())
+        if via:
+            for k in (1, 2, 3):
+                onward(way, lambda down, k=k: hop_via(zz, k, down).wait_send())
         if mode == "swap" and way != 0:
             send(x_ref.at[zz], blk(z, b), zs.at[0, zz], zr.at[z], (zz, b, c)).wait_send()
 
     def shared(zz, k):
-        received(blk(zz, (b, xn, yn, dg)[k], 1 - c), pr.at[zz, 4 + k])
+        received(blk(zz, columns[k], 1 - c), pr.at[zz, 4 + k])
 
     def end():
         pltpu.make_async_copy(own(), blk(mine, b), own_sem).wait()
@@ -349,14 +360,12 @@
             DMA((n, 8)),
             DMA((n, 8)),
         ]
-    if mode in ("all", "line"):
-        out += [pltpu.VMEM((2, lines, rows, cols), dtype)]
+    if mode == "line":
+        out += [pltpu.VMEM((2, lines, rows, cols), dtype), pltpu.VMEM((lines, rows, cols), dtype)]
+    if mode == "all":
+        out += [pltpu.VMEM((lines, rows, cols), dtype)]
     if mode != "plane":
         out += [DMA((2, lines)), DMA((2, lines))]
-    if mode == "line":
-        out += [pltpu.VMEM((lines, rows, cols), dtype)]
-    if mode == "all":
-        out += [pltpu.VMEM((n, 4, rows, cols), dtype), DMA]
     return out
 
 
@@ -372,52 +381,26 @@
         dst[at] = total.astype(dst.dtype)
 
 
-def reduce(spot, mode, p_ref, out_ref, scratch):
-    z, b, c, xn, yn, dg, lines = spot.z, spot.b, spot.c, spot.xn, spot.yn, spot.dg, spot.lines
+def reduce_parts(spot, mode, term, out_ref, scratch):
+    z, b, c, xn, yn = spot.z, spot.b, spot.c, spot.xn, spot.yn
     here = (z, b, c)
-    flat = mode == "plane"
-    planar = mode != "line"
-    steps = 1 if flat else lines
     scratch = list(scratch)
-    if planar:
-        pair, crossed, met, ps, pr = scratch[:5]
-        scratch = scratch[5:]
-        rows = pair.shape[-2]
-        lo, hi = pl.ds(0, rows // 2), pl.ds(rows // 2, rows // 2)
-    if mode in ("all", "line"):
-        passed = scratch.pop(0)
-    if mode != "plane":
-        zs, zr = scratch[:2]
-        scratch = scratch[2:]
-    if mode == "line":
-        total_ref = scratch[0]
-    if mode == "all":
-        kept, kept_sem = scratch
+    pair, crossed, met, ps, pr = scratch[:5]
+    passed = scratch[5] if mode == "all" else out_ref
+    zs, zr = scratch[-2:]
+    rows = pair.shape[-2]
+    lo, hi = pl.ds(0, rows // 2), pl.ds(rows // 2, rows // 2)
 
     def total(zz):
-        return met.at[zz, 0] if planar else total_ref.at[zz]
-
-    def term(zz, bb, cc):
-        return p_ref.at[bb, cc] if flat else p_ref.at[zz, bb, cc]
-
-    def each(d, fn):
-        if flat:
-            fn(0, 0)
-        else:
-            spot.each(d, fn)
-
-    def kept_term(zz, bb):
-        return kept.at[zz, bb] if mode == "all" else term(zz, bb, c)
-
-    bbs = (dg, xn, yn, b)
+        return met.at[zz, 0]
 
     def share(zz, k):
         return send(
-            term(zz, bbs[k], 1 - c), pair.at[zz, k], ps.at[zz, k], pr.at[zz, k], (z, b, 1 - c)
+            term(zz, k, 1 - c), pair.at[zz, k], ps.at[zz, k], pr.at[zz, k], (z, b, 1 - c)
         )
 
     def cross(zz, k):
-        piece = pair.at[zz, 0, (lo, hi)[k]]
+        piece = pair.at[zz, 3, (lo, hi)[k]]
         dev = (z, (yn, xn)[k], c)
         return send(piece, crossed.at[zz, k], ps.at[zz, 4 + k], pr.at[zz, 4 + k], dev)
 
@@ -425,27 +408,21 @@
         dev = (z, (xn, yn)[k], c)
         return send(pair.at[zz, 1 + k], met.at[zz, k], ps.at[zz, 6 + k], pr.at[zz, 6 + k], dev)
 
-    def hop(zz, way):
-        return send(
-            total(zz),
-            passed.at[way, zz],
-            zs.at[way, zz],
-            zr.at[way, zz],
-            (z + 1 - 2 * way, b, c),
-        )
+    def away(zz):
+        return send(total(zz), passed.at[z], zs.at[0, zz], zr.at[0, z], (zz, b, c))
 
     def received(piece, sem):
-        send(piece, piece, ps.at[0, 0] if planar else zs.at[0, 0], sem, here).wait_recv()
+        send(piece, piece, ps.at[0, 0], sem, here).wait_recv()
 
     def start(zz, way):
-        for k in range(4):
+        for k in (3, 1, 2, 0):
             share(zz, k).start()
 
     def first(zz, way):
-        for k in range(3):
+        for k in (3, 1, 2):
             received(pair.at[zz, k], pr.at[zz, k])
-            add_into(pair.at[zz, k], pair.at[zz, k], kept_term(zz, bbs[k]))
-            if k == 0:
+            add_into(pair.at[zz, k], pair.at[zz, k], term(zz, k, c))
+            if k == 3:
                 cross(zz, 0).start()
                 cross(zz, 1).start()
 
@@ -458,100 +435,212 @@
         meet(zz, 1).start()
 
     def third(zz, way):
-        received(pair.at[zz, 3], pr.at[zz, 3])
+        received(pair.at[zz, 0], pr.at[zz, 0])
         received(met.at[zz, 0], pr.at[zz, 6])
         received(met.at[zz, 1], pr.at[zz, 7])
-        dst = out_ref if flat else total(zz)
-        add_into(dst, met.at[zz, 0], met.at[zz, 1], pair.at[zz, 3], kept_term(zz, b))
-        if mode == "swap" and way != 0:
-            send(total(zz), out_ref.at[z], zs.at[0, zz], zr.at[0, z], (zz, b, c)).start()
-
-    def line(zz, way):
-        if way == 0:
-            base = total(zz) if planar else p_ref.at[zz]
-            both = (passed.at[0, zz], passed.at[1, zz])
-
-            @pl.when(z > 0)
+        dst = out_ref if mode == "plane" else total(zz)
+        add_into(dst, met.at[zz, 0], met.at[zz, 1], pair.at[zz, 0], term(zz, 0, c))
+        if mode != "plane":
+
+            @pl.when(zz != z)
             def _():
-                received(passed.at[0, zz], zr.at[0, zz])
-
-            @pl.when(z < lines - 1)
+                away(zz).start()
+
+    def end():
+        if mode == "plane":
+            return
+        for d in range(1, spot.lines):
+            spot.each(d, lambda zz, way: received(passed.at[zz], zr.at[0, zz]))
+        if mode == "swap":
+            add_into(out_ref.at[z], total(z))
+            return
+        for edge in range(spot.lines):
+
+            @pl.when(z == edge)
             def _():
-                received(passed.at[1, zz], zr.at[1, zz])
-
-            @pl.when(z == 0)
-            def _():
-                add_into(out_ref, base, both[1])
-
-            @pl.when(z == lines - 1)
-            def _():
-                add_into(out_ref, base, both[0])
-
-            @pl.when((z > 0) & (z < lines - 1))
-            def _():
-                add_into(out_ref, base, both[0], both[1])
-
-            return
+                others = [passed.at[q] for q in range(spot.lines) if q != edge]
+                add_into(out_ref, total(edge), *others)
+
+    def sent(zz, way):
+        for k in range(4):
+            share(zz, k).wait_send()
+
+    def drain(zz, way):
+        for k in range(2):
+            cross(zz, k).wait_send()
+            meet(zz, k).wait_send()
+        if mode != "plane" and way != 0:
+            away(zz).wait_send()
+
+    return {
+        "start": start,
+        "first": first,
+        "second": second,
+        "third": third,
+        "sent": sent,
+        "end": end,
+        "drain": drain,
+    }
+
+
+def reduce(spot, mode, p_ref, out_ref, scratch):
+    flat = mode == "plane"
+    steps = 1 if flat else spot.lines
+
+    columns = (spot.b, spot.xn, spot.yn, spot.dg)
+
+    def term(zz, k, cc):
+        return p_ref.at[columns[k], cc] if flat else p_ref.at[zz, columns[k], cc]
+
+    def each(d, fn):
+        if flat:
+            fn(0, 0)
+        else:
+            spot.each(d, fn)
+
+    parts = reduce_parts(spot, mode, term, out_ref, scratch)
+    order = list(range(steps - 1, -1, -1))
+    for d in order:
+        each(d, parts["start"])
+    yield
+    for s in range(steps + 2):
+        for lag, name in enumerate(("first", "second", "third")):
+            if 0 <= s - lag < steps:
+                each(order[s - lag], parts[name])
+        yield
+    parts["end"]()
+    for d in range(steps):
+        each(d, parts["sent"])
+        each(d, parts["drain"])
+    yield
+
+
+def reduce_line(spot, p_ref, out_ref, scratch):
+    passed, total_ref, zs, zr = scratch
+    z, b, c, lines = spot.z, spot.b, spot.c, spot.lines
+    here = (z, b, c)
+
+    def received(down, zz):
+        piece = passed.at[down, zz]
+        send(piece, piece, zs.at[0, 0], zr.at[down, zz], here).wait_recv()
+
+    def hop(src, zz, down):
+        return send(
+            src.at[zz], passed.at[down, zz], zs.at[down, zz], zr.at[down, zz], (z + 1 - 2 * down, b, c)
+        )
+
+    def step(zz, way):
         down = 1 if way > 0 else 0
         first_one = (z == lines - 1) if down else (z == 0)
-        base = total(zz) if planar else p_ref.at[zz]
 
         @pl.when(jnp.logical_not(first_one))
         def _():
-            received(passed.at[down, zz], zr.at[down, zz])
-            add_into(total(zz), base, passed.at[down, zz])
-            hop(zz, down).start()
+            received(down, zz)
+            add_into(total_ref.at[zz], p_ref.at[zz], passed.at[down, zz])
+            hop(total_ref, zz, down).start()
 
         @pl.when(first_one)
         def _():
-            if planar:
-                hop(zz, down).start()
-            else:
-                send(
-                    p_ref.at[zz],
-                    passed.at[down, zz],
-                    zs.at[down, zz],
-                    zr.at[down, zz],
-                    (z + 1 - 2 * down, b, c),
-                ).start()
-
-    order = list(range(steps - 1, -1, -1))
-    if planar:
-        for d in order:
-            each(d, start)
-    if mode == "all":
-        bring = pltpu.make_async_copy(p_ref.at[:, :, c], kept, kept_sem)
-        bring.start()
-        bring.wait()
-    lag = (1, 2, 3, 4) if planar else (9, 9, 9, 1)
+            hop(p_ref, zz, down).start()
+
+    for d in range(lines - 1, 0, -1):
+        spot.each(d, step)
+        yield
+
+    @pl.when(z > 0)
+    def _():
+        received(0, z)
+
+    @pl.when(z < lines - 1)
+    def _():
+        received(1, z)
+
+    @pl.when(z == 0)
+    def _():
+        add_into(out_ref, p_ref.at[z], passed.at[1, z])
+
+    @pl.when(z == lines - 1)
+    def _():
+        add_into(out_ref, p_ref.at[z], passed.at[0, z])
+
+    @pl.when((z > 0) & (z < lines - 1))
+    def _():
+        add_into(out_ref, p_ref.at[z], passed.at[0, z], passed.at[1, z])
+
+    for d in range(1, lines):
+        spot.each(d, lambda zz, way: hop(total_ref, zz, 1 if way > 0 else 0).wait_send())
     yield
-    for s in range(1, steps + 4):
-        for fn, behind in zip((first, second, third, line), lag):
-            i = s - behind
-            if not 0 <= i < steps or behind > 8:
-                continue
-            if fn is line and mode not in ("all", "line"):
-                continue
-            each(order[i], fn)
-        yield
-
-    def drain(zz, way):
-        if planar:
-            for k in range(4):
-                share(zz, k).wait_send()
-            for k in range(2):
-                cross(zz, k).wait_send()
-                meet(zz, k).wait_send()
-        if mode in ("all", "line") and way != 0:
-            hop(zz, 1 if way > 0 else 0).wait_send()
-        if mode == "swap" and way != 0:
-            send(total(zz), out_ref.at[z], zs.at[0, zz], zr.at[0, z], (zz, b, c)).wait_send()
-            received(out_ref.at[zz], zr.at[0, zz])
-
-    for d in range(steps):
-        each(d, drain)
-    if mode == "swap":
-        add_into(out_ref.at[z], total(z))
+
+
+def dot_tn(left, right):
+    return lax.dot_general(left, right, (((0,), (0,)), ((), ())), preferred_element_type=F32)
+
+
+def products_scratch(count, width, ff):
+    return [
+        pltpu.VMEM((3, count, ff), BF16),
+        pltpu.VMEM((2, count, 256), BF16),
+        pltpu.VMEM((2, 2, 256, ff), F32),
+        pltpu.VMEM((2, ff, 256), F32),
+        DMA((3,)),
+        DMA((2,)),
+        DMA((2, 2)),
+        DMA((2,)),
+    ]
+
+
+def products(ins, outs, scratch):
+    x_ref, dy_ref, a_ref, dg_ref, du_ref = ins
+    gate_out, up_out, down_out = outs
+    near, tile, wide, tall, n_sem, t_sem, w_sem, d_sem = scratch
+    half = x_ref.shape[1] // 256
+
+    def columns(n):
+        return pl.ds((n % half) * 256, 256)
+
+    def load(n):
+        src = x_ref if n < half else dy_ref
+        return pltpu.make_async_copy(src.at[:, columns(n)], tile.at[n % 2], t_sem.at[n % 2])
+
+    def store(n):
+        q = n % 2
+        if n < half:
+            return [
+                pltpu.make_async_copy(wide.at[q, 0], gate_out.at[columns(n)], w_sem.at[q, 0]),
+                pltpu.make_async_copy(wide.at[q, 1], up_out.at[columns(n)], w_sem.at[q, 1]),
+            ]
+        return [pltpu.make_async_copy(tall.at[q], down_out.at[:, columns(n)], d_sem.at[q])]
+
+    near_loads = [
+        pltpu.make_async_copy(src, near.at[i], n_sem.at[i])
+        for i, src in enumerate((a_ref, dg_ref, du_ref))
+    ]
+    for copy in near_loads:
+        copy.start()
+    load(0).start()
+    yield
+    for copy in near_loads:
+        copy.wait()
+    for n in range(2 * half):
+        load(n).wait()
+        if n + 1 < 2 * half:
+            load(n + 1).start()
+        if n % half >= 2:
+            for copy in store(n - 2):
+                copy.wait()
+        q = n % 2
+        if n < half:
+            wide[q, 0] = dot_tn(tile[q], near[1])
+            wide[q, 1] = dot_tn(tile[q], near[2])
+        else:
+            tall[q] = dot_tn(near[0], tile[q])
+        for copy in store(n):
+            copy.start()
+        if n % 3 == 2:
+            yield
+    for n in (half - 2, half - 1, 2 * half - 2, 2 * half - 1):
+        for copy in store(n):
+            copy.wait()
     yield
 
 
@@ -569,12 +658,24 @@
     cells = lax.axis_size("plane") * lax.axis_size("core")
     if cells != 8 or lines != 4:
         return [exchange_by_xla(kind, mode, x, lines, cells) for kind, mode, x in jobs]
-    in_specs, out_shapes, out_specs, scratch, counts = [], [], [], [], []
+    far, near = pl.BlockSpec(memory_space=pl.ANY), pl.BlockSpec(memory_space=pltpu.VMEM)
+    args, in_specs, out_shapes, out_specs, scratch, counts = [], [], [], [], [], []
     for kind, mode, x in jobs:
+        if kind == "products":
+            width, ff = x[0].shape[1], x[2].shape[1]
+            args += x
+            in_specs += [far] * 5
+            out_shapes += [jax.ShapeDtypeStruct((width, ff), F32)] * 2
+            out_shapes.append(jax.ShapeDtypeStruct((ff, width), F32))
+            out_specs += [far] * 3
+            own = products_scratch(x[0].shape[0], width, ff)
+            counts.append((5, 3, len(own)))
+            scratch += own
+            continue
         rows, cols = x.shape[-2:]
-        space = pltpu.VMEM if kind == "reduce" else pl.ANY
-        far = kind == "gather" or mode == "all"
-        in_specs.append(pl.BlockSpec(memory_space=pl.ANY if far else pltpu.VMEM))
+        spec = near if kind == "reduce" else far
+        args.append(x)
+        in_specs.append(spec)
         if kind == "gather":
             lead = {"line": (lines,), "plane": (4, 2)}.get(mode, (lines, 4, 2))
             out_shapes.append(jax.ShapeDtypeStruct((*lead, rows, cols), x.dtype))
@@ -585,37 +686,51 @@
             else:
                 out_shapes.append(jax.ShapeDtypeStruct((rows, cols), F32))
             own = reduce_scratch(mode, lines, rows, cols, x.dtype)
-        out_specs.append(pl.BlockSpec(memory_space=space))
+        out_specs.append(spec)
         scratch += own
-        counts.append(len(own))
-    n = len(jobs)
+        counts.append((1, 1, len(own)))
+    kinds = [(kind, mode) for kind, mode, _ in jobs]
 
     def body(*refs):
         spot = Spot(lines)
         spot.greet()
-        at = 2 * n
+        ins, outs, rest = 0, len(args), len(args) + len(out_shapes)
         makers = []
-        for i, (kind, mode, _) in enumerate(jobs):
-            mine = refs[at : at + counts[i]]
-            at += counts[i]
-            fn = gather if kind == "gather" else reduce
-            makers.append(fn(spot, mode, refs[i], refs[n + i], mine))
+        for (kind, mode), (n_in, n_out, n_rest) in zip(kinds, counts):
+            i, o, w = refs[ins : ins + n_in], refs[outs : outs + n_out], refs[rest : rest + n_rest]
+            ins, outs, rest = ins + n_in, outs + n_out, rest + n_rest
+            if kind == "products":
+                makers.append(products(i, o, w))
+            elif kind == "gather":
+                makers.append(gather(spot, mode, i[0], o[0], w))
+            elif mode == "line":
+                makers.append(reduce_line(spot, i[0], o[0], w))
+            else:
+                makers.append(reduce(spot, mode, i[0], o[0], w))
         run_steps(makers)
 
-    return pl.pallas_call(
+    outs = pl.pallas_call(
         body,
         out_shape=tuple(out_shapes),
         in_specs=in_specs,
         out_specs=tuple(out_specs),
         scratch_shapes=scratch,
         compiler_params=pltpu.CompilerParams(
-            collective_id=cid, has_side_effects=True, vmem_limit_bytes=60 << 20
+            collective_id=cid, has_side_effects=True, vmem_limit_bytes=62 << 20
         ),
         name=name,
-    )(*[x for _, _, x in jobs])
+    )(*args)
+    results, at = [], 0
+    for _, n_out, _ in counts:
+        results.append(outs[at] if n_out == 1 else outs[at : at + n_out])
+        at += n_out
+    return results
 
 
 def exchange_by_xla(kind, mode, x, lines, cells):
+    if kind == "products":
+        hidden, grad_slots, acts, grad_gate, grad_up = x
+        return dot(hidden.T, grad_gate), dot(hidden.T, grad_up), dot(acts.T, grad_slots)
     rows, cols = x.shape[-2:]
     if kind == "gather":
         if mode == "swap":
@@ -648,32 +763,50 @@
     return lax.dot_general(left, right, (((1,), (1,)), ((), ())), preferred_element_type=F32)
 
 
-def experts_body(capacity, experts, *refs):
+def experts_body(capacity, *refs):
     lines = 4
-    (h_ref, t_ref, sel_ref, spread_ref, named_ref, router_ref, gate_ref, up_ref, down_ref) = refs[:9]
-    (hall, tall, px, py, w_ref, dw_ref, x_out, dy_out, a_out, dg_out, du_out) = refs[9:20]
-    rest = list(refs[20:])
-    h_sems, t_sems = rest[:5], rest[5:10]
-    (wg, wu, wd, hb, tb, xs, zs, dys, acts, dgs, dus, rs, ys, stage, slot_w, acc) = rest[10:26]
-    (w_sem, l_sem, o_sem, p_sem) = rest[26:]
+    (h_ref, tall, own_w_ref, sel_ref, spread_ref, gate_ref, up_ref, down_ref) = refs[:8]
+    (hall, py, dw_all, w_ref, sum_ref, x_out, dy_out, a_out, dg_out, du_out) = refs[8:18]
+    rest = list(refs[18:])
+    h_sems, w_sems, dw_sems = rest[:7], rest[7:14], rest[14:21]
+    sum_scratch = rest[21:29]
+    (wg, wu, wd, hb, tb, xs, zs, dys, acts, dgs, dus, rs, ys) = rest[29:42]
+    (stage, stage_y, slot_w, acc, dw_ref, w_sem, l_sem, o_sem, p_sem) = rest[42:]
     spot = Spot(lines)
     z, b, c, xn, yn, dg_spot = spot.z, spot.b, spot.c, spot.xn, spot.yn, spot.dg
     me = (z * 4 + b) * 2 + c
     pair = 2 * capacity
     spot.greet()
-    steps_h = gather_parts(spot, h_ref, hall, h_sems)
-    steps_t = gather_parts(spot, t_ref, tall, t_sems)
-    both = (steps_h, steps_t)
+    steps_h = gather_parts(spot, h_ref, hall, h_sems, even=True)
+    steps_w = gather_parts(spot, own_w_ref, w_ref, w_sems)
+    steps_dw = gather_parts(spot, dw_ref, dw_all, dw_sems)
+    both = (steps_w, steps_h)
     columns = (b, xn, yn, dg_spot)
+    turn = [0]
+
+    def term(zz, k, cc):
+        return stage.at[turn[0] % 2, k, cc]
+
+    steps_r = reduce_parts(spot, "all", term, sum_ref, sum_scratch)
+
+    def sums(name, i):
+        turn[0] = i
+        steps_r[name](pick_order(z, i), 1)
+
+    def comm_dw(name, d):
+        spot.each(d, steps_dw[name])
+
     loads = [
         pltpu.make_async_copy(gate_ref, wg, w_sem.at[0]),
         pltpu.make_async_copy(up_ref, wu, w_sem.at[1]),
         pltpu.make_async_copy(down_ref, wd, w_sem.at[2]),
     ]
 
-    def comm(name, d):
+    def comm(*names):
         for s in both:
-            spot.each(d, s[name])
+            for name in names:
+                part, d = name.split()
+                spot.each(int(d), s[part])
 
     def load(i, k, n):
         zz, bb = pick_order(z, i), columns[k]
@@ -697,18 +830,9 @@
             copy.wait()
         rows = hb.shape[2]
         width = hb.shape[3]
-        hidden = hb.at[n % 2]
-        token = tb.at[n % 2]
-        cols = pl.ds(pl.multiple_of(which * 2 * rows, 2 * rows), 2 * rows)
-        logits = dot_nt(router_ref[...], hidden[...].reshape(2 * rows, width))
-        named = named_ref[:, cols] > 0.5
-        masked = jnp.where(named, logits, masked_score)
-        top = jnp.max(masked, axis=0, keepdims=True)
-        exponent = jnp.where(named, jnp.exp(masked - top), 0.0)
-        weights = exponent / jnp.sum(exponent, axis=0, keepdims=True)
-        w_ref[:, cols] = weights
-        expert_row = lax.broadcasted_iota(jnp.int32, weights.shape, 0)
-        mine = jnp.sum(jnp.where(expert_row == me, weights, 0.0), axis=0, keepdims=True)
+        mine = jnp.concatenate(
+            [w_ref[zz, bb, 0, pl.ds(me, 1), :], w_ref[zz, bb, 1, pl.ds(me, 1), :]], axis=1
+        )
         select = sel_ref[which]
         per_slot = jnp.sum(select.astype(F32) * mine, axis=1, keepdims=True)
         slot_w[i % 2, at, :] = jnp.broadcast_to(per_slot, (pair, 128))
@@ -768,18 +892,14 @@
             ys[:, part] = (slot_w[q, :, 0:1] * y).astype(BF16)
 
     def put(zz, bb, m):
-        return [
-            pltpu.make_async_copy(stage.at[m % 2, 0], px.at[zz, bb], p_sem.at[m % 2, 0]),
-            pltpu.make_async_copy(stage.at[m % 2, 1], py.at[zz, bb], p_sem.at[m % 2, 1]),
-        ]
+        return pltpu.make_async_copy(stage_y.at[m % 2], py.at[zz, bb], p_sem.at[m % 2])
 
     def place(i, k, m):
         zz, bb = pick_order(z, i), columns[k]
         at = pl.ds(pl.multiple_of(bb * pair, 16), pair)
         which = zz * 4 + bb
         if m >= 2:
-            for copy in put(zz, bb, m):
-                copy.wait()
+            put(zz, bb, m).wait()
         dw_slot = jnp.sum(acc[at, :], axis=1, keepdims=True)
         dw_ref[pl.ds(which, 1), :] = jnp.sum(
             sel_ref[which].astype(F32) * dw_slot, axis=0, keepdims=True
@@ -790,12 +910,16 @@
         @pl.loop(0, rs.shape[1] // 512)
         def _(j):
             part = pl.ds(pl.multiple_of(j * 512, 512), 512)
-            for n, src in enumerate((rs, ys)):
-                full = jnp.dot(spread, src[at, part], preferred_element_type=F32)
-                stage[m % 2, n, :, :, part] = full.astype(BF16).reshape(2, rows, 512)
-
-        for copy in put(zz, bb, m):
-            copy.start()
+            full = jnp.dot(spread, rs[at, part], preferred_element_type=F32)
+            stage[i % 2, k, :, :, part] = full.astype(BF16).reshape(2, rows, 512)
+            full = jnp.dot(spread, ys[at, part], preferred_element_type=F32)
+            stage_y[m % 2, :, :, part] = full.astype(BF16).reshape(2, rows, 512)
+
+        put(zz, bb, m).start()
+
+    def places(i):
+        for n, k in enumerate((3, 1, 2, 0)):
+            place(i, k, 4 * i + n)
 
     for s in both:
         s["start"]()
@@ -804,92 +928,114 @@
     for s in both:
         s["end"]()
     fetch(0, 0, 0)
-    comm("line", 1)
-    comm("plane", 0)
+    comm("line 1", "plane 0")
     fetch(0, 1, 1)
     pick(0, 0, 0)
     fetch(0, 2, 2)
     pick(0, 1, 1)
-    comm("line", 2)
+    comm("line 2", "plane 1", "cross 0")
     fetch(1, 0, 3)
     pick(0, 2, 2)
-    comm("plane", 1)
-    comm("cross", 0)
     fetch(0, 3, 4)
     pick(1, 0, 3)
     for copy in loads:
         copy.wait()
     fetch(1, 1, 5)
     pick(0, 3, 4)
-    comm("line", 3)
     inner(0)
-    comm("plane", 2)
+    comm("line 3", "plane 2", "cross 1")
     fetch(1, 2, 6)
     pick(1, 1, 5)
     outer(0)
-    comm("cross", 1)
     fetch(1, 3, 7)
     pick(1, 2, 6)
-    place(0, 0, 0)
-    place(0, 1, 1)
-    comm("plane", 3)
-    place(0, 2, 2)
-    place(0, 3, 3)
+    places(0)
+    comm("plane 3")
     pick(1, 3, 7)
+    sums("start", 0)
     inner(1)
     for copy in keep(0):
         copy.wait()
     fetch(2, 0, 8)
-    comm("cross", 2)
+    comm("cross 2")
     fetch(2, 1, 9)
     pick(2, 0, 8)
+    sums("first", 0)
     outer(1)
     fetch(2, 2, 10)
     pick(2, 1, 9)
-    for k in range(4):
-        place(1, k, 4 + k)
-    comm("cross", 3)
+    sums("second", 0)
+    places(1)
+    comm("cross 3")
     fetch(2, 3, 11)
     pick(2, 2, 10)
+    sums("start", 1)
     fetch(3, 0, 12)
     pick(2, 3, 11)
     inner(2)
     for copy in keep(1):
         copy.wait()
+    sums("third", 0)
     fetch(3, 1, 13)
     pick(3, 0, 12)
+    sums("first", 1)
     outer(2)
     fetch(3, 2, 14)
     pick(3, 1, 13)
-    for k in range(4):
-        place(2, k, 8 + k)
+    sums("second", 1)
+    sums("sent", 0)
+    places(2)
     fetch(3, 3, 15)
     pick(3, 2, 14)
+    sums("start", 2)
     pick(3, 3, 15)
+    sums("third", 1)
     inner(3)
+    sums("first", 2)
     outer(3)
-    for k in range(4):
-        place(3, k, 12 + k)
+    sums("second", 2)
+    sums("sent", 1)
+    places(3)
+    steps_dw["start"]()
+    sums("start", 3)
+    sums("third", 2)
+    comm_dw("line", 1)
+    comm_dw("plane", 0)
+    sums("first", 3)
+    comm_dw("line", 2)
+    comm_dw("plane", 1)
+    comm_dw("cross", 0)
+    sums("second", 3)
+    comm_dw("line", 3)
+    comm_dw("plane", 2)
+    comm_dw("cross", 1)
+    comm_dw("plane", 3)
+    comm_dw("cross", 2)
+    comm_dw("cross", 3)
+    sums("third", 3)
+    steps_r["end"]()
     for m in (0, 1):
-        for copy in put(z, b, m):
-            copy.wait()
+        put(z, b, m).wait()
     for i in (2, 3):
         for copy in keep(i):
             copy.wait()
+        sums("sent", i)
     for d in range(lines):
-        comm("drain", d)
-
-
-def experts_call(hidden_two, cotangent, routes_all, router, gate, up, down, capacity):
+        comm(f"drain {d}")
+        comm_dw("drain", d)
+        spot.each(d, steps_r["drain"])
+        for k in range(4):
+            spot.each(d, lambda zz, way, k=k: steps_dw["shared"](zz, k))
+    steps_dw["end"]()
+
+
+def experts_call(hidden_two, cotangent_all, own_weights, routes_all, gate, up, down, capacity):
     lines, experts = 4, 32
     rows, width = hidden_two.shape
     ff = gate.shape[1]
     pair = 2 * capacity
     group = 4 * pair
     me = (lax.axis_index("line") * 4 + lax.axis_index("plane")) * 2 + lax.axis_index("core")
-    named = jnp.any(
-        routes_all.T[:, None, :] == jnp.arange(experts, dtype=jnp.int32)[None, :, None], axis=0
-    )
     mine = jnp.any(routes_all == me, axis=1).reshape(experts, rows)
     rank = jnp.cumsum(mine.astype(jnp.int32), axis=1) - 1
     slot = rank + (jnp.arange(experts, dtype=jnp.int32) % 2 * capacity)[:, None]
@@ -903,25 +1049,26 @@
     wide = jax.ShapeDtypeStruct((lines, group, width), BF16)
     thin = jax.ShapeDtypeStruct((lines, group, ff), BF16)
     return pl.pallas_call(
-        functools.partial(experts_body, capacity, experts),
+        functools.partial(experts_body, capacity),
         out_shape=(
             all_rows,
             all_rows,
-            all_rows,
-            all_rows,
-            jax.ShapeDtypeStruct((experts, experts * rows), F32),
-            jax.ShapeDtypeStruct((experts // 2, 2 * rows), F32),
+            jax.ShapeDtypeStruct((lines, 4, 2, experts // 2, 2 * rows), F32),
+            jax.ShapeDtypeStruct((lines, 4, 2, experts, rows), F32),
+            jax.ShapeDtypeStruct((rows, width), F32),
             wide,
             wide,
             thin,
             thin,
             thin,
         ),
-        in_specs=[anywhere, anywhere, near, near, near, near, anywhere, anywhere, anywhere],
-        out_specs=(*[anywhere] * 4, near, near, *[anywhere] * 5),
+        in_specs=[anywhere, anywhere, near, near, near, anywhere, anywhere, anywhere],
+        out_specs=(*[anywhere] * 3, near, near, *[anywhere] * 5),
         scratch_shapes=[
             *gather_sems("all", lines),
             *gather_sems("all", lines),
+            *gather_sems("all", lines),
+            *reduce_scratch("all", lines, rows, width),
             pltpu.VMEM((width, ff), BF16),
             pltpu.VMEM((width, ff), BF16),
             pltpu.VMEM((ff, width), BF16),
@@ -935,30 +1082,31 @@
             pltpu.VMEM((2, group, ff), BF16),
             pltpu.VMEM((group, width), BF16),
             pltpu.VMEM((group, width), BF16),
-            pltpu.VMEM((2, 2, 2, rows, width), BF16),
+            pltpu.VMEM((2, 4, 2, rows, width), BF16),
+            pltpu.VMEM((2, 2, rows, width), BF16),
             pltpu.VMEM((2, group, 128), F32),
             pltpu.VMEM((group, 128), F32),
+            pltpu.VMEM((experts // 2, 2 * rows), F32),
             DMA((3,)),
             DMA((2, 2)),
             DMA((2, 5)),
-            DMA((2, 2)),
+            DMA((2,)),
         ],
         compiler_params=pltpu.CompilerParams(
-            collective_id=2, has_side_effects=True, vmem_limit_bytes=60 << 20
+            collective_id=2, has_side_effects=True, vmem_limit_bytes=67_000_000
         ),
         name="experts",
-    )(hidden_two, cotangent, select, spread, named.astype(F32), router.T, gate, up, down)
-
-
-def experts_by_xla(hidden_two, cotangent, routes_all, router, gate, up, down, capacity, me, experts):
+    )(hidden_two, cotangent_all, own_weights, select, spread, gate, up, down)
+
+
+def experts_by_xla(
+    hidden_two, cotangent, own_weights, routes_all, gate, up, down, capacity, me, experts
+):
     rows = hidden_two.shape[0]
     hidden_all = lax.all_gather(hidden_two, ALL, axis=0, tiled=True)
-    logits = dot(hidden_all, router)
+    gathered = lax.all_gather(own_weights, ALL)
     expert_ids = jnp.arange(experts, dtype=jnp.int32)
-    picked = jnp.any(routes_all[:, :, None] == expert_ids, axis=1)
-    masked = jnp.where(picked, logits, masked_score)
-    exponent = jnp.where(picked, jnp.exp(masked - jnp.max(masked, axis=1, keepdims=True)), 0.0)
-    weights_all = exponent / jnp.sum(exponent, axis=1, keepdims=True)
+    weights_all = gathered.transpose(0, 2, 1).reshape(experts * rows, experts)
     mine = jnp.any(routes_all == me, axis=1).reshape(experts, rows)
     weight_mine = jnp.sum(jnp.where(expert_ids == me, weights_all, 0.0), axis=1).reshape(
         experts, rows
@@ -1014,16 +1162,17 @@
     grad_weight_mine = jnp.sum(jnp.where(select, grad_weight_slot[:, :, None], 0.0), axis=1)
     out_rows = (slot_weight * expert_out).astype(BF16)
 
-    def placed_out(after):
-        return place(lax.optimization_barrier((out_rows, after))[0])
-
+    placed = place(grad_rows_in).reshape(experts, rows, D)
+    grad_weight, grad_rows_sum = exchange(
+        "sum_rows", 3, [("gather", "all", grad_weight_mine), ("reduce", "all", placed)]
+    )
+    placed_out = place(lax.optimization_barrier((out_rows, grad_rows_sum))[0])
     return (
         own_columns,
-        cotangent_all,
-        place(grad_rows_in),
         placed_out,
-        weights_all.T,
-        grad_weight_mine,
+        grad_weight,
+        gathered,
+        grad_rows_sum,
         expert_rows,
         grad_slots,
         expert_hidden,
@@ -1123,47 +1272,44 @@
     mixed_heads, log_total = attend(query_rot, key_rot, value_proj, allowed, score_scale)
     mixed_low = mixed_heads.reshape(lines * rows, Q_COLS).astype(BF16)
     projected = dot(mixed_low, weight_o).astype(BF16).reshape(lines, rows, D)
-    (projected,) = exchange("sum_residual", 1, [("reduce", "line", projected)])
+    jobs = [("reduce", "line", projected)]
+    if not large:
+        jobs.append(("gather", "all", cotangent))
+    projected, *cotangent_all = exchange("sum_residual", 1, jobs)
+    cotangent_all = None if large else cotangent_all[0]
     own_inputs = tokens.astype(F32)
     residual = own_inputs + projected
     ffn_scale = rms_scale(residual)
     ffn_normed = residual * ffn_scale
     hidden_two = (ffn_normed * gain_ffn).astype(BF16)
 
-    given = (hidden_two, cotangent, routes_all, router, gate_weight[0], up_weight[0], down_weight[0])
+    expert_ids = jnp.arange(experts, dtype=jnp.int32)
+    named = jnp.any(routes[:, :, None] == expert_ids, axis=1).T
+    logits = lax.dot_general(
+        router, hidden_two, (((0,), (1,)), ((), ())), preferred_element_type=F32
+    )
+    masked = jnp.where(named, logits, masked_score)
+    exponent = jnp.where(named, jnp.exp(masked - jnp.max(masked, axis=0, keepdims=True)), 0.0)
+    own_weights = exponent / jnp.sum(exponent, axis=0, keepdims=True)
+    weights = (gate_weight[0], up_weight[0], down_weight[0])
     if large:
-        done = experts_by_xla(*given, capacity, me, experts)
+        done = experts_by_xla(
+            hidden_two, cotangent, own_weights, routes_all, *weights, capacity, me, experts
+        )
     else:
-        done = experts_call(*given, capacity)
-    hidden_all, _, placed, placed_out, weights_all, grad_weight_mine = done[:6]
-    expert_rows, grad_slots, expert_hidden, grad_gate_act, grad_up_act = [
-        v.reshape(-1, v.shape[-1]) for v in done[6:]
-    ]
+        done = experts_call(
+            hidden_two, cotangent_all, own_weights, routes_all, *weights, capacity
+        )
+    hidden_all, placed_out, grad_weight, weights_all, grad_rows_sum = done[:5]
+    weights_all = weights_all.reshape(experts, experts, rows).transpose(1, 0, 2)
+    weights_all = weights_all.reshape(experts, experts * rows)
+    kept = [v.reshape(-1, v.shape[-1]) for v in done[5:]]
     if large:
         own_columns = hidden_all
     else:
         hidden_all = hidden_all.reshape(experts * rows, D)
         own_columns = lax.dynamic_slice_in_dim(hidden_all, me * own_rows, own_rows, axis=1)
-    grad_weight, grad_rows_sum = exchange(
-        "sum_rows",
-        3,
-        [
-            ("gather", "all", grad_weight_mine.reshape(experts, rows)),
-            ("reduce", "all", placed.reshape(lines, -1, 2, rows, D)),
-        ],
-    )
     grad_weight = grad_weight.reshape(experts, experts * rows)
-    if large:
-        placed_out = placed_out(grad_rows_sum)
-    else:
-        placed_out, grad_rows_sum = lax.optimization_barrier((placed_out, grad_rows_sum))
-    out_sum = lax.psum_scatter(
-        placed_out.reshape(experts * rows, D), ALL, scatter_dimension=0, tiled=True
-    )
-    block_out = (residual + out_sum.astype(F32)).astype(BF16)
-    grad_down = dot(expert_hidden.T, grad_slots)
-    grad_gate = dot(expert_rows.T, grad_gate_act)
-    grad_up = dot(expert_rows.T, grad_up_act)
 
     grad_logits = weights_all * (
         grad_weight - jnp.sum(weights_all * grad_weight, axis=0, keepdims=True)
@@ -1178,9 +1324,16 @@
     grad_hidden_two = dot(own_grad_logits, router.T) + grad_rows_sum.astype(F32)
     grad_gain_ffn = jnp.sum(grad_hidden_two * ffn_normed, axis=0)
     grad_residual = grad_out + norm_back(grad_hidden_two * gain_ffn, ffn_normed, ffn_scale)
-    (grad_attn,) = exchange(
-        "gather_grad", 4, [("gather", "line", grad_residual.astype(BF16))]
-    )
+    grad_attn, out_sum, (grad_gate, grad_up, grad_down) = exchange(
+        "gather_grad",
+        4,
+        [
+            ("gather", "line", grad_residual.astype(BF16)),
+            ("reduce", "all", placed_out.reshape(lines, -1, 2, rows, D)),
+            ("products", "", kept),
+        ],
+    )
+    block_out = (residual + out_sum).astype(BF16)
     grad_attn = grad_attn.reshape(lines * rows, D)
     output_part = dot(mixed_low.T, grad_attn).astype(BF16)
     grad_mixed = dot(grad_attn, weight_o.T).astype(BF16).reshape(lines, rows, GROUPS, HEAD_DIM)

time: 749 us -> 661 us (0.88)
  Pallas kernels: 588 us -> 535 us
  matrix products: 62.2 us -> 37.7 us
  between operations: 15.1 us -> 2.3 us
    pallas_call x5 -> x4, Pallas kernels: 389 us -> 329 us  [exchange(): pl.pallas_call(body, out_shape=tuple(out_shapes), in_specs=in_specs, out_...]
    dot_general x10 -> x7, matrix products: 54.8 us -> 31.1 us  [dot(): return jnp.dot(left, right, preferred_element_type=F32)]
    unnamed x114 -> x150, local copies, waits for them, and re-layouts: 15.7 us -> 27 us
  transfers between devices with their start and end apart: 1 -> 0, of which waited for: 0 -> 0; matrix products, arithmetic and copies ran while one was open for 10% -> 0% of each run, Pallas kernels for 23% -> 0%
where the time goes in v4:
time: 661 us; the launch traced here: 655 us
  Pallas kernels  535 us (81%)
  local copies, waits for them, and re-layouts  42.7 us (6%)
  matrix products  37.7 us (6%)
  other arithmetic  37.1 us (6%)
    pallas_call x4, Pallas kernels, exchange(): pl.pallas_call(body, out_shape=tuple(out_shapes), in_specs=in_specs, out_...  329 us
    pallas_call x1, Pallas kernels, experts_call(): pl.pallas_call(functools.partial(experts_body, capacity), out_shape=(all_...  206 us
    dot_general x7, matrix products, dot(): return jnp.dot(left, right, preferred_element_type=F32)  31.1 us
    unnamed x150, local copies, waits for them, and re-layouts  27 us

profile of v4, /device:TPU:0, one launch (start us, length us, event | category | flops | bytes accessed | tf_op | source)
XLA Modules:
  0.0 654.8 jit_solution(5846408260591361238)
XLA Ops:
  5.2 65.7 %gather_inputs.1 = (bf16[4,4,2,32,128]{4,3,2,1,0:T(8,128)(2,1)}, s32[4,4,2,16,128]{4,3,2,1,0:T(8,128)}, bf16[4,4,2,64,1280]{4,3,2,1,0:T(8,128)(2,1)}, bf16[4,128...) custom-call(bf16[32,128]{1,0:T(8,128)(2,1)} %fusion.59.refs_0_, s32[16,128]{1,0:T(8,128)} %pad_bitcast_fusion.refs_1_, ...), custom_call_target="tpu_custom_call" | custom-call | tf_op jit(solution)/shard_map/gather_inputs/pallas_call | solution.py:712
  73.9 2.2 multiply_reduce_fusion.1
  77.3 2.9 fusion.81
  81.4 2.0 fusion.41
  90.7 6.2 convolution_convert_fusion.2
  96.9 91.5 %sum_residual.1 = (f32[128,2048]{1,0:T(8,128)}, bf16[4,4,2,128,2048]{4,3,2,1,0:T(8,128)(2,1)}) custom-call(bf16[4,128,2048]{2,1,0:T(8,128)(2,1)} %bitcast.264, bf16[128,2048]{1,0:T(8,128)(2,1)} %refs_1_.1), custom_call_target="tpu_custom_call" | custom-call | tf_op jit(solution)/shard_map/sum_residual/pallas_call | solution.py:712
  188.4 2.1 multiply_reduce_fusion.6
  198.1 205.7 %experts.1 = (bf16[4,4,2,128,2048]{4,3,2,1,0:T(8,128)(2,1)}, bf16[4,4,2,128,2048]{4,3,2,1,0:T(8,128)(2,1)}, f32[4,4,2,16,256]{4,3,2,1,0:T(8,128)}, f32[4,4,2,32,...) custom-call(bf16[128,2048]{1,0:T(8,128)(2,1)} %copy-done.19, ...), custom_call_target="tpu_custom_call" | custom-call | tf_op jit(solution)/shard_map/experts/pallas_call | solution.py:1051
  407.3 2.3 fusion.26
  409.6 1.8 multiply_reduce_fusion.4
  413.6 100.8 %gather_grad.1 = (bf16[4,128,2048]{2,1,0:T(8,128)(2,1)}, f32[128,2048]{1,0:T(8,128)}, f32[2048,768]{1,0:T(8,128)}, f32[2048,768]{1,0:T(8,128)}, f32[768,2048]{1,0:T(8,128)}) custom-call(bf16[128,2048]{1,0:T(8,128)(2,1)} %fusion.75.refs_0_, bf16[4,4,2,128,2048]{4,3,2,1,0:T(8,128)(2,1)} %get-tuple-element.47.refs_1_, bf16[1536,2048]{1,0:T(8,128)(2,1)} %bitcast.244, ...), custom_call_target="tpu_custom_call" | custom-call | tf_op jit(solution)/shard_map/gather_grad/pallas_call | solution.py:712
  514.5 6.5 convolution_convert_fusion.1
  520.9 2.4 fusion.12
  535.0 2.5 multiply_reduce_fusion.2
  537.7 2.0 mul.473
  539.7 2.5 copy.181
  543.9 4.2 fusion.2
  548.2 6.6 %fusion.76 = (bf16[512,2048]{1,0:T(8,128)(2,1)}, f32[2048]{0:T(1024)S(1)}, bf16[512,2048]{1,0:T(8,128)(2,1)S(1)}) fusion(f32[512]{0:T(512)S(1)} %copy-done.58, bf16[4,128,2048]{2,1,0:T(8,128)(2,1)S(1)} %copy-done.16, f32[2048]{0:T(1024)S(1)} %copy-done.42, bf16[2048,1280]{1,0:T(8,128)(2,1)} %bitcast.297, bf16[512,128]{1,0:T(8,128)(2,1)S(1)} %bitcast.287, ...), kind=kOutput, calls=%fused_computation.186 | convolution fusion | flops 2695624704 | bytes 12863488 | tf_op jit(solution)/shard_map/dot_general | solution.py:33
  554.8 4.6 convolution_convert_fusion
  560.1 71.3 %sum_gradients.1 = (f32[4,4,2,48,128]{4,3,2,1,0:T(8,128)}, f32[128,2048]{1,0:T(8,128)}, bf16[4,64,1280]{2,1,0:T(8,128)(2,1)}, f32[128,2048]{1,0:T(8,128)}) custom-call(f32[48,128]{1,0:T(8,128)} %fusion.51.refs_0_, bf16[4,128,2048]{2,1,0:T(8,128)(2,1)} %bitcast.263, bf16[4,4,2,64,1280]{4,3,2,1,0:T(8,128)(2,1)} %bitcast.251, bf16[4,2,128,2048]{3,2,1,0:T(8,128)(2,1)} %bitcast.252), custom_call_target="tpu_custom_call" | custom-call | tf_op jit(solution)/shard_map/sum_gradients/pallas_call | solution.py:712
  635.6 1.7 fusion.21
  639.5 6.1 copy.274
  645.5 6.0 copy.275
  651.6 2.7 copy.276
  (236 shorter events, 50.1 us)
Async XLA Ops:
  0.7 3.1 copy-start.60
  0.7 3.7 copy-start.55
  0.7 3.9 copy-start.61
  70.9 5.9 copy-start.15
  72.5 8.9 %copy-start.45 = (f32[4,128]{1,0:T(4,128)}, f32[4,128]{1,0:T(4,128)S(1)}, u32[]{:S(2)}) copy-start(f32[4,128]{1,0:T(4,128)S(1)} %get-tuple-element.104) | copy-start | bytes 6148
  73.8 3.5 copy-start.37
  73.9 3.4 copy-start.41
  73.9 3.4 copy-start.62
  80.3 3.4 copy-start.6
  81.2 3.7 copy-start.53
  90.6 6.2 copy-start.33
  96.9 91.5 %copy-start.13 = (bf16[128,2048]{1,0:T(8,128)(2,1)S(1)}, bf16[128,2048]{1,0:T(8,128)(2,1)}, u32[]{:S(2)}) copy-start(bf16[128,2048]{1,0:T(8,128)(2,1)} %refs_3_.1) | copy-start | bytes 1572868
  188.4 3.2 copy-start.38
  190.5 3.9 copy-start.49
  191.6 5.3 copy-start.19
  192.0 6.0 copy-start.21
  514.4 6.5 copy-start.63
  514.5 6.5 copy-start.64
  543.9 4.2 copy-start.16
  543.9 4.2 copy-start.42
  543.9 4.2 copy-start.58
  631.4 3.8 copy-start.59
  639.5 12.1 %slice-start = ((s8[6291456]{0:T(1024)(128)(4,1)}), s8[4194304]{0:T(1024)(128)(4,1)S(1)}, s32[]{:S(2)}) async-start(s8[6291456]{0:T(1024)(128)(4,1)} %bitcast.246), calls=%async_computation | async-start | bytes 8388608
  645.5 6.0 slice-start.1
  (43 other events, 84.5 us)

commit v5 on v4

--- a/solution.py
+++ b/solution.py
@@ -414,17 +414,23 @@
     def received(piece, sem):
         send(piece, piece, ps.at[0, 0], sem, here).wait_recv()
 
+    def start_one(zz, k):
+        share(zz, k).start()
+
+    def first_one(zz, k):
+        received(pair.at[zz, k], pr.at[zz, k])
+        add_into(pair.at[zz, k], pair.at[zz, k], term(zz, k, c))
+        if k == 3:
+            cross(zz, 0).start()
+            cross(zz, 1).start()
+
     def start(zz, way):
         for k in (3, 1, 2, 0):
-            share(zz, k).start()
+            start_one(zz, k)
 
     def first(zz, way):
         for k in (3, 1, 2):
-            received(pair.at[zz, k], pr.at[zz, k])
-            add_into(pair.at[zz, k], pair.at[zz, k], term(zz, k, c))
-            if k == 3:
-                cross(zz, 0).start()
-                cross(zz, 1).start()
+            first_one(zz, k)
 
     def second(zz, way):
         received(crossed.at[zz, 0], pr.at[zz, 4])
@@ -475,6 +481,8 @@
     return {
         "start": start,
         "first": first,
+        "start one": start_one,
+        "first one": first_one,
         "second": second,
         "third": third,
         "sent": sent,
@@ -580,8 +588,8 @@
     return [
         pltpu.VMEM((3, count, ff), BF16),
         pltpu.VMEM((2, count, 256), BF16),
-        pltpu.VMEM((2, 2, 256, ff), F32),
-        pltpu.VMEM((2, ff, 256), F32),
+        pltpu.VMEM((2, 2, 256, ff), BF16),
+        pltpu.VMEM((2, ff, 256), BF16),
         DMA((3,)),
         DMA((2,)),
         DMA((2, 2)),
@@ -630,10 +638,10 @@
                 copy.wait()
         q = n % 2
         if n < half:
-            wide[q, 0] = dot_tn(tile[q], near[1])
-            wide[q, 1] = dot_tn(tile[q], near[2])
+            wide[q, 0] = dot_tn(tile[q], near[1]).astype(BF16)
+            wide[q, 1] = dot_tn(tile[q], near[2]).astype(BF16)
         else:
-            tall[q] = dot_tn(near[0], tile[q])
+            tall[q] = dot_tn(near[0], tile[q]).astype(BF16)
         for copy in store(n):
             copy.start()
         if n % 3 == 2:
@@ -665,8 +673,8 @@
             width, ff = x[0].shape[1], x[2].shape[1]
             args += x
             in_specs += [far] * 5
-            out_shapes += [jax.ShapeDtypeStruct((width, ff), F32)] * 2
-            out_shapes.append(jax.ShapeDtypeStruct((ff, width), F32))
+            out_shapes += [jax.ShapeDtypeStruct((width, ff), BF16)] * 2
+            out_shapes.append(jax.ShapeDtypeStruct((ff, width), BF16))
             out_specs += [far] * 3
             own = products_scratch(x[0].shape[0], width, ff)
             counts.append((5, 3, len(own)))
@@ -789,9 +797,9 @@
 
     steps_r = reduce_parts(spot, "all", term, sum_ref, sum_scratch)
 
-    def sums(name, i):
+    def sums(name, i, k=1):
         turn[0] = i
-        steps_r[name](pick_order(z, i), 1)
+        steps_r[name](pick_order(z, i), k)
 
     def comm_dw(name, d):
         spot.each(d, steps_dw[name])
@@ -808,25 +816,28 @@
                 part, d = name.split()
                 spot.each(int(d), s[part])
 
-    def load(i, k, n):
+    def load(n):
+        i, k = n // 4, n % 4
         zz, bb = pick_order(z, i), columns[k]
         return [
-            pltpu.make_async_copy(hall.at[zz, bb], hb.at[n % 2], l_sem.at[0, n % 2]),
-            pltpu.make_async_copy(tall.at[zz, bb], tb.at[n % 2], l_sem.at[1, n % 2]),
+            pltpu.make_async_copy(hall.at[zz, bb], hb.at[n % 3], l_sem.at[0, n % 3]),
+            pltpu.make_async_copy(tall.at[zz, bb], tb.at[n % 3], l_sem.at[1, n % 3]),
         ]
 
-    def fetch(i, k, n):
+    def fetch(n):
+        i, k = n // 4, n % 4
         zz = pick_order(z, i)
         for s in both:
             s["shared"](zz, k)
-        for copy in load(i, k, n):
+        for copy in load(n):
             copy.start()
 
-    def pick(i, k, n):
+    def pick(n):
+        i, k = n // 4, n % 4
         zz, bb = pick_order(z, i), columns[k]
         at = pl.ds(pl.multiple_of(bb * pair, 16), pair)
         which = zz * 4 + bb
-        for copy in load(i, k, n):
+        for copy in load(n):
             copy.wait()
         rows = hb.shape[2]
         width = hb.shape[3]
@@ -840,8 +851,8 @@
         @pl.loop(0, width // 512)
         def _(j):
             part = pl.ds(pl.multiple_of(j * 512, 512), 512)
-            h = hb[n % 2, :, :, part].reshape(2 * rows, 512)
-            t = tb[n % 2, :, :, part].reshape(2 * rows, 512)
+            h = hb[n % 3, :, :, part].reshape(2 * rows, 512)
+            t = tb[n % 3, :, :, part].reshape(2 * rows, 512)
             xs[i % 2, at, part] = jnp.dot(select, h, preferred_element_type=F32).astype(BF16)
             t = jnp.dot(select, t, preferred_element_type=F32)
             zs[i % 2, at, part] = t.astype(BF16)
@@ -918,8 +929,19 @@
         put(zz, bb, m).start()
 
     def places(i):
-        for n, k in enumerate((3, 1, 2, 0)):
+        order = (3, 1, 2, 0)
+        for n, k in enumerate(order):
             place(i, k, 4 * i + n)
+            if n >= 1:
+                sums("start one", i, order[n - 1])
+            if n >= 2:
+                sums("first one", i, order[n - 2])
+        sums("start one", i, 0)
+        sums("first one", i, 2)
+
+    def kept(i):
+        for copy in keep(i):
+            copy.wait()
 
     for s in both:
         s["start"]()
@@ -927,98 +949,90 @@
         copy.start()
     for s in both:
         s["end"]()
-    fetch(0, 0, 0)
+    fetch(0)
     comm("line 1", "plane 0")
-    fetch(0, 1, 1)
-    pick(0, 0, 0)
-    fetch(0, 2, 2)
-    pick(0, 1, 1)
-    comm("line 2", "plane 1", "cross 0")
-    fetch(1, 0, 3)
-    pick(0, 2, 2)
-    fetch(0, 3, 4)
-    pick(1, 0, 3)
+    fetch(1)
+    fetch(2)
+    pick(0)
+    pick(1)
+    comm("cross 0")
+    fetch(3)
+    pick(2)
+    comm("line 2")
+    fetch(4)
+    pick(3)
     for copy in loads:
         copy.wait()
-    fetch(1, 1, 5)
-    pick(0, 3, 4)
     inner(0)
-    comm("line 3", "plane 2", "cross 1")
-    fetch(1, 2, 6)
-    pick(1, 1, 5)
+    comm("plane 1")
+    fetch(5)
+    fetch(6)
+    pick(4)
     outer(0)
-    fetch(1, 3, 7)
-    pick(1, 2, 6)
+    pick(5)
+    pick(6)
+    comm("line 3", "cross 1")
+    fetch(7)
     places(0)
+    pick(7)
+    inner(1)
+    kept(0)
+    comm("plane 2")
+    fetch(8)
+    fetch(9)
+    fetch(10)
+    pick(8)
+    pick(9)
+    pick(10)
+    sums("second", 0)
+    outer(1)
+    comm("cross 2")
+    fetch(11)
+    places(1)
+    sums("third", 0)
     comm("plane 3")
-    pick(1, 3, 7)
-    sums("start", 0)
-    inner(1)
-    for copy in keep(0):
-        copy.wait()
-    fetch(2, 0, 8)
-    comm("cross 2")
-    fetch(2, 1, 9)
-    pick(2, 0, 8)
-    sums("first", 0)
-    outer(1)
-    fetch(2, 2, 10)
-    pick(2, 1, 9)
-    sums("second", 0)
-    places(1)
+    fetch(12)
+    fetch(13)
+    pick(11)
+    inner(2)
+    kept(1)
+    sums("second", 1)
+    fetch(14)
+    pick(12)
+    pick(13)
+    pick(14)
+    outer(2)
     comm("cross 3")
-    fetch(2, 3, 11)
-    pick(2, 2, 10)
-    sums("start", 1)
-    fetch(3, 0, 12)
-    pick(2, 3, 11)
-    inner(2)
-    for copy in keep(1):
-        copy.wait()
-    sums("third", 0)
-    fetch(3, 1, 13)
-    pick(3, 0, 12)
-    sums("first", 1)
-    outer(2)
-    fetch(3, 2, 14)
-    pick(3, 1, 13)
-    sums("second", 1)
+    fetch(15)
     sums("sent", 0)
     places(2)
-    fetch(3, 3, 15)
-    pick(3, 2, 14)
-    sums("start", 2)
-    pick(3, 3, 15)
     sums("third", 1)
+    pick(15)
     inner(3)
-    sums("first", 2)
+    sums("second", 2)
     outer(3)
-    sums("second", 2)
     sums("sent", 1)
     places(3)
     steps_dw["start"]()
-    sums("start", 3)
     sums("third", 2)
+    sums("second", 3)
     comm_dw("line", 1)
     comm_dw("plane", 0)
-    sums("first", 3)
     comm_dw("line", 2)
     comm_dw("plane", 1)
     comm_dw("cross", 0)
-    sums("second", 3)
     comm_dw("line", 3)
     comm_dw("plane", 2)
     comm_dw("cross", 1)
+    sums("third", 3)
     comm_dw("plane", 3)
     comm_dw("cross", 2)
     comm_dw("cross", 3)
-    sums("third", 3)
     steps_r["end"]()
     for m in (0, 1):
         put(z, b, m).wait()
     for i in (2, 3):
-        for copy in keep(i):
-            copy.wait()
+        kept(i)
         sums("sent", i)
     for d in range(lines):
         comm(f"drain {d}")
@@ -1072,8 +1086,8 @@
             pltpu.VMEM((width, ff), BF16),
             pltpu.VMEM((width, ff), BF16),
             pltpu.VMEM((ff, width), BF16),
-            pltpu.VMEM((2, 2, rows, width), BF16),
-            pltpu.VMEM((2, 2, rows, width), BF16),
+            pltpu.VMEM((3, 2, rows, width), BF16),
+            pltpu.VMEM((3, 2, rows, width), BF16),
             pltpu.VMEM((2, group, width), BF16),
             pltpu.VMEM((2, group, width), BF16),
             pltpu.VMEM((2, group, width), BF16),
@@ -1088,7 +1102,7 @@
             pltpu.VMEM((group, 128), F32),
             pltpu.VMEM((experts // 2, 2 * rows), F32),
             DMA((3,)),
-            DMA((2, 2)),
+            DMA((2, 3)),
             DMA((2, 5)),
             DMA((2,)),
         ],
@@ -1274,8 +1288,8 @@
     projected = dot(mixed_low, weight_o).astype(BF16).reshape(lines, rows, D)
     jobs = [("reduce", "line", projected)]
     if not large:
-        jobs.append(("gather", "all", cotangent))
-    projected, *cotangent_all = exchange("sum_residual", 1, jobs)
+        jobs.insert(0, ("gather", "all", cotangent))
+    *cotangent_all, projected = exchange("sum_residual", 1, jobs)
     cotangent_all = None if large else cotangent_all[0]
     own_inputs = tokens.astype(F32)
     residual = own_inputs + projected
@@ -1391,9 +1405,9 @@
         output_grad,
         router_grad,
         gains_grad,
-        grad_gate[None],
-        grad_up[None],
-        grad_down[None],
+        grad_gate[None].astype(F32),
+        grad_up[None].astype(F32),
+        grad_down[None].astype(F32),
     )
 
 

time: 661 us -> 663 us (level)
  other arithmetic: 37.1 us -> 52.3 us
  Pallas kernels: 535 us -> 524 us
    pallas_call x4, Pallas kernels: 329 us -> 318 us  [exchange(): pl.pallas_call(body, out_shape=tuple(out_shapes), in_specs=in_specs, out_...]
    unnamed x150 -> x145, local copies, waits for them, and re-layouts: 27 us -> 16.7 us
    convert_element_type x0 -> x3, other arithmetic: none -> 9.93 us  [the longest x1 3.55 us: on_device(): grad_down[None].astype(F32)]
where the time goes in v5:
time: 663 us; the launch traced here: 656 us
  Pallas kernels  524 us (79%)
  other arithmetic  52.3 us (8%)
  matrix products  41.2 us (6%)
  local copies, waits for them, and re-layouts  36.1 us (5%)
    pallas_call x4, Pallas kernels, exchange(): pl.pallas_call(body, out_shape=tuple(out_shapes), in_specs=in_specs, out_...  318 us
    pallas_call x1, Pallas kernels, experts_call(): pl.pallas_call(functools.partial(experts_body, capacity), out_shape=(all_...  205 us
    dot_general x7, matrix products, dot(): return jnp.dot(left, right, preferred_element_type=F32)  34.7 us
    unnamed x145, local copies, waits for them, and re-layouts  16.7 us

profile of v5, /device:TPU:0, one launch (start us, length us, event | category | flops | bytes accessed | tf_op | source)
XLA Modules:
  0.0 655.5 jit_solution(714272077393046391)
XLA Ops:
  7.8 65.7 %gather_inputs.1 = (bf16[4,4,2,32,128]{4,3,2,1,0:T(8,128)(2,1)}, s32[4,4,2,16,128]{4,3,2,1,0:T(8,128)}, bf16[4,4,2,64,1280]{4,3,2,1,0:T(8,128)(2,1)}, bf16[4,128...) custom-call(bf16[32,128]{1,0:T(8,128)(2,1)} %fusion.59.refs_0_, s32[16,128]{1,0:T(8,128)} %pad_bitcast_fusion.refs_1_, ...), custom_call_target="tpu_custom_call" | custom-call | tf_op jit(solution)/shard_map/gather_inputs/pallas_call | solution.py:720
  78.1 5.4 fusion.81
  86.5 2.1 fusion.9
  96.4 6.2 convolution_convert_fusion.2
  102.6 79.5 %sum_residual.1 = (bf16[4,4,2,128,2048]{4,3,2,1,0:T(8,128)(2,1)}, f32[128,2048]{1,0:T(8,128)}) custom-call(bf16[128,2048]{1,0:T(8,128)(2,1)} %refs_0_.1, bf16[4,128,2048]{2,1,0:T(8,128)(2,1)} %bitcast.265), custom_call_target="tpu_custom_call" | custom-call | tf_op jit(solution)/shard_map/sum_residual/pallas_call | solution.py:720
  191.7 205.4 %experts.1 = (bf16[4,4,2,128,2048]{4,3,2,1,0:T(8,128)(2,1)}, bf16[4,4,2,128,2048]{4,3,2,1,0:T(8,128)(2,1)}, f32[4,4,2,16,256]{4,3,2,1,0:T(8,128)}, f32[4,4,2,32,...) custom-call(bf16[128,2048]{1,0:T(8,128)(2,1)} %copy-done.22, ...), custom_call_target="tpu_custom_call" | custom-call | tf_op jit(solution)/shard_map/experts/pallas_call | solution.py:1065
  397.1 2.2 copy.175
  399.4 2.3 copy.222
  407.6 97.8 %gather_grad.1 = (bf16[4,128,2048]{2,1,0:T(8,128)(2,1)}, f32[128,2048]{1,0:T(8,128)}, bf16[2048,768]{1,0:T(8,128)(2,1)}, bf16[2048,768]{1,0:T(8,128)(2,1)}, bf16[768,2048]{1,0:T(8,128)(2,1)}) custom-call(bf16[128,2048]{1,0:T(8,128)(2,1)} %fusion.75.refs_0_, bf16[4,4,2,128,2048]{4,3,2,1,0:T(8,128)(2,1)} %get-tuple-element.47.refs_1_, ...), custom_call_target="tpu_custom_call" | custom-call | tf_op jit(solution)/shard_map/gather_grad/pallas_call | solution.py:720
  505.4 5.2 fusion.12
  520.6 2.5 multiply_reduce_fusion.2
  524.0 3.0 mul.473
  527.0 2.5 copy.181
  532.1 4.1 fusion.2
  538.5 6.6 %fusion.76 = (bf16[512,2048]{1,0:T(8,128)(2,1)}, f32[2048]{0:T(1024)S(1)}, bf16[512,2048]{1,0:T(8,128)(2,1)S(1)}) fusion(f32[512]{0:T(512)S(1)} %copy-done.63, bf16[4,128,2048]{2,1,0:T(8,128)(2,1)S(1)} %copy-done.19, f32[2048]{0:T(1024)S(1)} %copy-done.50, bf16[2048,1280]{1,0:T(8,128)(2,1)} %bitcast.299, bf16[512,128]{1,0:T(8,128)(2,1)S(1)} %bitcast.288, ...), kind=kOutput, calls=%fused_computation.189 | convolution fusion | flops 2695624704 | bytes 12863488 | tf_op jit(solution)/shard_map/dot_general | solution.py:33
  545.7 4.9 convolution_convert_fusion
  550.6 4.4 convolution_convert_fusion.1
  555.0 75.5 %sum_gradients.1 = (f32[4,4,2,48,128]{4,3,2,1,0:T(8,128)}, f32[128,2048]{1,0:T(8,128)}, bf16[4,64,1280]{2,1,0:T(8,128)(2,1)}, f32[128,2048]{1,0:T(8,128)}) custom-call(f32[48,128]{1,0:T(8,128)} %fusion.51.refs_0_, bf16[4,128,2048]{2,1,0:T(8,128)(2,1)} %bitcast.264, bf16[4,4,2,64,1280]{4,3,2,1,0:T(8,128)(2,1)} %bitcast.252, bf16[4,2,128,2048]{3,2,1,0:T(8,128)(2,1)} %bitcast.253), custom_call_target="tpu_custom_call" | custom-call | tf_op jit(solution)/shard_map/sum_gradients/pallas_call | solution.py:720
  632.2 3.4 fusion.21
  638.4 2.3 fusion.26
  640.7 2.3 copy.263
  644.4 3.2 bitcast_convert_fusion.2
  647.6 3.2 bitcast_convert_fusion.1
  650.8 3.6 bitcast_convert_fusion
  (233 shorter events, 60.2 us)
Async XLA Ops:
  73.5 4.1 copy-start.18
  74.9 11.7 %copy-start.59 = (f32[128]{0:T(128)}, f32[128]{0:T(128)S(1)}, u32[]{:S(2)}) copy-start(f32[128]{0:T(128)S(1)} %get-tuple-element.94) | copy-start | bytes 1540
  74.9 14.4 %copy-start.57 = (f32[128]{0:T(128)}, f32[128]{0:T(128)S(1)}, u32[]{:S(2)}) copy-start(f32[128]{0:T(128)S(1)} %get-tuple-element.93) | copy-start | bytes 1540
  96.3 6.2 copy-start.41
  102.6 79.5 %copy-start.16 = (bf16[128,2048]{1,0:T(8,128)(2,1)S(1)}, bf16[128,2048]{1,0:T(8,128)(2,1)}, u32[]{:S(2)}) copy-start(bf16[128,2048]{1,0:T(8,128)(2,1)} %refs_3_.1) | copy-start | bytes 1572868
  182.1 3.6 copy-start.54
  185.3 4.9 copy-start.22
  185.7 6.0 copy-start.24
  397.1 4.5 copy-start.34
  397.1 4.5 copy-start.33
  399.4 4.2 copy-start.5
  399.4 4.2 copy-start.25
  399.4 4.2 copy-start.56
  403.5 4.1 copy-start.39
  505.4 5.5 copy-start.47
  514.7 3.6 copy-start.36
  514.7 3.6 copy-start.38
  532.1 4.2 copy-start.15
  545.7 4.9 copy-start.42
  545.7 4.9 copy-start.65
  555.0 75.5 %copy-start.64 = (f32[128]{0:T(128)S(1)}, f32[128]{0:T(128)}, u32[]{:S(2)}) copy-start(f32[128]{0:T(128)} %get-tuple-element.86) | copy-start | bytes 1540
  555.0 75.5 %copy-start.17 = (bf16[128,2048]{1,0:T(8,128)(2,1)S(1)}, bf16[128,2048]{1,0:T(8,128)(2,1)}, u32[]{:S(2)}) copy-start(bf16[128,2048]{1,0:T(8,128)(2,1)} %refs_3_.1) | copy-start | bytes 1572868
  637.0 7.4 %copy-start.28 = (bf16[2048,768]{1,0:T(8,128)(2,1)S(1)}, bf16[2048,768]{1,0:T(8,128)(2,1)}, u32[]{:S(2)}) copy-start(bf16[2048,768]{1,0:T(8,128)(2,1)} %get-tuple-element.60) | copy-start | bytes 9437188
  650.8 3.6 copy-start.43
  (42 other events, 80.1 us)

commit v6 on v5

--- a/solution.py
+++ b/solution.py
@@ -335,7 +335,7 @@
 
     parts["start"]()
     yield
-    for s in range(1, steps + 2):
+    for s in range(1, steps + 2 if planar else steps):
         if s < steps:
             each(s, parts["line"])
         if planar and 0 <= s - 1 < steps:
@@ -515,7 +515,7 @@
         for lag, name in enumerate(("first", "second", "third")):
             if 0 <= s - lag < steps:
                 each(order[s - lag], parts[name])
-        yield
+                yield
     parts["end"]()
     for d in range(steps):
         each(d, parts["sent"])
@@ -661,6 +661,73 @@
             except StopIteration:
                 live.remove(g)
 
+def backward_scratch(lines, rows, width):
+    return [
+        *gather_sems("line", lines),
+        pltpu.VMEM((Q_COLS, width), BF16),
+        pltpu.VMEM((lines, rows, width), BF16),
+        pltpu.VMEM((lines * rows, Q_COLS), BF16),
+        pltpu.VMEM((GROUPS * rows, HEAD_DIM), BF16),
+        pltpu.VMEM((GROUPS * rows, HEAD_DIM), BF16),
+        DMA((2,)),
+    ]
+
+
+def backward(spot, ins, outs, scratch):
+    (own_ref, wo_ref, q_ref, k_ref, v_ref, lse_ref, mask_ref, cos_ref, sin_ref, proj_ref, gain_ref) = ins
+    rows_ref, out_ref, gain_out = outs
+    wo, near, mixed, query, upstream, sem = scratch[-6:]
+    lines, rows = near.shape[:2]
+    score_scale = HEAD_DIM ** (-0.5)
+    bring = pltpu.make_async_copy(wo_ref, wo, sem.at[0])
+    bring.start()
+    gain_out[...] = jnp.zeros_like(gain_out)
+    yield from gather(spot, "line", own_ref, rows_ref, scratch[:-6])
+    load = pltpu.make_async_copy(rows_ref, near, sem.at[1])
+    load.start()
+    bring.wait()
+    load.wait()
+    for j in range(Q_COLS // 256):
+        part = pl.ds(j * 256, 256)
+        full = dot_nt(near[...].reshape(lines * rows, near.shape[2]), wo[part, :])
+        mixed[:, part] = full.astype(BF16)
+        if j % 2:
+            yield
+
+    def norm_part(i, grad, columns, which):
+        turned = grad * cos_ref[i] + pltpu.roll(grad, HEAD_DIM // 2, axis=1) * sin_ref[i]
+        x = proj_ref[i, :, columns]
+        scale = rms_scale(x)
+        normed = x * scale
+        at = pl.ds(which, 1)
+        gain_out[at, :] = gain_out[at, :] + jnp.sum(turned * normed, axis=0, keepdims=True)
+        up = turned * gain_ref[at, :]
+        out_ref[i, :, columns] = norm_back(up, normed, scale).astype(BF16)
+
+    for i in range(lines):
+        keys, values = k_ref[i], v_ref[i]
+        for h in range(GROUPS):
+            at, columns = pl.ds(h * rows, rows), pl.ds(h * HEAD_DIM, HEAD_DIM)
+            query[at, :] = q_ref[i, :, columns]
+            upstream[at, :] = mixed[pl.ds(i * rows, rows), columns]
+        scores = dot_nt(query[...], keys) * score_scale
+        allowed = jnp.concatenate([mask_ref[i]] * GROUPS, axis=0) > 0.5
+        probs = jnp.where(allowed, jnp.exp(scores - lse_ref[i]), 0.0)
+        grad_probs = dot_nt(upstream[...], values)
+        mean = jnp.sum(probs * grad_probs, axis=1, keepdims=True)
+        grad_scores = (probs * (grad_probs - mean)).astype(BF16)
+        grad_query = jnp.dot(grad_scores, keys, preferred_element_type=F32) * score_scale
+        grad_keys = dot_tn(grad_scores, query[...]) * score_scale
+        grad_values = dot_tn(probs.astype(BF16), upstream[...])
+        yield
+        for h in range(GROUPS):
+            part = grad_query[h * rows : (h + 1) * rows]
+            norm_part(i, part, pl.ds(h * HEAD_DIM, HEAD_DIM), 0)
+        norm_part(i, grad_keys, pl.ds(Q_COLS, HEAD_DIM), 1)
+        out_ref[i, :, pl.ds(Q_COLS + HEAD_DIM, HEAD_DIM)] = grad_values.astype(BF16)
+        yield
+
+
 def exchange(name, cid, jobs):
     lines = lax.axis_size("line")
     cells = lax.axis_size("plane") * lax.axis_size("core")
@@ -678,6 +745,18 @@
             out_specs += [far] * 3
             own = products_scratch(x[0].shape[0], width, ff)
             counts.append((5, 3, len(own)))
+            scratch += own
+            continue
+        if kind == "backward":
+            rows, width = x[0].shape
+            args += x
+            in_specs += [far] * 2 + [near] * 9
+            out_shapes.append(jax.ShapeDtypeStruct((lines, rows, width), BF16))
+            out_shapes.append(jax.ShapeDtypeStruct((lines, rows, x[9].shape[2]), BF16))
+            out_shapes.append(jax.ShapeDtypeStruct((8, HEAD_DIM), F32))
+            out_specs += [far, near, near]
+            own = backward_scratch(lines, rows, width)
+            counts.append((11, 3, len(own)))
             scratch += own
             continue
         rows, cols = x.shape[-2:]
@@ -709,6 +788,8 @@
             ins, outs, rest = ins + n_in, outs + n_out, rest + n_rest
             if kind == "products":
                 makers.append(products(i, o, w))
+            elif kind == "backward":
+                makers.append(backward(spot, i, o, w))
             elif kind == "gather":
                 makers.append(gather(spot, mode, i[0], o[0], w))
             elif mode == "line":
@@ -724,7 +805,7 @@
         out_specs=tuple(out_specs),
         scratch_shapes=scratch,
         compiler_params=pltpu.CompilerParams(
-            collective_id=cid, has_side_effects=True, vmem_limit_bytes=62 << 20
+            collective_id=cid, has_side_effects=True, vmem_limit_bytes=67_000_000
         ),
         name=name,
     )(*args)
@@ -1338,39 +1419,57 @@
     grad_hidden_two = dot(own_grad_logits, router.T) + grad_rows_sum.astype(F32)
     grad_gain_ffn = jnp.sum(grad_hidden_two * ffn_normed, axis=0)
     grad_residual = grad_out + norm_back(grad_hidden_two * gain_ffn, ffn_normed, ffn_scale)
-    grad_attn, out_sum, (grad_gate, grad_up, grad_down) = exchange(
-        "gather_grad",
-        4,
-        [
-            ("gather", "line", grad_residual.astype(BF16)),
-            ("reduce", "all", placed_out.reshape(lines, -1, 2, rows, D)),
-            ("products", "", kept),
-        ],
-    )
+    grad_low = grad_residual.astype(BF16)
+    jobs = [
+        ("reduce", "all", placed_out.reshape(lines, -1, 2, rows, D)),
+        ("products", "", kept),
+    ]
+    if large:
+        jobs.insert(0, ("gather", "line", grad_low))
+    else:
+        turn_back = [jnp.concatenate([v, w], axis=-1) for v, w in ((cosine, cosine), (sine_table, -sine_table))]
+        given = (
+            grad_low,
+            weight_o,
+            query_rot.reshape(lines, rows, Q_COLS),
+            key_rot,
+            value_proj,
+            log_total.reshape(lines, GROUPS * rows, 1),
+            allowed.astype(F32),
+            *turn_back,
+            proj.reshape(lines, rows, width),
+            jnp.pad(gains[2 * D :].reshape(2, HEAD_DIM), ((0, 6), (0, 0))),
+        )
+        jobs.insert(0, ("backward", "", given))
+    came, out_sum, (grad_gate, grad_up, grad_down) = exchange("gather_grad", 4, jobs)
     block_out = (residual + out_sum).astype(BF16)
-    grad_attn = grad_attn.reshape(lines * rows, D)
+    grad_attn = (came if large else came[0]).reshape(lines * rows, D)
     output_part = dot(mixed_low.T, grad_attn).astype(BF16)
-    grad_mixed = dot(grad_attn, weight_o.T).astype(BF16).reshape(lines, rows, GROUPS, HEAD_DIM)
-    grad_query_rot, grad_key_rot, grad_value_rot = attend_back(
-        query_rot, key_rot, value_proj, allowed, score_scale, log_total, grad_mixed
-    )
-    grad_value_proj = grad_value_rot.astype(BF16)
-    grad_query_gained = rotate(grad_query_rot, cosine[:, :, None], -sine_table[:, :, None])
-    grad_gain_query = jnp.sum(grad_query_gained * query_normed, axis=(0, 1, 2))
-    grad_query_proj = norm_back(grad_query_gained * gain_query, query_normed, query_scale).astype(
-        BF16
-    )
-    grad_key_gained = rotate(grad_key_rot, cosine, -sine_table)
-    grad_gain_key = jnp.sum(grad_key_gained * key_normed, axis=(0, 1))
-    grad_key_proj = norm_back(grad_key_gained * gain_key, key_normed, key_scale).astype(BF16)
-    grad_proj = jnp.concatenate(
-        [
-            grad_query_proj.reshape(lines * rows, Q_COLS),
-            grad_key_proj.reshape(lines * rows, HEAD_DIM),
-            grad_value_proj.reshape(lines * rows, HEAD_DIM),
-        ],
-        axis=1,
-    )
+    if large:
+        grad_mixed = dot(grad_attn, weight_o.T).astype(BF16).reshape(lines, rows, GROUPS, HEAD_DIM)
+        grad_query_rot, grad_key_rot, grad_value_rot = attend_back(
+            query_rot, key_rot, value_proj, allowed, score_scale, log_total, grad_mixed
+        )
+        grad_value_proj = grad_value_rot.astype(BF16)
+        grad_query_gained = rotate(grad_query_rot, cosine[:, :, None], -sine_table[:, :, None])
+        grad_gain_query = jnp.sum(grad_query_gained * query_normed, axis=(0, 1, 2))
+        grad_query_proj = norm_back(grad_query_gained * gain_query, query_normed, query_scale).astype(
+            BF16
+        )
+        grad_key_gained = rotate(grad_key_rot, cosine, -sine_table)
+        grad_gain_key = jnp.sum(grad_key_gained * key_normed, axis=(0, 1))
+        grad_key_proj = norm_back(grad_key_gained * gain_key, key_normed, key_scale).astype(BF16)
+        grad_proj = jnp.concatenate(
+            [
+                grad_query_proj.reshape(lines * rows, Q_COLS),
+                grad_key_proj.reshape(lines * rows, HEAD_DIM),
+                grad_value_proj.reshape(lines * rows, HEAD_DIM),
+            ],
+            axis=1,
+        )
+    else:
+        grad_proj = came[1].reshape(lines * rows, width)
+        grad_gain_query, grad_gain_key = came[2][0], came[2][1]
     hidden_one_part = dot(grad_proj, weight_qkv.T)
     grad_gain_attn = jnp.sum(hidden_one_part * attn_normed, axis=0)
     qkv_part = dot(hidden_one.T, grad_proj).astype(BF16)

time: 663 us -> 639 us (0.964)
  Pallas kernels: 524 us -> 537 us
  local copies, waits for them, and re-layouts: 36.1 us -> 23.5 us
  matrix products: 41.2 us -> 29.1 us
  other arithmetic: 52.3 us -> 41.7 us
    pallas_call x4, Pallas kernels: 318 us -> 331 us  [exchange(): pl.pallas_call(body, out_shape=tuple(out_shapes), in_specs=in_specs, out_...]
    dot_general x7 -> x6, matrix products: 34.7 us -> 25 us  [dot(): return jnp.dot(left, right, preferred_element_type=F32)]
    unnamed x145 -> x129, local copies, waits for them, and re-layouts: 16.7 us -> 8.95 us
where the time goes in v6:
time: 639 us; the launch traced here: 633 us
  Pallas kernels  537 us (84%)
  other arithmetic  41.7 us (7%)
  matrix products  29.1 us (5%)
  local copies, waits for them, and re-layouts  23.5 us (4%)
    pallas_call x4, Pallas kernels, exchange(): pl.pallas_call(body, out_shape=tuple(out_shapes), in_specs=in_specs, out_...  331 us
    pallas_call x1, Pallas kernels, experts_call(): pl.pallas_call(functools.partial(experts_body, capacity), out_shape=(all_...  206 us
    dot_general x6, matrix products, dot(): return jnp.dot(left, right, preferred_element_type=F32)  25 us

profile of v6, /device:TPU:0, one launch (start us, length us, event | category | flops | bytes accessed | tf_op | source)
XLA Modules:
  0.0 633.1 jit_solution(11817425112722621928)
XLA Ops:
  5.2 65.7 %gather_inputs.1 = (bf16[4,4,2,32,128]{4,3,2,1,0:T(8,128)(2,1)}, s32[4,4,2,16,128]{4,3,2,1,0:T(8,128)}, bf16[4,4,2,64,1280]{4,3,2,1,0:T(8,128)(2,1)}, bf16[4,128...) custom-call(bf16[32,128]{1,0:T(8,128)(2,1)} %fusion.39.refs_0_, s32[16,128]{1,0:T(8,128)} %pad_bitcast_fusion.refs_1_, ...), custom_call_target="tpu_custom_call" | custom-call | tf_op jit(solution)/shard_map/gather_inputs/pallas_call | solution.py:801
  75.7 2.2 multiply_reduce_fusion
  79.1 2.9 fusion.58
  82.3 2.0 fusion.22
  93.0 6.2 convolution_convert_fusion.1
  99.2 79.4 %sum_residual.1 = (bf16[4,4,2,128,2048]{4,3,2,1,0:T(8,128)(2,1)}, f32[128,2048]{1,0:T(8,128)}) custom-call(bf16[128,2048]{1,0:T(8,128)(2,1)} %refs_0_.1, bf16[4,128,2048]{2,1,0:T(8,128)(2,1)} %bitcast.202), custom_call_target="tpu_custom_call" | custom-call | tf_op jit(solution)/shard_map/sum_residual/pallas_call | solution.py:801
  178.6 2.2 multiply_reduce_fusion.4
  185.8 1.5 fusion.3.refs_4_
  188.4 205.9 %experts.1 = (bf16[4,4,2,128,2048]{4,3,2,1,0:T(8,128)(2,1)}, bf16[4,4,2,128,2048]{4,3,2,1,0:T(8,128)(2,1)}, f32[4,4,2,16,256]{4,3,2,1,0:T(8,128)}, f32[4,4,2,32,...) custom-call(bf16[128,2048]{1,0:T(8,128)(2,1)} %copy-done.13, ...), custom_call_target="tpu_custom_call" | custom-call | tf_op jit(solution)/shard_map/experts/pallas_call | solution.py:1146
  395.5 1.3 fusion.21
  397.8 2.4 fusion.16
  400.9 2.6 fusion.50.refs_0_
  403.5 3.3 add.187.refs_5_
  406.8 1.5 copy_bitcast_fusion.refs_2_
  410.7 112.3 %gather_grad.1 = (bf16[4,128,2048]{2,1,0:T(8,128)(2,1)}, bf16[4,128,1280]{2,1,0:T(8,128)(2,1)}, f32[8,128]{1,0:T(8,128)}, f32[128,2048]{1,0:T(8,128)}, bf16[2048...) custom-call(bf16[128,2048]{1,0:T(8,128)(2,1)} %fusion.50.refs_0_, ...), custom_call_target="tpu_custom_call" | custom-call | tf_op jit(solution)/shard_map/gather_grad/pallas_call | solution.py:801
  523.1 6.5 %convolution_convert_fusion = bf16[1024,2048]{1,0:T(8,128)(2,1)} fusion(bf16[512,2048]{1,0:T(8,128)(2,1)} %bitcast.237, bf16[64,8,8,128]{3,2,1,0:T(8,128)(2,1)} %bitcast.212), kind=kOutput, calls=%fused_computation.6 | convolution fusion | flops 2149580800 | bytes 7340032 | tf_op jit(solution)/shard_map/dot_general | solution.py:33
  529.6 4.7 bitcast_convert_fusion
  534.3 4.1 fusion.51
  539.8 73.4 %sum_gradients.1 = (f32[4,4,2,48,128]{4,3,2,1,0:T(8,128)}, f32[128,2048]{1,0:T(8,128)}, bf16[4,64,1280]{2,1,0:T(8,128)(2,1)}, f32[128,2048]{1,0:T(8,128)}) custom-call(f32[48,128]{1,0:T(8,128)} %fusion.31.refs_0_, bf16[4,128,2048]{2,1,0:T(8,128)(2,1)} %bitcast.201, bf16[4,4,2,64,1280]{4,3,2,1,0:T(8,128)(2,1)} %bitcast.191, bf16[4,2,128,2048]{3,2,1,0:T(8,128)(2,1)} %bitcast.194), custom_call_target="tpu_custom_call" | custom-call | tf_op jit(solution)/shard_map/sum_gradients/pallas_call | solution.py:801
  617.6 1.7 fusion.12
  620.3 1.5 dynamic-slice_reduce_fusion
  621.8 3.5 bitcast_convert_fusion.1
  625.3 3.2 bitcast_convert_fusion.2
  628.5 3.2 bitcast_convert_fusion.3
  (208 shorter events, 37.8 us)
Async XLA Ops:
  0.7 3.1 copy-start.53
  0.7 3.7 copy-start.48
  0.7 3.9 copy-start.54
  70.9 7.6 %copy-start.11 = (bf16[4,128,2048]{2,1,0:T(8,128)(2,1)S(1)}, bf16[4,128,2048]{2,1,0:T(8,128)(2,1)}, u32[]{:S(2)}) copy-start(bf16[4,128,2048]{2,1,0:T(8,128)(2,1)} %get-tuple-element.39) | copy-start | bytes 6291460
  75.7 3.4 copy-start.55
  92.9 6.2 copy-start.32
  178.6 3.4 copy-start.39
  182.0 5.3 copy-start.13
  182.4 6.0 copy-start.15
  397.1 3.1 copy-start.1
  397.1 3.1 copy-start.16
  400.8 5.9 copy-start.7
  400.8 5.9 copy-start.9
  406.8 3.2 copy-start.43
  523.1 6.5 %copy-start.28 = (bf16[4,128,2048]{2,1,0:T(8,128)(2,1)S(1)}, bf16[4,128,2048]{2,1,0:T(8,128)(2,1)}, u32[]{:S(2)}) copy-start(bf16[4,128,2048]{2,1,0:T(8,128)(2,1)} %copy-done.27) | copy-start | bytes 6291460
  523.1 6.5 %copy-start.56 = (bf16[4,128,1280]{2,1,0:T(8,128)(2,1)S(1)}, bf16[4,128,1280]{2,1,0:T(8,128)(2,1)}, u32[]{:S(2)}) copy-start(bf16[4,128,1280]{2,1,0:T(8,128)(2,1)} %get-tuple-element.56) | copy-start | bytes 3932164
  523.1 11.2 %slice-start = ((s8[5242880]{0:T(1024)(128)(4,1)}), s8[4194304]{0:T(1024)(128)(4,1)S(1)}, s32[]{:S(2)}) async-start(s8[5242880]{0:T(1024)(128)(4,1)} %bitcast.234), calls=%async_computation | async-start | bytes 8388608
  529.6 4.7 copy-start.12
  529.6 4.7 copy-start.51
  529.6 4.7 slice-start.1
  617.5 4.2 copy-start.20
  621.8 3.6 copy-start.19
  625.3 3.2 copy-start.18
  628.5 3.2 copy-start.33
  (35 other events, 78.7 us)

commit v7 on v6

--- a/solution.py
+++ b/solution.py
@@ -153,14 +153,14 @@
     return [DMA, DMA((2, n)), DMA((n,)), DMA((n, 8)), DMA((n, 8)), DMA((2, n, 3)), DMA((n, 3))]
 
 
-def gather_parts(spot, x_ref, out_ref, sems, mode="all", even=False):
+def gather_parts(spot, x_ref, out_ref, sems, mode="all", even=False, direct=False):
     own_sem, zs, zr, ps, pr, vs, vr = sems
     z, b, c, xn, yn, dg, lines = spot.z, spot.b, spot.c, spot.xn, spot.yn, spot.dg, spot.lines
     here = (z, b, c)
     rows = out_ref.shape[-2]
     flat = mode == "plane"
     planar = mode != "line"
-    relayed = mode in ("all", "line")
+    relayed = mode in ("all", "line") and not direct
     via = rows // 4 if even else 0
     last = pl.ds(rows - via, via)
     columns = (b, xn, yn, dg)
@@ -241,18 +241,17 @@
             received(blk(zz, columns[k]).at[last], vr.at[zz, k - 1])
         onward(way, lambda down: hop_via(zz, k, down).start())
 
+    def straight(zz):
+        src = x_ref.at[zz] if mode == "swap" else x_ref
+        return send(src, blk(z, b), zs.at[0, zz], zr.at[z], (zz, b, c))
+
     def start():
         pltpu.make_async_copy(own(), blk(mine, b), own_sem).start()
         if relayed:
             onward(0, lambda down: hop(z, down, 0).start())
-        if mode == "swap":
+        if mode == "swap" or direct:
             for d in range(lines - 1, 0, -1):
-                spot.each(
-                    d,
-                    lambda zz, way: send(
-                        x_ref.at[zz], blk(z, b), zs.at[0, zz], zr.at[z], (zz, b, c)
-                    ).start(),
-                )
+                spot.each(d, lambda zz, way: straight(zz).start())
         if planar:
             for copy in plane_copies(mine, 0):
                 copy.start()
@@ -295,8 +294,8 @@
         if via:
             for k in (1, 2, 3):
                 onward(way, lambda down, k=k: hop_via(zz, k, down).wait_send())
-        if mode == "swap" and way != 0:
-            send(x_ref.at[zz], blk(z, b), zs.at[0, zz], zr.at[z], (zz, b, c)).wait_send()
+        if (mode == "swap" or direct) and way != 0:
+            straight(zz).wait_send()
 
     def shared(zz, k):
         received(blk(zz, columns[k], 1 - c), pr.at[zz, 4 + k])
@@ -868,7 +867,7 @@
     spot.greet()
     steps_h = gather_parts(spot, h_ref, hall, h_sems, even=True)
     steps_w = gather_parts(spot, own_w_ref, w_ref, w_sems)
-    steps_dw = gather_parts(spot, dw_ref, dw_all, dw_sems)
+    steps_dw = gather_parts(spot, dw_ref, dw_all, dw_sems, direct=True)
     both = (steps_w, steps_h)
     columns = (b, xn, yn, dg_spot)
     turn = [0]
@@ -1096,19 +1095,14 @@
     places(3)
     steps_dw["start"]()
     sums("third", 2)
+    for d in (1, 2, 3):
+        comm_dw("line", d)
     sums("second", 3)
-    comm_dw("line", 1)
-    comm_dw("plane", 0)
-    comm_dw("line", 2)
-    comm_dw("plane", 1)
-    comm_dw("cross", 0)
-    comm_dw("line", 3)
-    comm_dw("plane", 2)
-    comm_dw("cross", 1)
+    for d in range(4):
+        comm_dw("plane", d)
     sums("third", 3)
-    comm_dw("plane", 3)
-    comm_dw("cross", 2)
-    comm_dw("cross", 3)
+    for d in range(4):
+        comm_dw("cross", d)
     steps_r["end"]()
     for m in (0, 1):
         put(z, b, m).wait()

time: 639 us -> 628 us (0.983)
  Pallas kernels: 537 us -> 525 us
    pallas_call x1, Pallas kernels: 206 us -> 198 us  [experts_call(): pl.pallas_call(functools.partial(experts_body, capacity), out_shape=(all_...]
where the time goes in v7:
time: 628 us; the launch traced here: 622 us
  Pallas kernels  525 us (84%)
  other arithmetic  41.7 us (7%)
  matrix products  29.1 us (5%)
  local copies, waits for them, and re-layouts  23.5 us (4%)
    pallas_call x4, Pallas kernels, exchange(): pl.pallas_call(body, out_shape=tuple(out_shapes), in_specs=in_specs, out_...  327 us
    pallas_call x1, Pallas kernels, experts_call(): pl.pallas_call(functools.partial(experts_body, capacity), out_shape=(all_...  198 us
    dot_general x6, matrix products, dot(): return jnp.dot(left, right, preferred_element_type=F32)  25 us

profile of v7, /device:TPU:0, one launch (start us, length us, event | category | flops | bytes accessed | tf_op | source)
XLA Modules:
  0.0 621.8 jit_solution(12581875074238400305)
XLA Ops:
  5.2 65.7 %gather_inputs.1 = (bf16[4,4,2,32,128]{4,3,2,1,0:T(8,128)(2,1)}, s32[4,4,2,16,128]{4,3,2,1,0:T(8,128)}, bf16[4,4,2,64,1280]{4,3,2,1,0:T(8,128)(2,1)}, bf16[4,128...) custom-call(bf16[32,128]{1,0:T(8,128)(2,1)} %fusion.39.refs_0_, s32[16,128]{1,0:T(8,128)} %pad_bitcast_fusion.refs_1_, ...), custom_call_target="tpu_custom_call" | custom-call | tf_op jit(solution)/shard_map/gather_inputs/pallas_call | solution.py:800
  75.7 2.2 multiply_reduce_fusion
  79.1 2.9 fusion.58
  82.3 2.0 fusion.22
  93.0 6.2 %convolution_convert_fusion.1 = bf16[512,2048]{1,0:T(8,128)(2,1)} fusion(bf16[1024,2048]{1,0:T(8,128)(2,1)} %bitcast.192, bf16[64,8,8,128]{3,2,1,0:T(8,128)(2,1)S(1)} %bitcast.211), kind=kOutput, calls=%fused_computation.10 | convolution fusion | flops 2148532224 | bytes 7340032 | tf_op jit(solution)/shard_map/dot_general | solution.py:33
  99.2 79.4 %sum_residual.1 = (bf16[4,4,2,128,2048]{4,3,2,1,0:T(8,128)(2,1)}, f32[128,2048]{1,0:T(8,128)}) custom-call(bf16[128,2048]{1,0:T(8,128)(2,1)} %refs_0_.1, bf16[4,128,2048]{2,1,0:T(8,128)(2,1)} %bitcast.202), custom_call_target="tpu_custom_call" | custom-call | tf_op jit(solution)/shard_map/sum_residual/pallas_call | solution.py:800
  178.6 2.2 multiply_reduce_fusion.4
  185.8 1.5 fusion.3.refs_4_
  188.4 197.9 %experts.1 = (bf16[4,4,2,128,2048]{4,3,2,1,0:T(8,128)(2,1)}, bf16[4,4,2,128,2048]{4,3,2,1,0:T(8,128)(2,1)}, f32[4,4,2,16,256]{4,3,2,1,0:T(8,128)}, f32[4,4,2,32,...) custom-call(bf16[128,2048]{1,0:T(8,128)(2,1)} %copy-done.13, ...), custom_call_target="tpu_custom_call" | custom-call | tf_op jit(solution)/shard_map/experts/pallas_call | solution.py:1140
  387.5 1.3 fusion.21
  389.9 2.4 fusion.16
  392.9 2.6 fusion.50.refs_0_
  395.5 3.3 add.187.refs_5_
  398.8 1.5 copy_bitcast_fusion.refs_2_
  402.8 108.5 %gather_grad.1 = (bf16[4,128,2048]{2,1,0:T(8,128)(2,1)}, bf16[4,128,1280]{2,1,0:T(8,128)(2,1)}, f32[8,128]{1,0:T(8,128)}, f32[128,2048]{1,0:T(8,128)}, bf16[2048...) custom-call(bf16[128,2048]{1,0:T(8,128)(2,1)} %fusion.50.refs_0_, ...), custom_call_target="tpu_custom_call" | custom-call | tf_op jit(solution)/shard_map/gather_grad/pallas_call | solution.py:800
  511.3 6.5 %convolution_convert_fusion = bf16[1024,2048]{1,0:T(8,128)(2,1)} fusion(bf16[512,2048]{1,0:T(8,128)(2,1)} %bitcast.237, bf16[64,8,8,128]{3,2,1,0:T(8,128)(2,1)} %bitcast.212), kind=kOutput, calls=%fused_computation.6 | convolution fusion | flops 2149580800 | bytes 7340032 | tf_op jit(solution)/shard_map/dot_general | solution.py:33
  517.8 4.7 bitcast_convert_fusion
  522.6 4.1 fusion.51
  528.1 73.9 %sum_gradients.1 = (f32[4,4,2,48,128]{4,3,2,1,0:T(8,128)}, f32[128,2048]{1,0:T(8,128)}, bf16[4,64,1280]{2,1,0:T(8,128)(2,1)}, f32[128,2048]{1,0:T(8,128)}) custom-call(f32[48,128]{1,0:T(8,128)} %fusion.31.refs_0_, bf16[4,128,2048]{2,1,0:T(8,128)(2,1)} %bitcast.201, bf16[4,4,2,64,1280]{4,3,2,1,0:T(8,128)(2,1)} %bitcast.191, bf16[4,2,128,2048]{3,2,1,0:T(8,128)(2,1)} %bitcast.194), custom_call_target="tpu_custom_call" | custom-call | tf_op jit(solution)/shard_map/sum_gradients/pallas_call | solution.py:800
  606.2 1.7 fusion.12
  609.0 1.5 dynamic-slice_reduce_fusion
  610.5 3.5 bitcast_convert_fusion.1
  614.0 3.2 bitcast_convert_fusion.2
  617.2 3.2 bitcast_convert_fusion.3
  (208 shorter events, 37.8 us)
Async XLA Ops:
  0.7 3.1 copy-start.53
  0.7 3.7 copy-start.48
  0.7 3.9 copy-start.54
  70.9 7.6 %copy-start.11 = (bf16[4,128,2048]{2,1,0:T(8,128)(2,1)S(1)}, bf16[4,128,2048]{2,1,0:T(8,128)(2,1)}, u32[]{:S(2)}) copy-start(bf16[4,128,2048]{2,1,0:T(8,128)(2,1)} %get-tuple-element.39) | copy-start | bytes 6291460
  75.7 3.4 copy-start.55
  92.9 6.2 %copy-start.32 = (bf16[4,128,8,128]{3,2,1,0:T(8,128)(2,1)}, bf16[4,128,8,128]{3,2,1,0:T(8,128)(2,1)S(1)}, u32[]{:S(2)}) copy-start(bf16[4,128,8,128]{3,2,1,0:T(8,128)(2,1)S(1)} %copy.115) | copy-start | bytes 3145732
  178.6 3.4 copy-start.39
  182.0 5.3 copy-start.13
  182.4 6.0 copy-start.15
  389.2 3.1 copy-start.1
  389.2 3.1 copy-start.16
  392.9 5.9 copy-start.7
  392.9 5.9 copy-start.9
  398.8 3.2 copy-start.43
  511.3 6.5 %copy-start.28 = (bf16[4,128,2048]{2,1,0:T(8,128)(2,1)S(1)}, bf16[4,128,2048]{2,1,0:T(8,128)(2,1)}, u32[]{:S(2)}) copy-start(bf16[4,128,2048]{2,1,0:T(8,128)(2,1)} %copy-done.27) | copy-start | bytes 6291460
  511.3 6.5 %copy-start.56 = (bf16[4,128,1280]{2,1,0:T(8,128)(2,1)S(1)}, bf16[4,128,1280]{2,1,0:T(8,128)(2,1)}, u32[]{:S(2)}) copy-start(bf16[4,128,1280]{2,1,0:T(8,128)(2,1)} %get-tuple-element.56) | copy-start | bytes 3932164
  511.3 11.2 %slice-start = ((s8[5242880]{0:T(1024)(128)(4,1)}), s8[4194304]{0:T(1024)(128)(4,1)S(1)}, s32[]{:S(2)}) async-start(s8[5242880]{0:T(1024)(128)(4,1)} %bitcast.234), calls=%async_computation | async-start | bytes 8388608
  517.8 4.7 copy-start.12
  517.8 4.7 copy-start.51
  517.8 4.7 slice-start.1
  606.2 4.2 copy-start.20
  610.5 3.6 copy-start.19
  614.0 3.2 copy-start.18
  617.2 3.2 copy-start.33
  (35 other events, 78.7 us)
